TPU v7x, 8 devices: a whole 2x2x1 slice. The times are simulated.
8 devices in a mesh: dp: 8 (over z, y, x, core).
Axes of the slice: x: 2, y: 2, z: 1, core: 2. Of those that a mesh axis runs over, the one named last changes fastest.
Arguments:
- local_grads: bfloat16 [8, 49152, 768], P('dp')
- master: float32 [49152, 768], P('dp')
- mom_first: float32 [49152, 768], P('dp')
- mom_second: float32 [49152, 768], P('dp')
- learn_rate: float32 [], replicated
Outputs:
- output 1: float32 [49152, 768], P('dp')
- output 2: float32 [49152, 768], P('dp')
- output 3: float32 [49152, 768], P('dp')
- output 4: bfloat16 [49152, 768], replicated
All inputs are finite; a program needn't handle non-finite values.
Results may differ from a plain program's by a relative error of at most 0.001.
Values are sent between devices in bfloat16 or wider.
A program may use at most 1 GiB of HBM per device.

v0:
```python
import jax
import jax.numpy as jnp
from jax import lax
from jax.sharding import PartitionSpec as P, NamedSharding

LAYERS = 2
MIX_RANK = 32
DECAY_RANK = 64
ADAM_STEP = 10


def layout_runs(model_width, total_rows):
    ffn_width = 7 * model_width // 2
    layer_rows = 6 * model_width + 2 * ffn_width + 16 + 10 * MIX_RANK + 2 * DECAY_RANK
    vocab_rows = (total_rows - LAYERS * layer_rows - 4) // 2
    base_rule = (1.0, 0.0)
    decay_rule = (1.0, 0.1)
    time_rule = (2.0, 0.0)
    pieces = [(vocab_rows, decay_rule)]
    for layer_idx in range(LAYERS):
        lead_rows = 12 if layer_idx == 0 else 10
        pieces = pieces + [(lead_rows + 10 * MIX_RANK, base_rule), (1, time_rule), (2 * DECAY_RANK, base_rule), (1, time_rule), (5 * model_width, decay_rule), (4, base_rule), (2 * ffn_width + model_width, decay_rule)]
    pieces = pieces + [(2, base_rule), (vocab_rows, decay_rule)]
    run_starts = []
    next_row = 0
    for run_len, run_rule in pieces:
        run_starts.append(next_row)
        next_row = next_row + run_len
    lr_values = [run_rule[0] for run_len, run_rule in pieces]
    decay_values = [run_rule[1] for run_len, run_rule in pieces]
    return run_starts, lr_values, decay_values


def row_rules(row_ids, model_width, total_rows):
    run_starts, lr_values, decay_values = layout_runs(model_width, total_rows)
    later_starts = jnp.asarray(run_starts[1:], jnp.int32)
    run_index = jnp.sum((row_ids[:, None] >= later_starts[None, :]).astype(jnp.int32), axis=1)
    lr_factor = jnp.asarray(lr_values, jnp.float32)[run_index]
    decay_rate = jnp.asarray(decay_values, jnp.float32)[run_index]
    return lr_factor[:, None], decay_rate[:, None]


def adam_rows(grad_rows, master_rows, first_rows, second_rows, clip_scale, learn_rate, lr_factor, decay_rate):
    clipped = grad_rows * clip_scale
    new_first = 0.9 * first_rows + 0.1 * clipped
    new_second = 0.99 * second_rows + 0.01 * (clipped * clipped)
    first_hat = new_first / (1.0 - 0.9 ** ADAM_STEP)
    second_hat = new_second / (1.0 - 0.99 ** ADAM_STEP)
    step_size = learn_rate * lr_factor
    new_master = master_rows - step_size * (first_hat / (jnp.sqrt(second_hat) + 1e-8) + decay_rate * master_rows)
    return new_master, new_first, new_second


def solution(mesh):
    dev_count = mesh.shape['dp']

    def device_step(local_grads, master, mom_first, mom_second, learn_rate):
        shard_rows = master.shape[0]
        model_width = master.shape[1]
        total_rows = shard_rows * dev_count
        grad_shard = lax.psum_scatter(local_grads[0].astype(jnp.float32), 'dp', scatter_dimension=0, tiled=True) / dev_count
        square_sum = lax.psum(jnp.sum(grad_shard * grad_shard), 'dp')
        clip_scale = jnp.minimum(1.0, 1.0 / (jnp.sqrt(square_sum) + 1e-6))
        row_ids = lax.axis_index('dp') * shard_rows + lax.iota(jnp.int32, shard_rows)
        lr_factor, decay_rate = row_rules(row_ids, model_width, total_rows)
        new_master, new_first, new_second = adam_rows(grad_shard, master, mom_first, mom_second, clip_scale, learn_rate, lr_factor, decay_rate)
        working = lax.all_gather(new_master.astype(jnp.bfloat16), 'dp', axis=0, tiled=True)
        return new_master, new_first, new_second, working

    return jax.shard_map(device_step, mesh=mesh, in_specs=(P('dp', None, None), P('dp', None), P('dp', None), P('dp', None), P()), out_specs=(P('dp', None), P('dp', None), P('dp', None), P(None, None)), check_vma=False)
```

profile of v0, /device:TPU:0, one launch (start us, length us, event | category | flops | bytes accessed | tf_op | source)
XLA Modules:
  0.0 1375.5 jit_solution(15299603286395650553)
XLA Ops:
  7.2 0.0 reduce-scatter.2.cloned.1.call-start
  7.2 75.4 %bitcast_convert_fusion = f32[49152,768]{1,0:T(8,128)} fusion(bf16[1,49152,768]{2,1,0:T(8,128)(2,1)} %param.8), kind=kLoop, calls=%fused_computation | loop fusion | flops 37748736 | bytes 226492416 | tf_op jit(solution)/shard_map/convert_element_type | solution.py:61
  82.6 0.0 copy-start
  82.6 0.0 reduce-scatter.2.cloned.1.call-update
  82.6 0.0 all-gather.2.cloned.1.call-start
  83.3 0.0 copy-done
  83.3 0.1 convert_reduce_fusion
  83.5 0.1 compare_select_fusion.2
  83.6 0.7 compare_reduce_fusion.9
  84.3 0.1 compare_select_fusion.3
  84.4 812.8 %reduce-scatter.2.cloned.1.call-done = f32[6144,768]{1,0:T(8,128)} async-done(((f32[49152,768]{1,0:T(8,128)}), f32[6144,768]{1,0:T(8,128)}) %reduce-scatter.2.cloned.1.call-update) | async-done | bytes 18874384 | tf_op jit(solution)/shard_map/reduce_scatter | solution.py:61
  897.2 11.8 multiply_reduce_fusion
  909.1 22.5 %psum.7 = f32[]{:T(128)} all-reduce(f32[]{:T(128)} %multiply_reduce_fusion), channel_id=1, replica_groups=mesh['dp'=8] {'dp'}, use_global_device_ids=true, to_apply=%region_3.0 | all-reduce | flops 1 | bytes 8 | tf_op jit(solution)/shard_map/psum | solution.py:62
  932.3 50.4 %fusion = (bf16[6144,768]{1,0:T(8,128)(2,1)}, f32[6144,768]{1,0:T(8,128)}, f32[6144,768]{1,0:T(8,128)}, f32[6144,768]{1,0:T(8,128)}) fusion(f32[6144,768]{1,0:T(8,128)} %param.9, f32[6144]{0:T(1024)S(1)} %get-tuple-element.21, f32[6144]{0:T(1024)S(1)} %get-tuple-element.20, f32[6144,768]{1,0:T(8,128)} %reduce-scatter.2.cloned.1.call-done, f32[]{:T(128)S(6)} %mul.75, ...), kind=kLoop, calls=%fused_computation.31 | loop fusion | flops 80216064 | bytes 141606912 | tf_op jit(solution)/shard_map/convert_element_type | solution.py:67
  982.7 0.0 all-gather.2.cloned.1.call-update
  982.7 335.6 %all-gather.2.cloned.1.call-done = bf16[49152,768]{1,0:T(8,128)(2,1)} async-done(((bf16[6144,768]{1,0:T(8,128)(2,1)}), bf16[49152,768]{1,0:T(8,128)(2,1)}) %all-gather.2.cloned.1.call-update) | async-done | bytes 75497488 | tf_op jit(solution)/shard_map/all_gather | solution.py:67
  1318.3 50.3 %copy.14 = bf16[49152,768]{1,0:T(8,128)(2,1)} copy(bf16[49152,768]{1,0:T(8,128)(2,1)} %all-gather.2.cloned.1.call-done) | data formatting | bytes 150994944
  (2 shorter events, 0.0 us)
Async XLA Ops:
  7.2 890.1 %reduce-scatter.2.cloned.1.call-start = ((), (), s32[]{:S(2)}) async-start(), calls=%async_computation.1 | async-start | bytes 169869312 | tf_op jit(solution)/shard_map/reduce_scatter | solution.py:61
  82.6 0.7 copy-start
  82.6 1235.7 %all-gather.2.cloned.1.call-start = ((), (), s32[]{:S(2)}) async-start(), calls=%async_computation.2 | async-start | bytes 84934656 | tf_op jit(solution)/shard_map/all_gather | solution.py:67
Sparse Core Ops, SparseCore 0:
  82.7 814.4 reduce-scatter.1
  982.8 335.4 all-gather.1
where the time goes:
time: 1380 us
  waiting for transfers between devices  1150 us (83%)
  other arithmetic  139 us (10%)
  local copies, waits for them, and re-layouts  50.3 us (4%)
  blocking collectives  22.5 us (2%)
  between operations  15.5 us (1%)
    reduce_scatter x1, waiting for transfers between devices, device_step(): lax.psum_scatter(local_grads[0].astype(jnp.float32), 'dp', scatter_dimens...  813 us
    all_gather x1, waiting for transfers between devices, device_step(): lax.all_gather(new_master.astype(jnp.bfloat16), 'dp', axis=0, tiled=True)  336 us
    convert_element_type x1, other arithmetic, device_step(): local_grads[0].astype(jnp.float32)  75.4 us
    convert_element_type x1, other arithmetic, device_step(): new_master.astype(jnp.bfloat16)  50.4 us
    unnamed x3, local copies, waits for them, and re-layouts  50.3 us
  transfers between devices with their start and end apart: 2, of which 2 were waited for; matrix products, arithmetic and copies ran while one was open for 0% of the time, Pallas kernels for 0%

commit v1 on v0

--- a/solution.py
+++ b/solution.py
@@ -1,12 +1,19 @@
+import functools
+
 import jax
 import jax.numpy as jnp
 from jax import lax
-from jax.sharding import PartitionSpec as P, NamedSharding
+from jax.experimental import pallas as pl
+from jax.experimental.pallas import tpu as pltpu
+from jax.sharding import PartitionSpec as P
 
 LAYERS = 2
 MIX_RANK = 32
 DECAY_RANK = 64
 ADAM_STEP = 10
+MESH = pl.DeviceIdType.MESH
+TILE = 256
+SLAB = 32
 
 
 def layout_runs(model_width, total_rows):
@@ -51,6 +58,204 @@
     return new_master, new_first, new_second
 
 
+def places():
+    me = lax.axis_index('dp')
+    core = me % 2
+    x = (me // 2) % 2
+    y = me // 4
+    x_chip = y * 2 + (1 - x)
+    y_chip = (1 - y) * 2 + x
+    d_chip = (1 - y) * 2 + (1 - x)
+    return me, core, me + 1 - 2 * core, x_chip, y_chip, d_chip
+
+
+def greet(partners):
+    barrier = pltpu.get_barrier_semaphore()
+    for partner in partners:
+        pl.semaphore_signal(barrier, inc=1, device_id=(partner,), device_id_type=MESH)
+    pl.semaphore_wait(barrier, len(partners))
+
+
+def reduce_kernel(shard, grads, total_ref, clip_ref, x_raw, y_raw, mate_raw, x_sum, y_sum,
+                  relay, blocks, sums, finals, squares, norm_mine, norm_all,
+                  x_sent, y_sent, mate_sent, xs_sent, ys_sent, x_got, y_got, mate_got, xs_got, ys_got,
+                  load_sem, store_sem, norm_sent, norm_got):
+    half = shard // 2
+    tiles = half // TILE
+    me, core, mate, x_chip, y_chip, d_chip = places()
+    mate_core = 1 - core
+    x_peer, y_peer, d_peer = x_chip * 2 + core, y_chip * 2 + core, d_chip * 2 + core
+    everyone = [mate, x_chip * 2, x_chip * 2 + 1, y_chip * 2, y_chip * 2 + 1, d_chip * 2, d_chip * 2 + 1]
+    greet(everyone)
+
+    def rows(tile):
+        return pl.ds(pl.multiple_of(tile * TILE, TILE), TILE)
+
+    def grad_tile(owner, part, tile):
+        return grads.at[0, pl.ds(pl.multiple_of(owner * shard + part * half + tile * TILE, TILE), TILE), :]
+
+    def remote(src, dst, sent, got, device):
+        return pltpu.make_async_remote_copy(src_ref=src, dst_ref=dst, send_sem=sent, recv_sem=got, device_id=(device,), device_id_type=MESH)
+
+    def send_raw(stage, tile):
+        x_owner = d_chip if stage == 0 else x_chip
+        y_owner = d_chip if stage == 0 else y_chip
+        for dest in range(2):
+            remote(grad_tile(x_owner * 2 + dest, 0, tile), x_raw.at[stage, core, rows(tile)], x_sent.at[tile], x_got.at[stage, core, tile], x_chip * 2 + dest).start()
+            remote(grad_tile(y_owner * 2 + dest, 1, tile), y_raw.at[stage, core, rows(tile)], y_sent.at[tile], y_got.at[stage, core, tile], y_chip * 2 + dest).start()
+        first = y_chip * 2 + mate_core if stage == 0 else mate
+        second = x_chip * 2 + mate_core if stage == 0 else mate
+        remote(grad_tile(first, 0, tile), mate_raw.at[2 * stage, rows(tile)], mate_sent.at[tile], mate_got.at[2 * stage, tile], mate).start()
+        remote(grad_tile(second, 1, tile), mate_raw.at[2 * stage + 1, rows(tile)], mate_sent.at[tile], mate_got.at[2 * stage + 1, tile], mate).start()
+
+    def arrived(ref, sem):
+        remote(ref, ref, sem, sem, mate).wait_recv()
+
+    def wait_raw(stage, tile):
+        for source in range(2):
+            arrived(x_raw.at[stage, source, rows(tile)], x_got.at[stage, source, tile])
+            arrived(y_raw.at[stage, source, rows(tile)], y_got.at[stage, source, tile])
+        for part in range(2):
+            arrived(mate_raw.at[2 * stage + part, rows(tile)], mate_got.at[2 * stage + part, tile])
+
+    def loads(stage, tile):
+        owners = (y_peer, x_peer) if stage == 0 else (me, me)
+        out = []
+        for part in range(2):
+            far = x_raw if part == 0 else y_raw
+            sources = [grad_tile(owners[part], part, tile), mate_raw.at[2 * stage + part, rows(tile)], far.at[stage, 0, rows(tile)], far.at[stage, 1, rows(tile)]]
+            for k, source in enumerate(sources):
+                out.append(pltpu.make_async_copy(source, blocks.at[part, k], load_sem.at[part, k]))
+        return out
+
+    @pl.loop(0, tiles)
+    def _(tile):
+        send_raw(0, tile)
+
+    @pl.loop(0, tiles)
+    def _(tile):
+        send_raw(1, tile)
+        wait_raw(0, tile)
+        copies = loads(0, tile)
+        for copy in copies:
+            copy.start()
+        for part in range(2):
+            for copy in copies[4 * part:4 * part + 4]:
+                copy.wait()
+
+            @pl.loop(0, TILE // SLAB)
+            def _(slab):
+                at = pl.ds(pl.multiple_of(slab * SLAB, SLAB), SLAB)
+                parts = [blocks[part, k, at, :].astype(jnp.float32) for k in range(4)]
+                relay[part, tile, at, :] = (parts[0] + parts[1]) + (parts[2] + parts[3])
+
+            if part == 0:
+                remote(relay.at[0, tile], y_sum.at[rows(tile)], ys_sent.at[tile], ys_got.at[tile], y_peer).start()
+            else:
+                remote(relay.at[1, tile], x_sum.at[rows(tile)], xs_sent.at[tile], xs_got.at[tile], x_peer).start()
+
+    squares[...] = jnp.zeros_like(squares)
+
+    def total_tile(part, tile):
+        return total_ref.at[pl.ds(pl.multiple_of(part * half + tile * TILE, TILE), TILE), :]
+
+    @pl.loop(0, tiles)
+    def _(tile):
+        wait_raw(1, tile)
+        copies = loads(1, tile)
+        for copy in copies:
+            copy.start()
+        arrived(y_sum.at[rows(tile)], ys_got.at[tile])
+        first_sum = pltpu.make_async_copy(y_sum.at[rows(tile)], sums.at[0], load_sem.at[0, 4])
+        first_sum.start()
+        arrived(x_sum.at[rows(tile)], xs_got.at[tile])
+        second_sum = pltpu.make_async_copy(x_sum.at[rows(tile)], sums.at[1], load_sem.at[1, 4])
+        second_sum.start()
+        for part in range(2):
+            for copy in copies[4 * part:4 * part + 4]:
+                copy.wait()
+            (first_sum, second_sum)[part].wait()
+
+            @pl.when(tile > 0)
+            def _():
+                pltpu.make_async_copy(finals.at[part], total_tile(part, tile), store_sem.at[part]).wait()
+
+            @pl.loop(0, TILE // SLAB)
+            def _(slab):
+                at = pl.ds(pl.multiple_of(slab * SLAB, SLAB), SLAB)
+                parts = [blocks[part, k, at, :].astype(jnp.float32) for k in range(4)]
+                mean = ((parts[0] + parts[1]) + (parts[2] + parts[3]) + sums[part, at, :]) * 0.125
+                finals[part, at, :] = mean
+                squares[...] += jnp.sum((mean * mean).reshape(SLAB // 8, 8, mean.shape[1]), axis=0)
+
+            pltpu.make_async_copy(finals.at[part], total_tile(part, tile), store_sem.at[part]).start()
+
+    width = squares.shape[1]
+    packed = squares[:, 0:128]
+    for lane in range(1, width // 128):
+        packed = packed + squares[:, lane * 128:lane * 128 + 128]
+    norm_mine[...] = packed
+    norm_all[me] = packed
+    for part in range(2):
+        pltpu.make_async_copy(finals.at[part], total_tile(part, 0), store_sem.at[part]).wait()
+    for k, partner in enumerate(everyone):
+        remote(norm_mine, norm_all.at[me], norm_sent.at[k], norm_got.at[me], partner).start()
+    for k, partner in enumerate(everyone):
+        arrived(norm_all.at[partner], norm_got.at[partner])
+    squared = norm_all[0]
+    for k in range(1, 8):
+        squared = squared + norm_all[k]
+    norm = jnp.sqrt(jnp.sum(squared))
+    clip_ref[...] = jnp.broadcast_to(jnp.minimum(1.0, 1.0 / (norm + 1e-6)), clip_ref.shape)
+
+    for k, partner in enumerate(everyone):
+        remote(norm_mine, norm_mine, norm_sent.at[k], norm_sent.at[k], partner).wait_send()
+
+    @pl.loop(0, tiles)
+    def _(tile):
+        for ref, sem in ((x_raw.at[:, :, rows(tile)], x_sent), (y_raw.at[:, :, rows(tile)], y_sent), (mate_raw.at[:, rows(tile)], mate_sent),
+                         (x_sum.at[rows(tile)], xs_sent), (y_sum.at[rows(tile)], ys_sent)):
+            remote(ref, ref, sem.at[tile], sem.at[tile], mate).wait_send()
+
+
+def reduce_grads(local_grads, shard):
+    width = local_grads.shape[2]
+    half = shard // 2
+    tiles = half // TILE
+    any_spec = pl.BlockSpec(memory_space=pl.ANY)
+    bf16, f32 = jnp.bfloat16, jnp.float32
+    dma = pltpu.SemaphoreType.DMA
+    outs = pl.pallas_call(
+        functools.partial(reduce_kernel, shard),
+        out_shape=[
+            jax.ShapeDtypeStruct((shard, width), f32),
+            jax.ShapeDtypeStruct((8, 128), f32),
+            jax.ShapeDtypeStruct((2, 2, half, width), bf16),
+            jax.ShapeDtypeStruct((2, 2, half, width), bf16),
+            jax.ShapeDtypeStruct((4, half, width), bf16),
+            jax.ShapeDtypeStruct((half, width), f32),
+            jax.ShapeDtypeStruct((half, width), f32),
+        ],
+        in_specs=[any_spec],
+        out_specs=[any_spec, pl.BlockSpec(memory_space=pltpu.VMEM)] + [any_spec] * 5,
+        scratch_shapes=[
+            pltpu.VMEM((2, tiles, TILE, width), f32),
+            pltpu.VMEM((2, 4, TILE, width), bf16),
+            pltpu.VMEM((2, TILE, width), f32),
+            pltpu.VMEM((2, TILE, width), f32),
+            pltpu.VMEM((8, width), f32),
+            pltpu.VMEM((8, 128), f32),
+            pltpu.VMEM((8, 8, 128), f32),
+            dma((tiles,)), dma((tiles,)), dma((tiles,)), dma((tiles,)), dma((tiles,)),
+            dma((2, 2, tiles)), dma((2, 2, tiles)), dma((4, tiles)), dma((tiles,)), dma((tiles,)),
+            dma((2, 5)), dma((2,)), dma((7,)), dma((8,)),
+        ],
+        compiler_params=pltpu.CompilerParams(collective_id=0, has_side_effects=True, vmem_limit_bytes=56 * 2 ** 20),
+        name='reduce_grads',
+    )(local_grads)
+    return outs[0], outs[1]
+
+
 def solution(mesh):
     dev_count = mesh.shape['dp']
 
@@ -58,9 +263,8 @@
         shard_rows = master.shape[0]
         model_width = master.shape[1]
         total_rows = shard_rows * dev_count
-        grad_shard = lax.psum_scatter(local_grads[0].astype(jnp.float32), 'dp', scatter_dimension=0, tiled=True) / dev_count
-        square_sum = lax.psum(jnp.sum(grad_shard * grad_shard), 'dp')
-        clip_scale = jnp.minimum(1.0, 1.0 / (jnp.sqrt(square_sum) + 1e-6))
+        grad_shard, clip = reduce_grads(local_grads, shard_rows)
+        clip_scale = clip[0, 0]
         row_ids = lax.axis_index('dp') * shard_rows + lax.iota(jnp.int32, shard_rows)
         lr_factor, decay_rate = row_rules(row_ids, model_width, total_rows)
         new_master, new_first, new_second = adam_rows(grad_shard, master, mom_first, mom_second, clip_scale, learn_rate, lr_factor, decay_rate)

time: 1380 us -> 1080 us (0.78)
  waiting for transfers between devices: 1150 us -> 334 us
  Pallas kernels: 0 us -> 622 us
  other arithmetic: 139 us -> 52.8 us
  blocking collectives: 22.5 us -> 0 us
    reduce_scatter x1 -> x0, waiting for transfers between devices: 813 us -> none  [device_step(): lax.psum_scatter(local_grads[0].astype(jnp.float32), 'dp', scatter_dimens...]
    pallas_call x0 -> x1, Pallas kernels: none -> 622 us  [reduce_grads(): pl.pallas_call(functools.partial(reduce_kernel, shard), out_shape=[jax.Sh...]
    convert_element_type x1 -> x0, other arithmetic: 75.4 us -> none  [device_step(): local_grads[0].astype(jnp.float32)]
    psum x1 -> x0, blocking collectives: 22.5 us -> none  [device_step(): square_sum = lax.psum(jnp.sum(grad_shard * grad_shard), 'dp')]
    unnamed x3 -> x1, local copies, waits for them, and re-layouts: 50.3 us -> 50.3 us
  transfers between devices with their start and end apart: 2 -> 1, of which waited for: 2 -> 1; matrix products, arithmetic and copies ran while one was open for 0% -> 0% of each run, Pallas kernels for 0% -> 0%
where the time goes in v1:
time: 1080 us; the launch traced here: 1070 us
  Pallas kernels  622 us (58%)
  waiting for transfers between devices  334 us (31%)
  other arithmetic  52.8 us (5%)
  local copies, waits for them, and re-layouts  51.5 us (5%)
  between operations  14.7 us (1%)
    pallas_call x1, Pallas kernels, reduce_grads(): pl.pallas_call(functools.partial(reduce_kernel, shard), out_shape=[jax.Sh...  622 us
    all_gather x1, waiting for transfers between devices, device_step(): lax.all_gather(new_master.astype(jnp.bfloat16), 'dp', axis=0, tiled=True)  334 us
    convert_element_type x1, other arithmetic, device_step(): new_master.astype(jnp.bfloat16)  51.1 us
    unnamed x1, local copies, waits for them, and re-layouts  50.3 us
  transfers between devices with their start and end apart: 1, of which 1 were waited for; matrix products, arithmetic and copies ran while one was open for 0% of the time, Pallas kernels for 0%

profile of v1, /device:TPU:0, one launch (start us, length us, event | category | flops | bytes accessed | tf_op | source)
XLA Modules:
  0.0 1074.5 jit_solution(15545672254717440365)
XLA Ops:
  7.2 0.0 all-gather.2.cloned.1.call-start
  7.2 0.8 convert_reduce_fusion
  8.0 0.1 compare_select_fusion.2
  8.1 0.1 compare_select_fusion.3
  8.2 0.7 compare_reduce_fusion.9
  9.6 621.7 %reduce_grads.1 = (f32[6144,768]{1,0:T(8,128)}, f32[8,128]{1,0:T(8,128)}, bf16[2,2,3072,768]{3,2,1,0:T(8,128)(2,1)}, bf16[2,2,3072,768]{3,2,1,0:T(8,128)(2,1)}, ...) custom-call(bf16[1,49152,768]{2,1,0:T(8,128)(2,1)} %grads.1), custom_call_target="tpu_custom_call" | custom-call | tf_op jit(solution)/shard_map/reduce_grads/pallas_call | solution.py:228
  631.3 1.2 slice.3
  632.6 51.1 %fusion = (bf16[6144,768]{1,0:T(8,128)(2,1)}, f32[6144,768]{1,0:T(8,128)}, f32[6144,768]{1,0:T(8,128)}, f32[6144,768]{1,0:T(8,128)}) fusion(f32[6144,768]{1,0:T(8,128)} %param.9, f32[6144]{0:T(1024)S(1)} %get-tuple-element.25, f32[6144]{0:T(1024)S(1)} %get-tuple-element.24, f32[6144,768]{1,0:T(8,128)} %get-tuple-element.6, f32[]{:T(128)} %bitcast.2, ...), kind=kLoop, calls=%fused_computation.29 | loop fusion | flops 80216064 | bytes 141606912 | tf_op jit(solution)/shard_map/convert_element_type | solution.py:271
  683.6 0.0 all-gather.2.cloned.1.call-update
  683.7 333.7 %all-gather.2.cloned.1.call-done = bf16[49152,768]{1,0:T(8,128)(2,1)} async-done(((bf16[6144,768]{1,0:T(8,128)(2,1)}), bf16[49152,768]{1,0:T(8,128)(2,1)}) %all-gather.2.cloned.1.call-update) | async-done | bytes 75497488 | tf_op jit(solution)/shard_map/all_gather | solution.py:271
  1017.3 50.3 %copy.14 = bf16[49152,768]{1,0:T(8,128)(2,1)} copy(bf16[49152,768]{1,0:T(8,128)(2,1)} %all-gather.2.cloned.1.call-done) | data formatting | bytes 150994944
  (2 shorter events, 0.0 us)
Async XLA Ops:
  7.2 1010.2 %all-gather.2.cloned.1.call-start = ((), (), s32[]{:S(2)}) async-start(), calls=%async_computation | async-start | bytes 84934656 | tf_op jit(solution)/shard_map/all_gather | solution.py:271
Sparse Core Ops, SparseCore 0:
  683.8 333.5 all-gather.1

commit v2 on v1

--- a/solution.py
+++ b/solution.py
@@ -14,6 +14,11 @@
 MESH = pl.DeviceIdType.MESH
 TILE = 256
 SLAB = 32
+ADAM_TILE = 192
+ADAM_SLAB = 32
+CHUNKS = (384, 384, 768, 768, 1152, 1152, 768, 768)
+ADAM_FLOPS = 60
+PLACE_FLOPS = 16
 
 
 def layout_runs(model_width, total_rows):
@@ -38,26 +43,6 @@
     return run_starts, lr_values, decay_values
 
 
-def row_rules(row_ids, model_width, total_rows):
-    run_starts, lr_values, decay_values = layout_runs(model_width, total_rows)
-    later_starts = jnp.asarray(run_starts[1:], jnp.int32)
-    run_index = jnp.sum((row_ids[:, None] >= later_starts[None, :]).astype(jnp.int32), axis=1)
-    lr_factor = jnp.asarray(lr_values, jnp.float32)[run_index]
-    decay_rate = jnp.asarray(decay_values, jnp.float32)[run_index]
-    return lr_factor[:, None], decay_rate[:, None]
-
-
-def adam_rows(grad_rows, master_rows, first_rows, second_rows, clip_scale, learn_rate, lr_factor, decay_rate):
-    clipped = grad_rows * clip_scale
-    new_first = 0.9 * first_rows + 0.1 * clipped
-    new_second = 0.99 * second_rows + 0.01 * (clipped * clipped)
-    first_hat = new_first / (1.0 - 0.9 ** ADAM_STEP)
-    second_hat = new_second / (1.0 - 0.99 ** ADAM_STEP)
-    step_size = learn_rate * lr_factor
-    new_master = master_rows - step_size * (first_hat / (jnp.sqrt(second_hat) + 1e-8) + decay_rate * master_rows)
-    return new_master, new_first, new_second
-
-
 def places():
     me = lax.axis_index('dp')
     core = me % 2
@@ -84,7 +69,7 @@
     tiles = half // TILE
     me, core, mate, x_chip, y_chip, d_chip = places()
     mate_core = 1 - core
-    x_peer, y_peer, d_peer = x_chip * 2 + core, y_chip * 2 + core, d_chip * 2 + core
+    x_peer, y_peer = x_chip * 2 + core, y_chip * 2 + core
     everyone = [mate, x_chip * 2, x_chip * 2 + 1, y_chip * 2, y_chip * 2 + 1, d_chip * 2, d_chip * 2 + 1]
     greet(everyone)
 
@@ -200,7 +185,7 @@
         pltpu.make_async_copy(finals.at[part], total_tile(part, 0), store_sem.at[part]).wait()
     for k, partner in enumerate(everyone):
         remote(norm_mine, norm_all.at[me], norm_sent.at[k], norm_got.at[me], partner).start()
-    for k, partner in enumerate(everyone):
+    for partner in everyone:
         arrived(norm_all.at[partner], norm_got.at[partner])
     squared = norm_all[0]
     for k in range(1, 8):
@@ -256,19 +241,136 @@
     return outs[0], outs[1]
 
 
+def adam_kernel(first_row, shard, total_rows, rate_ref, clip_ref, grad, master, first, second, *refs):
+    new_master, new_first, new_second, rounded = refs[-4:]
+    width = grad.shape[1]
+    run_starts, lr_values, decay_values = layout_runs(width, total_rows)
+    start = lax.axis_index('dp') * shard + first_row + pl.program_id(0) * ADAM_TILE
+    rate = rate_ref[0]
+    clip_scale = clip_ref[0:1, 0:1]
+
+    @pl.loop(0, ADAM_TILE // ADAM_SLAB)
+    def _(slab):
+        at = pl.ds(pl.multiple_of(slab * ADAM_SLAB, ADAM_SLAB), ADAM_SLAB)
+        row = start + slab * ADAM_SLAB + lax.broadcasted_iota(jnp.int32, (ADAM_SLAB, 128), 0)
+        lr_factor = jnp.full((ADAM_SLAB, 128), lr_values[0], jnp.float32)
+        decay = jnp.full((ADAM_SLAB, 128), decay_values[0], jnp.float32)
+        for k in range(1, len(run_starts)):
+            later = row >= run_starts[k]
+            if lr_values[k] != lr_values[k - 1]:
+                lr_factor = jnp.where(later, lr_values[k], lr_factor)
+            if decay_values[k] != decay_values[k - 1]:
+                decay = jnp.where(later, decay_values[k], decay)
+        step_size = rate * lr_factor
+        for lane in range(width // 128):
+            cols = pl.ds(lane * 128, 128)
+            clipped = grad[at, cols] * clip_scale
+            old = master[at, cols]
+            next_first = 0.9 * first[at, cols] + 0.1 * clipped
+            next_second = 0.99 * second[at, cols] + 0.01 * (clipped * clipped)
+            first_hat = next_first / (1.0 - 0.9 ** ADAM_STEP)
+            second_hat = next_second / (1.0 - 0.99 ** ADAM_STEP)
+            value = old - step_size * (first_hat / (jnp.sqrt(second_hat) + 1e-8) + decay * old)
+            new_first[at, cols] = next_first
+            new_second[at, cols] = next_second
+            new_master[at, cols] = value
+            rounded[at, cols] = value.astype(jnp.bfloat16)
+
+
+def adam_chunk(first_row, chunk, rate, clip, grad, states, previous, total_rows):
+    shard, width = grad.shape
+    block = pl.BlockSpec((ADAM_TILE, width), lambda step: (first_row // ADAM_TILE + step, 0))
+    own = pl.BlockSpec((ADAM_TILE, width), lambda step: (step, 0))
+    any_spec = pl.BlockSpec(memory_space=pl.ANY)
+    smem = pl.BlockSpec(memory_space=pltpu.SMEM)
+    vmem = pl.BlockSpec((8, 128), lambda step: (0, 0))
+    full = jax.ShapeDtypeStruct((shard, width), jnp.float32)
+    return pl.pallas_call(
+        functools.partial(adam_kernel, first_row, shard, total_rows),
+        grid=(chunk // ADAM_TILE,),
+        out_shape=[full] * 3 + [jax.ShapeDtypeStruct((chunk, width), jnp.bfloat16)],
+        in_specs=[smem, vmem] + [block] * 4 + [any_spec] * len(previous),
+        out_specs=[block] * 3 + [own],
+        input_output_aliases={6 + k: k for k in range(len(previous))},
+        compiler_params=pltpu.CompilerParams(vmem_limit_bytes=56 * 2 ** 20),
+        cost_estimate=pl.CostEstimate(flops=ADAM_FLOPS * chunk * width, bytes_accessed=30 * chunk * width, transcendentals=0),
+    )(rate, clip, grad, *states, *previous)
+
+
+def place_kernel(count, shard, first_row, partners, *refs):
+    pieces = refs[:count]
+    target, held, loaded, stored = refs[-4:]
+    me, core, _, x_chip, y_chip, d_chip = places()
+    chips = {'m': me // 2, 'x': x_chip, 'y': y_chip, 'd': d_chip}
+    rows = held.shape[1]
+    for k in range(count):
+        pltpu.make_async_copy(pieces[k], held.at[k], loaded.at[k]).start()
+
+    def store(k):
+        chip, far = partners[k]
+        owner = chips[chip] * 2 + (core if far == 0 else 1 - core)
+        at = pl.multiple_of(owner * shard + first_row, 128)
+        return pltpu.make_async_copy(held.at[k], target.at[pl.ds(at, rows)], stored.at[k])
+
+    for k in range(count):
+        pltpu.make_async_copy(pieces[k], held.at[k], loaded.at[k]).wait()
+        store(k).start()
+    for k in range(count):
+        store(k).wait()
+
+
+def place(shard, first_row, labelled, target, total_rows):
+    pieces = [piece for _, piece in labelled]
+    partners = [label for label, _ in labelled]
+    rows, width = pieces[0].shape
+    count = len(pieces)
+    any_spec = pl.BlockSpec(memory_space=pl.ANY)
+    previous = [] if target is None else [target]
+    return pl.pallas_call(
+        functools.partial(place_kernel, count, shard, first_row, partners),
+        out_shape=jax.ShapeDtypeStruct((total_rows, width), jnp.bfloat16),
+        in_specs=[any_spec] * (count + len(previous)),
+        out_specs=any_spec,
+        scratch_shapes=[pltpu.VMEM((count, rows, width), jnp.bfloat16), pltpu.SemaphoreType.DMA((count,)), pltpu.SemaphoreType.DMA((count,))],
+        input_output_aliases={count: 0} if previous else {},
+        compiler_params=pltpu.CompilerParams(vmem_limit_bytes=56 * 2 ** 20),
+        cost_estimate=pl.CostEstimate(flops=PLACE_FLOPS * count * rows * width, bytes_accessed=4 * count * rows * width, transcendentals=0),
+    )(*pieces, *previous)
+
+
+def swap(value, bit):
+    return lax.ppermute(value, 'dp', [(i, i ^ bit) for i in range(8)])
+
+
 def solution(mesh):
     dev_count = mesh.shape['dp']
 
     def device_step(local_grads, master, mom_first, mom_second, learn_rate):
-        shard_rows = master.shape[0]
-        model_width = master.shape[1]
-        total_rows = shard_rows * dev_count
-        grad_shard, clip = reduce_grads(local_grads, shard_rows)
-        clip_scale = clip[0, 0]
-        row_ids = lax.axis_index('dp') * shard_rows + lax.iota(jnp.int32, shard_rows)
-        lr_factor, decay_rate = row_rules(row_ids, model_width, total_rows)
-        new_master, new_first, new_second = adam_rows(grad_shard, master, mom_first, mom_second, clip_scale, learn_rate, lr_factor, decay_rate)
-        working = lax.all_gather(new_master.astype(jnp.bfloat16), 'dp', axis=0, tiled=True)
-        return new_master, new_first, new_second, working
+        shard = master.shape[0]
+        total_rows = shard * dev_count
+        grad_shard, clip = reduce_grads(local_grads, shard)
+        rate = learn_rate.reshape(1)
+        previous = []
+        chunks = []
+        first_row = 0
+        for chunk in CHUNKS:
+            outs = adam_chunk(first_row, chunk, rate, clip, grad_shard, (master, mom_first, mom_second), previous, total_rows)
+            previous = list(outs[:3])
+            chunks.append((first_row, outs[3]))
+            first_row += chunk
+        target = None
+        pieces = []
+        for index, (first_row, mine) in enumerate(chunks):
+            from_x = swap(mine, 2)
+            from_y = swap(mine, 4)
+            from_d = swap(from_x, 4) if index % 2 == 0 else swap(from_y, 2)
+            near = [(('m', 0), mine), (('m', 1), swap(mine, 1)), (('x', 0), from_x), (('x', 1), swap(from_x, 1)), (('y', 0), from_y), (('y', 1), swap(from_y, 1))]
+            far = [(('d', 0), from_d), (('d', 1), swap(from_d, 1))]
+            pieces.append((first_row, near, far))
+        for first_row, near, far in pieces:
+            target = place(shard, first_row, near, target, total_rows)
+        for first_row, near, far in pieces:
+            target = place(shard, first_row, far, target, total_rows)
+        return (*previous, target)
 
     return jax.shard_map(device_step, mesh=mesh, in_specs=(P('dp', None, None), P('dp', None), P('dp', None), P('dp', None), P()), out_specs=(P('dp', None), P('dp', None), P('dp', None), P(None, None)), check_vma=False)

time: 1080 us -> 1020 us (0.944)
  Pallas kernels: 622 us -> 759 us
  waiting for transfers between devices: 334 us -> 231 us
  other arithmetic: 52.8 us -> 0 us
  local copies, waits for them, and re-layouts: 51.5 us -> 3.51 us
  starting transfers between devices: 0.04 us -> 24.4 us
  between operations: 14.7 us -> 1.81 us
    all_gather x1 -> x0, waiting for transfers between devices: 334 us -> none  [device_step(): lax.all_gather(new_master.astype(jnp.bfloat16), 'dp', axis=0, tiled=True)]
    ppermute x0 -> x56, waiting for transfers between devices: none -> 231 us  [swap(): return lax.ppermute(value, 'dp', [(i, i ^ bit) for i in range(8)])]
    pallas_call x0 -> x24, Pallas kernels: none -> 137 us  [the longest x8 69.4 us: adam_chunk(): pl.pallas_call(functools.partial(adam_kernel, first_row, shard, total_row...]
    convert_element_type x1 -> x0, other arithmetic: 51.1 us -> none  [device_step(): new_master.astype(jnp.bfloat16)]
    unnamed x1 -> x84, local copies, waits for them, and re-layouts: 50.3 us -> 3.51 us
    ppermute x0 -> x56, starting transfers between devices: none -> 24.4 us  [swap(): return lax.ppermute(value, 'dp', [(i, i ^ bit) for i in range(8)])]
  transfers between devices with their start and end apart: 1 -> 56, of which waited for: 1 -> 24; matrix products, arithmetic and copies ran while one was open for 0% -> 0% of each run, Pallas kernels for 0% -> 13%
where the time goes in v2:
time: 1020 us
  Pallas kernels  759 us (74%)
  waiting for transfers between devices  231 us (23%)
  starting transfers between devices  24.4 us (2%)
    pallas_call x1, Pallas kernels, reduce_grads(): pl.pallas_call(functools.partial(reduce_kernel, shard), out_shape=[jax.Sh...  622 us
    ppermute x56, waiting for transfers between devices, swap(): return lax.ppermute(value, 'dp', [(i, i ^ bit) for i in range(8)])  231 us
    pallas_call x8, Pallas kernels, adam_chunk(): pl.pallas_call(functools.partial(adam_kernel, first_row, shard, total_row...  69.4 us
    pallas_call x16, Pallas kernels, place(): pl.pallas_call(functools.partial(place_kernel, count, shard, first_row, p...  67.7 us
    ppermute x56, starting transfers between devices, swap(): return lax.ppermute(value, 'dp', [(i, i ^ bit) for i in range(8)])  24.4 us
  transfers between devices with their start and end apart: 56, of which 24 were waited for; matrix products, arithmetic and copies ran while one was open for 0% of the time, Pallas kernels for 13%

profile of v2, /device:TPU:0, one launch (start us, length us, event | category | flops | bytes accessed | tf_op | source)
XLA Modules:
  0.0 1019.9 jit_solution(6626609182634369859)
XLA Ops:
  0.6 621.9 %reduce_grads.1 = (f32[6144,768]{1,0:T(8,128)}, f32[8,128]{1,0:T(8,128)}, bf16[2,2,3072,768]{3,2,1,0:T(8,128)(2,1)}, bf16[2,2,3072,768]{3,2,1,0:T(8,128)(2,1)}, ...) custom-call(bf16[1,49152,768]{2,1,0:T(8,128)(2,1)} %grads.1), custom_call_target="tpu_custom_call" | custom-call | tf_op jit(solution)/shard_map/reduce_grads/pallas_call | solution.py:213
  623.2 4.7 shard_map.84
  629.9 4.7 shard_map.85
  636.6 7.7 collective-permute-done.21.refs_2_
  646.3 8.6 shard_map.86
  659.6 8.7 shard_map.87
  670.0 12.6 %shard_map.88 = (f32[6144,768]{1,0:T(8,128)}, f32[6144,768]{1,0:T(8,128)}, f32[6144,768]{1,0:T(8,128)}, bf16[1152,768]{1,0:T(8,128)(2,1)}) custom-call(f32[1]{0:T(128)} %bitcast.5.rate_ref, f32[8,128]{1,0:T(8,128)} %get-tuple-element.38.clip_ref, f32[6144,768]{1,0:T(8,128)} %get-tuple-element.39.grad, ...), custom_call_target="tpu_custom_call", output_to_operand_aliasing={{0}: (6, {}), {1}: (7, {}), {2}: (8, {})} | custom-call | flops 53084160 | bytes 26542080 | tf_op jit(solution)/shard_map/pallas_call | solution.py:288
  684.1 12.6 %shard_map.89 = (f32[6144,768]{1,0:T(8,128)}, f32[6144,768]{1,0:T(8,128)}, f32[6144,768]{1,0:T(8,128)}, bf16[1152,768]{1,0:T(8,128)(2,1)}) custom-call(f32[1]{0:T(128)} %bitcast.6.rate_ref, f32[8,128]{1,0:T(8,128)} %get-tuple-element.38.clip_ref, f32[6144,768]{1,0:T(8,128)} %get-tuple-element.39.grad, ...), custom_call_target="tpu_custom_call", output_to_operand_aliasing={{0}: (6, {}), {1}: (7, {}), {2}: (8, {})} | custom-call | flops 53084160 | bytes 26542080 | tf_op jit(solution)/shard_map/pallas_call | solution.py:288
  696.8 8.9 shard_map.90
  707.5 3.1 collective-permute-done.41.refs_2_
  711.6 8.7 shard_map.91
  722.4 13.6 %collective-permute-done.3.refs_2_ = bf16[768,768]{1,0:T(8,128)(2,1)} collective-permute-done((bf16[768,768]{1,0:T(8,128)(2,1)}, bf16[768,768]{1,0:T(8,128)(2,1)}, u32[]{:S(2)}, u32[]{:S(2)}) %collective-permute-start.3) | collective-permute-done | bytes 1179680 | tf_op jit(solution)/shard_map/ppermute | solution.py:342
  738.0 23.1 %collective-permute-done.25.refs_2_ = bf16[768,768]{1,0:T(8,128)(2,1)S(1)} collective-permute-done((bf16[768,768]{1,0:T(8,128)(2,1)}, bf16[768,768]{1,0:T(8,128)(2,1)S(1)}, u32[]{:S(2)}, u32[]{:S(2)}) %collective-permute-start.25) | collective-permute-done | bytes 1179680 | tf_op jit(solution)/shard_map/ppermute | solution.py:342
  761.7 3.3 collective-permute-done.refs_4_
  765.6 12.1 %collective-permute-done.22.refs_0_ = bf16[384,768]{1,0:T(8,128)(2,1)S(1)} collective-permute-done((bf16[384,768]{1,0:T(8,128)(2,1)}, bf16[384,768]{1,0:T(8,128)(2,1)S(1)}, u32[]{:S(2)}, u32[]{:S(2)}) %collective-permute-start.22) | collective-permute-done | bytes 589856 | tf_op jit(solution)/shard_map/ppermute | solution.py:342
  778.2 33.5 %collective-permute-done.19.refs_0_ = bf16[384,768]{1,0:T(8,128)(2,1)S(1)} collective-permute-done((bf16[384,768]{1,0:T(8,128)(2,1)}, bf16[384,768]{1,0:T(8,128)(2,1)S(1)}, u32[]{:S(2)}, u32[]{:S(2)}) %collective-permute-start.19) | collective-permute-done | bytes 589856 | tf_op jit(solution)/shard_map/ppermute | solution.py:342
  813.6 35.0 %collective-permute-done.33.refs_2_ = bf16[1152,768]{1,0:T(8,128)(2,1)S(1)} collective-permute-done((bf16[1152,768]{1,0:T(8,128)(2,1)S(1)}, bf16[1152,768]{1,0:T(8,128)(2,1)S(1)}, u32[]{:S(2)}, u32[]{:S(2)}) %collective-permute-start.33) | collective-permute-done | bytes 1769504 | tf_op jit(solution)/shard_map/ppermute | solution.py:342
  851.3 3.3 collective-permute-done.20.refs_1_
  863.6 21.5 %collective-permute-done.16.refs_0_ = bf16[768,768]{1,0:T(8,128)(2,1)S(1)} collective-permute-done((bf16[768,768]{1,0:T(8,128)(2,1)S(1)}, bf16[768,768]{1,0:T(8,128)(2,1)S(1)}, u32[]{:S(2)}, u32[]{:S(2)}) %collective-permute-start.16) | collective-permute-done | bytes 1179680 | tf_op jit(solution)/shard_map/ppermute | solution.py:342
  887.7 22.8 %collective-permute-done.4.refs_0_ = bf16[768,768]{1,0:T(8,128)(2,1)} collective-permute-done((bf16[768,768]{1,0:T(8,128)(2,1)}, bf16[768,768]{1,0:T(8,128)(2,1)}, u32[]{:S(2)}, u32[]{:S(2)}) %collective-permute-start.4) | collective-permute-done | bytes 1179680 | tf_op jit(solution)/shard_map/ppermute | solution.py:342
  912.2 35.4 %collective-permute-done.10.refs_0_ = bf16[1152,768]{1,0:T(8,128)(2,1)} collective-permute-done((bf16[1152,768]{1,0:T(8,128)(2,1)S(1)}, bf16[1152,768]{1,0:T(8,128)(2,1)}, u32[]{:S(2)}, u32[]{:S(2)}) %collective-permute-start.10) | collective-permute-done | bytes 1769504 | tf_op jit(solution)/shard_map/ppermute | solution.py:342
  952.0 3.0 shard_map.92.refs_6_
  955.0 3.0 shard_map.93.refs_6_
  958.0 5.9 shard_map.94.refs_6_
  963.9 5.9 shard_map.95.refs_6_
  969.7 8.3 shard_map.96.refs_6_
  978.0 8.3 shard_map.97.refs_6_
  986.4 5.9 shard_map.98.refs_6_
  992.2 5.9 shard_map.99.refs_2_
  1002.4 2.7 shard_map.102.refs_2_
  1007.8 3.3 shard_map.104.refs_2_
  1011.1 3.3 shard_map.105.refs_2_
  (189 shorter events, 56.9 us)
Async XLA Ops:
  657.3 39.4 %collective-permute-start.15 = (bf16[768,768]{1,0:T(8,128)(2,1)}, bf16[768,768]{1,0:T(8,128)(2,1)S(1)}, u32[]{:S(2)}, u32[]{:S(2)}) collective-permute-start(bf16[768,768]{1,0:T(8,128)(2,1)} %get-tuple-element.69.refs_0_), channel_id=1, source_target_pairs={{0,2},{1,3},{2,0},{3,1},{4,6},{5,7},{6,4},{7,5}} | collective-permute-start | bytes 3538952 | tf_op jit(solution)/shard_map/ppermute | solution.py:342
  657.8 47.9 %collective-permute-start.46 = (bf16[768,768]{1,0:T(8,128)(2,1)}, bf16[768,768]{1,0:T(8,128)(2,1)S(1)}, u32[]{:S(2)}, u32[]{:S(2)}) collective-permute-start(bf16[768,768]{1,0:T(8,128)(2,1)} %get-tuple-element.69.refs_0_), channel_id=1, source_target_pairs={{0,4},{1,5},{2,6},{3,7},{4,0},{5,1},{6,2},{7,3}} | collective-permute-start | bytes 3538952 | tf_op jit(solution)/shard_map/ppermute | solution.py:342
  659.0 47.3 %collective-permute-start.44 = (bf16[768,768]{1,0:T(8,128)(2,1)}, bf16[768,768]{1,0:T(8,128)(2,1)S(1)}, u32[]{:S(2)}, u32[]{:S(2)}) collective-permute-start(bf16[768,768]{1,0:T(8,128)(2,1)} %get-tuple-element.69.refs_0_), channel_id=1, source_target_pairs={{0,1},{1,0},{2,3},{3,2},{4,5},{5,4},{6,7},{7,6}} | collective-permute-start | bytes 3538952 | tf_op jit(solution)/shard_map/ppermute | solution.py:342
  669.2 41.4 %collective-permute-start.41 = (bf16[768,768]{1,0:T(8,128)(2,1)}, bf16[768,768]{1,0:T(8,128)(2,1)S(1)}, u32[]{:S(2)}, u32[]{:S(2)}) collective-permute-start(bf16[768,768]{1,0:T(8,128)(2,1)} %get-tuple-element.68.refs_0_), channel_id=1, source_target_pairs={{0,2},{1,3},{2,0},{3,1},{4,6},{5,7},{6,4},{7,5}} | collective-permute-start | bytes 3538952 | tf_op jit(solution)/shard_map/ppermute | solution.py:342
  682.6 37.7 %collective-permute-start.12 = (bf16[768,768]{1,0:T(8,128)(2,1)S(1)}, bf16[768,768]{1,0:T(8,128)(2,1)}, u32[]{:S(2)}, u32[]{:S(2)}) collective-permute-start(bf16[768,768]{1,0:T(8,128)(2,1)S(1)} %copy-done.15), channel_id=1, source_target_pairs={{0,4},{1,5},{2,6},{3,7},{4,0},{5,1},{6,2},{7,3}} | collective-permute-start | bytes 3538952 | tf_op jit(solution)/shard_map/ppermute | solution.py:342
  705.7 30.2 %collective-permute-start.3 = (bf16[768,768]{1,0:T(8,128)(2,1)}, bf16[768,768]{1,0:T(8,128)(2,1)}, u32[]{:S(2)}, u32[]{:S(2)}) collective-permute-start(bf16[768,768]{1,0:T(8,128)(2,1)} %get-tuple-element.65.refs_0_), channel_id=1, source_target_pairs={{0,2},{1,3},{2,0},{3,1},{4,6},{5,7},{6,4},{7,5}} | collective-permute-start | bytes 3538952 | tf_op jit(solution)/shard_map/ppermute | solution.py:342
  706.3 30.2 %collective-permute-start.30 = (bf16[768,768]{1,0:T(8,128)(2,1)}, bf16[768,768]{1,0:T(8,128)(2,1)}, u32[]{:S(2)}, u32[]{:S(2)}) collective-permute-start(bf16[768,768]{1,0:T(8,128)(2,1)} %get-tuple-element.65.refs_0_), channel_id=1, source_target_pairs={{0,4},{1,5},{2,6},{3,7},{4,0},{5,1},{6,2},{7,3}} | collective-permute-start | bytes 3538952 | tf_op jit(solution)/shard_map/ppermute | solution.py:342
  720.3 40.8 %collective-permute-start.25 = (bf16[768,768]{1,0:T(8,128)(2,1)}, bf16[768,768]{1,0:T(8,128)(2,1)S(1)}, u32[]{:S(2)}, u32[]{:S(2)}) collective-permute-start(bf16[768,768]{1,0:T(8,128)(2,1)} %get-tuple-element.64.refs_0_), channel_id=1, source_target_pairs={{0,2},{1,3},{2,0},{3,1},{4,6},{5,7},{6,4},{7,5}} | collective-permute-start | bytes 3538952 | tf_op jit(solution)/shard_map/ppermute | solution.py:342
  720.9 91.4 %collective-permute-start.9 = (bf16[1152,768]{1,0:T(8,128)(2,1)S(1)}, bf16[1152,768]{1,0:T(8,128)(2,1)S(1)}, u32[]{:S(2)}, u32[]{:S(2)}) collective-permute-start(bf16[1152,768]{1,0:T(8,128)(2,1)S(1)} %copy-done), channel_id=1, source_target_pairs={{0,2},{1,3},{2,0},{3,1},{4,6},{5,7},{6,4},{7,5}} | collective-permute-start | bytes 5308424 | tf_op jit(solution)/shard_map/ppermute | solution.py:342
  736.5 41.1 %collective-permute-start.22 = (bf16[384,768]{1,0:T(8,128)(2,1)}, bf16[384,768]{1,0:T(8,128)(2,1)S(1)}, u32[]{:S(2)}, u32[]{:S(2)}) collective-permute-start(bf16[384,768]{1,0:T(8,128)(2,1)} %copy-done.29), channel_id=1, source_target_pairs={{0,4},{1,5},{2,6},{3,7},{4,0},{5,1},{6,2},{7,3}} | collective-permute-start | bytes 1769480 | tf_op jit(solution)/shard_map/ppermute | solution.py:342
  761.1 50.6 %collective-permute-start.19 = (bf16[384,768]{1,0:T(8,128)(2,1)}, bf16[384,768]{1,0:T(8,128)(2,1)S(1)}, u32[]{:S(2)}, u32[]{:S(2)}) collective-permute-start(bf16[384,768]{1,0:T(8,128)(2,1)} %copy-done.32), channel_id=1, source_target_pairs={{0,2},{1,3},{2,0},{3,1},{4,6},{5,7},{6,4},{7,5}} | collective-permute-start | bytes 1769480 | tf_op jit(solution)/shard_map/ppermute | solution.py:342
  765.0 48.1 %collective-permute-start.38 = (bf16[1152,768]{1,0:T(8,128)(2,1)S(1)}, bf16[1152,768]{1,0:T(8,128)(2,1)S(1)}, u32[]{:S(2)}, u32[]{:S(2)}) collective-permute-start(bf16[1152,768]{1,0:T(8,128)(2,1)S(1)} %copy-done), channel_id=1, source_target_pairs={{0,4},{1,5},{2,6},{3,7},{4,0},{5,1},{6,2},{7,3}} | collective-permute-start | bytes 5308424 | tf_op jit(solution)/shard_map/ppermute | solution.py:342
  765.6 47.6 %collective-permute-start.36 = (bf16[1152,768]{1,0:T(8,128)(2,1)S(1)}, bf16[1152,768]{1,0:T(8,128)(2,1)S(1)}, u32[]{:S(2)}, u32[]{:S(2)}) collective-permute-start(bf16[1152,768]{1,0:T(8,128)(2,1)S(1)} %copy-done), channel_id=1, source_target_pairs={{0,1},{1,0},{2,3},{3,2},{4,5},{5,4},{6,7},{7,6}} | collective-permute-start | bytes 5308424 | tf_op jit(solution)/shard_map/ppermute | solution.py:342
  777.6 71.0 %collective-permute-start.33 = (bf16[1152,768]{1,0:T(8,128)(2,1)S(1)}, bf16[1152,768]{1,0:T(8,128)(2,1)S(1)}, u32[]{:S(2)}, u32[]{:S(2)}) collective-permute-start(bf16[1152,768]{1,0:T(8,128)(2,1)S(1)} %copy-done.1), channel_id=1, source_target_pairs={{0,2},{1,3},{2,0},{3,1},{4,6},{5,7},{6,4},{7,5}} | collective-permute-start | bytes 5308424 | tf_op jit(solution)/shard_map/ppermute | solution.py:342
  811.7 39.0 %collective-permute-start.6 = (bf16[1152,768]{1,0:T(8,128)(2,1)S(1)}, bf16[1152,768]{1,0:T(8,128)(2,1)S(1)}, u32[]{:S(2)}, u32[]{:S(2)}) collective-permute-start(bf16[1152,768]{1,0:T(8,128)(2,1)S(1)} %copy-done.1), channel_id=1, source_target_pairs={{0,4},{1,5},{2,6},{3,7},{4,0},{5,1},{6,2},{7,3}} | collective-permute-start | bytes 5308424 | tf_op jit(solution)/shard_map/ppermute | solution.py:342
  812.2 38.5 %collective-permute-start.32 = (bf16[1152,768]{1,0:T(8,128)(2,1)S(1)}, bf16[1152,768]{1,0:T(8,128)(2,1)S(1)}, u32[]{:S(2)}, u32[]{:S(2)}) collective-permute-start(bf16[1152,768]{1,0:T(8,128)(2,1)S(1)} %copy-done.1), channel_id=1, source_target_pairs={{0,1},{1,0},{2,3},{3,2},{4,5},{5,4},{6,7},{7,6}} | collective-permute-start | bytes 5308424 | tf_op jit(solution)/shard_map/ppermute | solution.py:342
  813.1 41.7 %collective-permute-start.45 = (bf16[768,768]{1,0:T(8,128)(2,1)S(1)}, bf16[768,768]{1,0:T(8,128)(2,1)S(1)}, u32[]{:S(2)}, u32[]{:S(2)}) collective-permute-start(bf16[768,768]{1,0:T(8,128)(2,1)S(1)} %collective-permute-done.15.refs_2_), channel_id=1, source_target_pairs={{0,1},{1,0},{2,3},{3,2},{4,5},{5,4},{6,7},{7,6}} | collective-permute-start | bytes 3538952 | tf_op jit(solution)/shard_map/ppermute | solution.py:342
  813.1 42.3 %collective-permute-start.47 = (bf16[768,768]{1,0:T(8,128)(2,1)S(1)}, bf16[768,768]{1,0:T(8,128)(2,1)S(1)}, u32[]{:S(2)}, u32[]{:S(2)}) collective-permute-start(bf16[768,768]{1,0:T(8,128)(2,1)S(1)} %collective-permute-done.46.refs_4_), channel_id=1, source_target_pairs={{0,1},{1,0},{2,3},{3,2},{4,5},{5,4},{6,7},{7,6}} | collective-permute-start | bytes 3538952 | tf_op jit(solution)/shard_map/ppermute | solution.py:342
  858.0 29.2 %collective-permute-start.13 = (bf16[768,768]{1,0:T(8,128)(2,1)}, bf16[768,768]{1,0:T(8,128)(2,1)}, u32[]{:S(2)}, u32[]{:S(2)}) collective-permute-start(bf16[768,768]{1,0:T(8,128)(2,1)} %collective-permute-done.12.refs_4_), channel_id=1, source_target_pairs={{0,2},{1,3},{2,0},{3,1},{4,6},{5,7},{6,4},{7,5}} | collective-permute-start | bytes 3538952 | tf_op jit(solution)/shard_map/ppermute | solution.py:342
  859.7 50.9 %collective-permute-start.4 = (bf16[768,768]{1,0:T(8,128)(2,1)}, bf16[768,768]{1,0:T(8,128)(2,1)}, u32[]{:S(2)}, u32[]{:S(2)}) collective-permute-start(bf16[768,768]{1,0:T(8,128)(2,1)} %collective-permute-done.3.refs_2_), channel_id=1, source_target_pairs={{0,4},{1,5},{2,6},{3,7},{4,0},{5,1},{6,2},{7,3}} | collective-permute-start | bytes 3538952 | tf_op jit(solution)/shard_map/ppermute | solution.py:342
  861.4 50.2 %collective-permute-start.37 = (bf16[1152,768]{1,0:T(8,128)(2,1)S(1)}, bf16[1152,768]{1,0:T(8,128)(2,1)S(1)}, u32[]{:S(2)}, u32[]{:S(2)}) collective-permute-start(bf16[1152,768]{1,0:T(8,128)(2,1)S(1)} %collective-permute-done.9.refs_2_), channel_id=1, source_target_pairs={{0,1},{1,0},{2,3},{3,2},{4,5},{5,4},{6,7},{7,6}} | collective-permute-start | bytes 5308424 | tf_op jit(solution)/shard_map/ppermute | solution.py:342
  863.1 48.5 %collective-permute-start.1 = (bf16[768,768]{1,0:T(8,128)(2,1)S(1)}, bf16[768,768]{1,0:T(8,128)(2,1)}, u32[]{:S(2)}, u32[]{:S(2)}) collective-permute-start(bf16[768,768]{1,0:T(8,128)(2,1)S(1)} %collective-permute-done.refs_4_), channel_id=1, source_target_pairs={{0,2},{1,3},{2,0},{3,1},{4,6},{5,7},{6,4},{7,5}} | collective-permute-start | bytes 3538952 | tf_op jit(solution)/shard_map/ppermute | solution.py:342
  887.2 60.5 %collective-permute-start.10 = (bf16[1152,768]{1,0:T(8,128)(2,1)S(1)}, bf16[1152,768]{1,0:T(8,128)(2,1)}, u32[]{:S(2)}, u32[]{:S(2)}) collective-permute-start(bf16[1152,768]{1,0:T(8,128)(2,1)S(1)} %collective-permute-done.9.refs_2_), channel_id=1, source_target_pairs={{0,4},{1,5},{2,6},{3,7},{4,0},{5,1},{6,2},{7,3}} | collective-permute-start | bytes 5308424 | tf_op jit(solution)/shard_map/ppermute | solution.py:342
  910.5 39.1 %collective-permute-start.7 = (bf16[1152,768]{1,0:T(8,128)(2,1)S(1)}, bf16[1152,768]{1,0:T(8,128)(2,1)}, u32[]{:S(2)}, u32[]{:S(2)}) collective-permute-start(bf16[1152,768]{1,0:T(8,128)(2,1)S(1)} %collective-permute-done.6.refs_4_), channel_id=1, source_target_pairs={{0,2},{1,3},{2,0},{3,1},{4,6},{5,7},{6,4},{7,5}} | collective-permute-start | bytes 5308424 | tf_op jit(solution)/shard_map/ppermute | solution.py:342
  911.6 38.0 %collective-permute-start.34 = (bf16[1152,768]{1,0:T(8,128)(2,1)S(1)}, bf16[1152,768]{1,0:T(8,128)(2,1)S(1)}, u32[]{:S(2)}, u32[]{:S(2)}) collective-permute-start(bf16[1152,768]{1,0:T(8,128)(2,1)S(1)} %collective-permute-done.33.refs_2_), channel_id=1, source_target_pairs={{0,1},{1,0},{2,3},{3,2},{4,5},{5,4},{6,7},{7,6}} | collective-permute-start | bytes 5308424 | tf_op jit(solution)/shard_map/ppermute | solution.py:342
  911.6 38.5 %collective-permute-start.35 = (bf16[1152,768]{1,0:T(8,128)(2,1)S(1)}, bf16[1152,768]{1,0:T(8,128)(2,1)S(1)}, u32[]{:S(2)}, u32[]{:S(2)}) collective-permute-start(bf16[1152,768]{1,0:T(8,128)(2,1)S(1)} %collective-permute-done.6.refs_4_), channel_id=1, source_target_pairs={{0,1},{1,0},{2,3},{3,2},{4,5},{5,4},{6,7},{7,6}} | collective-permute-start | bytes 5308424 | tf_op jit(solution)/shard_map/ppermute | solution.py:342
  912.1 38.1 %collective-permute-start.17 = (bf16[768,768]{1,0:T(8,128)(2,1)S(1)}, bf16[768,768]{1,0:T(8,128)(2,1)S(1)}, u32[]{:S(2)}, u32[]{:S(2)}) collective-permute-start(bf16[768,768]{1,0:T(8,128)(2,1)S(1)} %collective-permute-done.16.refs_0_), channel_id=1, source_target_pairs={{0,1},{1,0},{2,3},{3,2},{4,5},{5,4},{6,7},{7,6}} | collective-permute-start | bytes 3538952 | tf_op jit(solution)/shard_map/ppermute | solution.py:342
  947.6 60.2 %collective-permute-start.11 = (bf16[1152,768]{1,0:T(8,128)(2,1)}, bf16[1152,768]{1,0:T(8,128)(2,1)}, u32[]{:S(2)}, u32[]{:S(2)}) collective-permute-start(bf16[1152,768]{1,0:T(8,128)(2,1)} %collective-permute-done.10.refs_0_), channel_id=1, source_target_pairs={{0,1},{1,0},{2,3},{3,2},{4,5},{5,4},{6,7},{7,6}} | collective-permute-start | bytes 5308424 | tf_op jit(solution)/shard_map/ppermute | solution.py:342
  949.6 61.5 %collective-permute-start.8 = (bf16[1152,768]{1,0:T(8,128)(2,1)}, bf16[1152,768]{1,0:T(8,128)(2,1)}, u32[]{:S(2)}, u32[]{:S(2)}) collective-permute-start(bf16[1152,768]{1,0:T(8,128)(2,1)} %collective-permute-done.7.refs_0_), channel_id=1, source_target_pairs={{0,1},{1,0},{2,3},{3,2},{4,5},{5,4},{6,7},{7,6}} | collective-permute-start | bytes 5308424 | tf_op jit(solution)/shard_map/ppermute | solution.py:342
  949.6 55.4 %collective-permute-start.14 = (bf16[768,768]{1,0:T(8,128)(2,1)}, bf16[768,768]{1,0:T(8,128)(2,1)}, u32[]{:S(2)}, u32[]{:S(2)}) collective-permute-start(bf16[768,768]{1,0:T(8,128)(2,1)} %collective-permute-done.13.refs_0_), channel_id=1, source_target_pairs={{0,1},{1,0},{2,3},{3,2},{4,5},{5,4},{6,7},{7,6}} | collective-permute-start | bytes 3538952 | tf_op jit(solution)/shard_map/ppermute | solution.py:342
  950.2 64.3 %collective-permute-start.5 = (bf16[768,768]{1,0:T(8,128)(2,1)}, bf16[768,768]{1,0:T(8,128)(2,1)}, u32[]{:S(2)}, u32[]{:S(2)}) collective-permute-start(bf16[768,768]{1,0:T(8,128)(2,1)} %collective-permute-done.4.refs_0_), channel_id=1, source_target_pairs={{0,1},{1,0},{2,3},{3,2},{4,5},{5,4},{6,7},{7,6}} | collective-permute-start | bytes 3538952 | tf_op jit(solution)/shard_map/ppermute | solution.py:342
  951.5 65.7 %collective-permute-start.2 = (bf16[768,768]{1,0:T(8,128)(2,1)}, bf16[768,768]{1,0:T(8,128)(2,1)}, u32[]{:S(2)}, u32[]{:S(2)}) collective-permute-start(bf16[768,768]{1,0:T(8,128)(2,1)} %collective-permute-done.1.refs_0_), channel_id=1, source_target_pairs={{0,1},{1,0},{2,3},{3,2},{4,5},{5,4},{6,7},{7,6}} | collective-permute-start | bytes 3538952 | tf_op jit(solution)/shard_map/ppermute | solution.py:342
  (66 other events, 2486.0 us)

commit v3 on v2

--- a/solution.py
+++ b/solution.py
@@ -16,9 +16,10 @@
 SLAB = 32
 ADAM_TILE = 192
 ADAM_SLAB = 32
-CHUNKS = (384, 384, 768, 768, 1152, 1152, 768, 768)
+CHUNKS = (384, 384, 1152, 1152, 960, 960, 384, 384, 192, 192)
 ADAM_FLOPS = 60
 PLACE_FLOPS = 16
+PLACE_VMEM = 24 * 2 ** 20
 
 
 def layout_runs(model_width, total_rows):
@@ -61,8 +62,8 @@
     pl.semaphore_wait(barrier, len(partners))
 
 
-def reduce_kernel(shard, grads, total_ref, clip_ref, x_raw, y_raw, mate_raw, x_sum, y_sum,
-                  relay, blocks, sums, finals, squares, norm_mine, norm_all,
+def reduce_kernel(shard, grads, total_ref, clip_ref, x_raw, y_raw, mate_raw,
+                  relay, blocks, x_sum, y_sum, finals, squares, norm_mine, norm_all,
                   x_sent, y_sent, mate_sent, xs_sent, ys_sent, x_got, y_got, mate_got, xs_got, ys_got,
                   load_sem, store_sem, norm_sent, norm_got):
     half = shard // 2
@@ -135,9 +136,9 @@
                 relay[part, tile, at, :] = (parts[0] + parts[1]) + (parts[2] + parts[3])
 
             if part == 0:
-                remote(relay.at[0, tile], y_sum.at[rows(tile)], ys_sent.at[tile], ys_got.at[tile], y_peer).start()
+                remote(relay.at[0, tile], y_sum.at[tile], ys_sent.at[tile], ys_got.at[tile], y_peer).start()
             else:
-                remote(relay.at[1, tile], x_sum.at[rows(tile)], xs_sent.at[tile], xs_got.at[tile], x_peer).start()
+                remote(relay.at[1, tile], x_sum.at[tile], xs_sent.at[tile], xs_got.at[tile], x_peer).start()
 
     squares[...] = jnp.zeros_like(squares)
 
@@ -150,16 +151,14 @@
         copies = loads(1, tile)
         for copy in copies:
             copy.start()
-        arrived(y_sum.at[rows(tile)], ys_got.at[tile])
-        first_sum = pltpu.make_async_copy(y_sum.at[rows(tile)], sums.at[0], load_sem.at[0, 4])
-        first_sum.start()
-        arrived(x_sum.at[rows(tile)], xs_got.at[tile])
-        second_sum = pltpu.make_async_copy(x_sum.at[rows(tile)], sums.at[1], load_sem.at[1, 4])
-        second_sum.start()
         for part in range(2):
             for copy in copies[4 * part:4 * part + 4]:
                 copy.wait()
-            (first_sum, second_sum)[part].wait()
+            if part == 0:
+                arrived(y_sum.at[tile], ys_got.at[tile])
+            else:
+                arrived(x_sum.at[tile], xs_got.at[tile])
+            far_sum = (y_sum, x_sum)[part]
 
             @pl.when(tile > 0)
             def _():
@@ -169,7 +168,7 @@
             def _(slab):
                 at = pl.ds(pl.multiple_of(slab * SLAB, SLAB), SLAB)
                 parts = [blocks[part, k, at, :].astype(jnp.float32) for k in range(4)]
-                mean = ((parts[0] + parts[1]) + (parts[2] + parts[3]) + sums[part, at, :]) * 0.125
+                mean = ((parts[0] + parts[1]) + (parts[2] + parts[3]) + far_sum[tile, at, :]) * 0.125
                 finals[part, at, :] = mean
                 squares[...] += jnp.sum((mean * mean).reshape(SLAB // 8, 8, mean.shape[1]), axis=0)
 
@@ -199,7 +198,7 @@
     @pl.loop(0, tiles)
     def _(tile):
         for ref, sem in ((x_raw.at[:, :, rows(tile)], x_sent), (y_raw.at[:, :, rows(tile)], y_sent), (mate_raw.at[:, rows(tile)], mate_sent),
-                         (x_sum.at[rows(tile)], xs_sent), (y_sum.at[rows(tile)], ys_sent)):
+                         (x_sum.at[tile], xs_sent), (y_sum.at[tile], ys_sent)):
             remote(ref, ref, sem.at[tile], sem.at[tile], mate).wait_send()
 
 
@@ -218,22 +217,21 @@
             jax.ShapeDtypeStruct((2, 2, half, width), bf16),
             jax.ShapeDtypeStruct((2, 2, half, width), bf16),
             jax.ShapeDtypeStruct((4, half, width), bf16),
-            jax.ShapeDtypeStruct((half, width), f32),
-            jax.ShapeDtypeStruct((half, width), f32),
         ],
         in_specs=[any_spec],
-        out_specs=[any_spec, pl.BlockSpec(memory_space=pltpu.VMEM)] + [any_spec] * 5,
+        out_specs=[any_spec, pl.BlockSpec(memory_space=pltpu.VMEM)] + [any_spec] * 3,
         scratch_shapes=[
             pltpu.VMEM((2, tiles, TILE, width), f32),
             pltpu.VMEM((2, 4, TILE, width), bf16),
-            pltpu.VMEM((2, TILE, width), f32),
+            pltpu.VMEM((tiles, TILE, width), f32),
+            pltpu.VMEM((tiles, TILE, width), f32),
             pltpu.VMEM((2, TILE, width), f32),
             pltpu.VMEM((8, width), f32),
             pltpu.VMEM((8, 128), f32),
             pltpu.VMEM((8, 8, 128), f32),
             dma((tiles,)), dma((tiles,)), dma((tiles,)), dma((tiles,)), dma((tiles,)),
             dma((2, 2, tiles)), dma((2, 2, tiles)), dma((4, tiles)), dma((tiles,)), dma((tiles,)),
-            dma((2, 5)), dma((2,)), dma((7,)), dma((8,)),
+            dma((2, 4)), dma((2,)), dma((7,)), dma((8,)),
         ],
         compiler_params=pltpu.CompilerParams(collective_id=0, has_side_effects=True, vmem_limit_bytes=56 * 2 ** 20),
         name='reduce_grads',
@@ -297,44 +295,42 @@
     )(rate, clip, grad, *states, *previous)
 
 
-def place_kernel(count, shard, first_row, partners, *refs):
+def place_kernel(spots, shard, *refs):
+    count = len(spots)
     pieces = refs[:count]
-    target, held, loaded, stored = refs[-4:]
+    target, stored = refs[-2:]
     me, core, _, x_chip, y_chip, d_chip = places()
     chips = {'m': me // 2, 'x': x_chip, 'y': y_chip, 'd': d_chip}
-    rows = held.shape[1]
+
+    def store(k):
+        chip, side, first_row = spots[k]
+        owner = chips[chip] * 2 + (core if side == 0 else 1 - core)
+        at = pl.multiple_of(owner * shard + first_row, 64)
+        return pltpu.make_async_copy(pieces[k], target.at[pl.ds(at, pieces[k].shape[0])], stored.at[k])
+
     for k in range(count):
-        pltpu.make_async_copy(pieces[k], held.at[k], loaded.at[k]).start()
-
-    def store(k):
-        chip, far = partners[k]
-        owner = chips[chip] * 2 + (core if far == 0 else 1 - core)
-        at = pl.multiple_of(owner * shard + first_row, 128)
-        return pltpu.make_async_copy(held.at[k], target.at[pl.ds(at, rows)], stored.at[k])
-
-    for k in range(count):
-        pltpu.make_async_copy(pieces[k], held.at[k], loaded.at[k]).wait()
         store(k).start()
     for k in range(count):
         store(k).wait()
 
 
-def place(shard, first_row, labelled, target, total_rows):
+def place(shard, labelled, target, total_rows):
+    spots = [spot for spot, _ in labelled]
     pieces = [piece for _, piece in labelled]
-    partners = [label for label, _ in labelled]
-    rows, width = pieces[0].shape
+    width = pieces[0].shape[1]
     count = len(pieces)
     any_spec = pl.BlockSpec(memory_space=pl.ANY)
     previous = [] if target is None else [target]
+    size = sum(piece.size for piece in pieces)
     return pl.pallas_call(
-        functools.partial(place_kernel, count, shard, first_row, partners),
+        functools.partial(place_kernel, spots, shard),
         out_shape=jax.ShapeDtypeStruct((total_rows, width), jnp.bfloat16),
-        in_specs=[any_spec] * (count + len(previous)),
+        in_specs=[pl.BlockSpec(memory_space=pltpu.VMEM)] * count + [any_spec] * len(previous),
         out_specs=any_spec,
-        scratch_shapes=[pltpu.VMEM((count, rows, width), jnp.bfloat16), pltpu.SemaphoreType.DMA((count,)), pltpu.SemaphoreType.DMA((count,))],
+        scratch_shapes=[pltpu.SemaphoreType.DMA((count,))],
         input_output_aliases={count: 0} if previous else {},
-        compiler_params=pltpu.CompilerParams(vmem_limit_bytes=56 * 2 ** 20),
-        cost_estimate=pl.CostEstimate(flops=PLACE_FLOPS * count * rows * width, bytes_accessed=4 * count * rows * width, transcendentals=0),
+        compiler_params=pltpu.CompilerParams(vmem_limit_bytes=PLACE_VMEM),
+        cost_estimate=pl.CostEstimate(flops=PLACE_FLOPS * size, bytes_accessed=4 * size, transcendentals=0),
     )(*pieces, *previous)
 
 
@@ -358,19 +354,20 @@
             previous = list(outs[:3])
             chunks.append((first_row, outs[3]))
             first_row += chunk
-        target = None
-        pieces = []
+        near, far = [], []
         for index, (first_row, mine) in enumerate(chunks):
             from_x = swap(mine, 2)
             from_y = swap(mine, 4)
             from_d = swap(from_x, 4) if index % 2 == 0 else swap(from_y, 2)
-            near = [(('m', 0), mine), (('m', 1), swap(mine, 1)), (('x', 0), from_x), (('x', 1), swap(from_x, 1)), (('y', 0), from_y), (('y', 1), swap(from_y, 1))]
-            far = [(('d', 0), from_d), (('d', 1), swap(from_d, 1))]
-            pieces.append((first_row, near, far))
-        for first_row, near, far in pieces:
-            target = place(shard, first_row, near, target, total_rows)
-        for first_row, near, far in pieces:
-            target = place(shard, first_row, far, target, total_rows)
+            near += [(('m', 0, first_row), mine), (('m', 1, first_row), swap(mine, 1))]
+            near += [(('x', 0, first_row), from_x), (('x', 1, first_row), swap(from_x, 1))]
+            near += [(('y', 0, first_row), from_y), (('y', 1, first_row), swap(from_y, 1))]
+            far += [(('d', 0, first_row), from_d), (('d', 1, first_row), swap(from_d, 1))]
+        target = None
+        for pair in range(len(CHUNKS) // 2):
+            target = place(shard, near[12 * pair:12 * pair + 12], target, total_rows)
+        for pair in range(len(CHUNKS) // 2):
+            target = place(shard, far[4 * pair:4 * pair + 4], target, total_rows)
         return (*previous, target)
 
     return jax.shard_map(device_step, mesh=mesh, in_specs=(P('dp', None, None), P('dp', None), P('dp', None), P('dp', None), P()), out_specs=(P('dp', None), P('dp', None), P('dp', None), P(None, None)), check_vma=False)

time: 1020 us -> 1100 us (1.078)
  local copies, waits for them, and re-layouts: 3.51 us -> 55.2 us
  waiting for transfers between devices: 231 us -> 269 us
  Pallas kernels: 759 us -> 735 us
  starting transfers between devices: 24.4 us -> 37.1 us
    unnamed x84 -> x198, local copies, waits for them, and re-layouts: 3.51 us -> 55.2 us
    ppermute x56 -> x70, waiting for transfers between devices: 231 us -> 269 us  [swap(): return lax.ppermute(value, 'dp', [(i, i ^ bit) for i in range(8)])]
    pallas_call x16 -> x10, Pallas kernels: 67.7 us -> 39.5 us  [place(): pl.pallas_call(functools.partial(place_kernel, spots, shard), out_shape=j...]
    ppermute x56 -> x70, starting transfers between devices: 24.4 us -> 37.1 us  [swap(): return lax.ppermute(value, 'dp', [(i, i ^ bit) for i in range(8)])]
    pallas_call x8 -> x10, Pallas kernels: 69.4 us -> 74.5 us  [adam_chunk(): pl.pallas_call(functools.partial(adam_kernel, first_row, shard, total_row...]
  transfers between devices with their start and end apart: 56 -> 70, of which waited for: 24 -> 24; matrix products, arithmetic and copies ran while one was open for 0% -> 0% of each run, Pallas kernels for 13% -> 3%
where the time goes in v3:
time: 1100 us
  Pallas kernels  735 us (67%)
  waiting for transfers between devices  269 us (24%)
  local copies, waits for them, and re-layouts  55.2 us (5%)
  starting transfers between devices  37.1 us (3%)
    pallas_call x1, Pallas kernels, reduce_grads(): pl.pallas_call(functools.partial(reduce_kernel, shard), out_shape=[jax.Sh...  621 us
    ppermute x70, waiting for transfers between devices, swap(): return lax.ppermute(value, 'dp', [(i, i ^ bit) for i in range(8)])  269 us
    pallas_call x10, Pallas kernels, adam_chunk(): pl.pallas_call(functools.partial(adam_kernel, first_row, shard, total_row...  74.5 us
    unnamed x198, local copies, waits for them, and re-layouts  55.2 us
    pallas_call x10, Pallas kernels, place(): pl.pallas_call(functools.partial(place_kernel, spots, shard), out_shape=j...  39.5 us
    ppermute x70, starting transfers between devices, swap(): return lax.ppermute(value, 'dp', [(i, i ^ bit) for i in range(8)])  37.1 us
  transfers between devices with their start and end apart: 70, of which 24 were waited for; matrix products, arithmetic and copies ran while one was open for 0% of the time, Pallas kernels for 3%

profile of v3, /device:TPU:0, one launch (start us, length us, event | category | flops | bytes accessed | tf_op | source)
XLA Modules:
  0.0 1097.9 jit_solution(6499254263002471640)
XLA Ops:
  0.6 620.7 %reduce_grads.1 = (f32[6144,768]{1,0:T(8,128)}, f32[8,128]{1,0:T(8,128)}, bf16[2,2,3072,768]{3,2,1,0:T(8,128)(2,1)}, bf16[2,2,3072,768]{3,2,1,0:T(8,128)(2,1)}, bf16[4,3072,768]{2,1,0:T(8,128)(2,1)}) custom-call(bf16[1,49152,768]{2,1,0:T(8,128)(2,1)} %grads.1), custom_call_target="tpu_custom_call" | custom-call | tf_op jit(solution)/shard_map/reduce_grads/pallas_call | solution.py:212
  621.9 4.8 shard_map.84
  626.7 4.7 shard_map.85
  631.4 12.4 %shard_map.86 = (f32[6144,768]{1,0:T(8,128)}, f32[6144,768]{1,0:T(8,128)}, f32[6144,768]{1,0:T(8,128)}, bf16[1152,768]{1,0:T(8,128)(2,1)}) custom-call(f32[1]{0:T(128)} %bitcast.3.rate_ref, f32[8,128]{1,0:T(8,128)} %get-tuple-element.46.clip_ref, f32[6144,768]{1,0:T(8,128)} %get-tuple-element.47.grad, ...), custom_call_target="tpu_custom_call", output_to_operand_aliasing={{0}: (6, {}), {1}: (7, {}), {2}: (8, {})} | custom-call | flops 53084160 | bytes 26542080 | tf_op jit(solution)/shard_map/pallas_call | solution.py:286
  643.9 12.4 %shard_map.87 = (f32[6144,768]{1,0:T(8,128)}, f32[6144,768]{1,0:T(8,128)}, f32[6144,768]{1,0:T(8,128)}, bf16[1152,768]{1,0:T(8,128)(2,1)}) custom-call(f32[1]{0:T(128)} %bitcast.4.rate_ref, f32[8,128]{1,0:T(8,128)} %get-tuple-element.46.clip_ref, f32[6144,768]{1,0:T(8,128)} %get-tuple-element.47.grad, ...), custom_call_target="tpu_custom_call", output_to_operand_aliasing={{0}: (6, {}), {1}: (7, {}), {2}: (8, {})} | custom-call | flops 53084160 | bytes 26542080 | tf_op jit(solution)/shard_map/pallas_call | solution.py:286
  656.3 11.6 %shard_map.88 = (f32[6144,768]{1,0:T(8,128)}, f32[6144,768]{1,0:T(8,128)}, f32[6144,768]{1,0:T(8,128)}, bf16[960,768]{1,0:T(8,128)(2,1)}) custom-call(f32[1]{0:T(128)} %bitcast.5.rate_ref, f32[8,128]{1,0:T(8,128)} %get-tuple-element.46.clip_ref, f32[6144,768]{1,0:T(8,128)} %get-tuple-element.47.grad, ...), custom_call_target="tpu_custom_call", output_to_operand_aliasing={{0}: (6, {}), {1}: (7, {}), {2}: (8, {})} | custom-call | flops 44236800 | bytes 22118400 | tf_op jit(solution)/shard_map/pallas_call | solution.py:286
  667.9 11.6 %shard_map.89 = (f32[6144,768]{1,0:T(8,128)}, f32[6144,768]{1,0:T(8,128)}, f32[6144,768]{1,0:T(8,128)}, bf16[960,768]{1,0:T(8,128)(2,1)}) custom-call(f32[1]{0:T(128)} %bitcast.6.rate_ref, f32[8,128]{1,0:T(8,128)} %get-tuple-element.46.clip_ref, f32[6144,768]{1,0:T(8,128)} %get-tuple-element.47.grad, ...), custom_call_target="tpu_custom_call", output_to_operand_aliasing={{0}: (6, {}), {1}: (7, {}), {2}: (8, {})} | custom-call | flops 44236800 | bytes 22118400 | tf_op jit(solution)/shard_map/pallas_call | solution.py:286
  679.5 4.7 shard_map.90
  684.2 4.8 shard_map.91
  689.0 3.6 shard_map.92
  692.7 3.8 shard_map.93
  700.6 6.0 collective-permute-done.35.refs_8_
  709.3 15.4 %collective-permute-done.refs_2_ = bf16[192,768]{1,0:T(8,128)(2,1)S(1)} collective-permute-done((bf16[192,768]{1,0:T(8,128)(2,1)}, bf16[192,768]{1,0:T(8,128)(2,1)S(1)}, u32[]{:S(2)}, u32[]{:S(2)}) %collective-permute-start) | collective-permute-done | bytes 294944 | tf_op jit(solution)/shard_map/ppermute | solution.py:338
  731.5 10.6 collective-permute-done.24.refs_2_
  746.2 8.5 collective-permute-done.43.refs_8_
  758.0 7.7 collective-permute-done.6.refs_2_
  776.5 5.0 collective-permute-done.4.refs_2_
  799.2 34.8 %collective-permute-done.28.refs_2_ = bf16[384,768]{1,0:T(8,128)(2,1)S(1)} collective-permute-done((bf16[384,768]{1,0:T(8,128)(2,1)S(1)}, bf16[384,768]{1,0:T(8,128)(2,1)S(1)}, u32[]{:S(2)}, u32[]{:S(2)}) %collective-permute-start.28) | collective-permute-done | bytes 589856 | tf_op jit(solution)/shard_map/ppermute | solution.py:338
  836.0 10.3 collective-permute-done.10.refs_2_
  852.1 29.4 %collective-permute-done.12.refs_2_ = bf16[960,768]{1,0:T(8,128)(2,1)S(1)} collective-permute-done((bf16[960,768]{1,0:T(8,128)(2,1)S(1)}, bf16[960,768]{1,0:T(8,128)(2,1)S(1)}, u32[]{:S(2)}, u32[]{:S(2)}) %collective-permute-start.12) | collective-permute-done | bytes 1474592 | tf_op jit(solution)/shard_map/ppermute | solution.py:338
  885.7 33.7 %collective-permute-done.59.refs_8_ = bf16[1152,768]{1,0:T(8,128)(2,1)S(1)} collective-permute-done((bf16[1152,768]{1,0:T(8,128)(2,1)S(1)}, bf16[1152,768]{1,0:T(8,128)(2,1)S(1)}, u32[]{:S(2)}, u32[]{:S(2)}) %collective-permute-start.59) | collective-permute-done | bytes 1769504 | tf_op jit(solution)/shard_map/ppermute | solution.py:338
  922.9 33.0 %collective-permute-done.18.refs_2_ = bf16[1152,768]{1,0:T(8,128)(2,1)S(1)} collective-permute-done((bf16[1152,768]{1,0:T(8,128)(2,1)S(1)}, bf16[1152,768]{1,0:T(8,128)(2,1)S(1)}, u32[]{:S(2)}, u32[]{:S(2)}) %collective-permute-start.18) | collective-permute-done | bytes 1769504 | tf_op jit(solution)/shard_map/ppermute | solution.py:338
  967.7 27.0 %collective-permute-done.16.refs_2_ = bf16[960,768]{1,0:T(8,128)(2,1)S(1)} collective-permute-done((bf16[960,768]{1,0:T(8,128)(2,1)S(1)}, bf16[960,768]{1,0:T(8,128)(2,1)S(1)}, u32[]{:S(2)}, u32[]{:S(2)}) %collective-permute-start.16) | collective-permute-done | bytes 1474592 | tf_op jit(solution)/shard_map/ppermute | solution.py:338
  997.9 34.1 %collective-permute-done.22.refs_2_ = bf16[1152,768]{1,0:T(8,128)(2,1)S(1)} collective-permute-done((bf16[1152,768]{1,0:T(8,128)(2,1)S(1)}, bf16[1152,768]{1,0:T(8,128)(2,1)S(1)}, u32[]{:S(2)}, u32[]{:S(2)}) %collective-permute-start.22) | collective-permute-done | bytes 1769504 | tf_op jit(solution)/shard_map/ppermute | solution.py:338
  1053.4 3.0 shard_map.94.refs_12_
  1056.4 8.7 shard_map.95.refs_12_
  1065.3 7.8 shard_map.96.refs_12_
  1073.3 3.5 shard_map.97.refs_12_
  1084.2 3.4 shard_map.100.refs_4_
  1088.1 4.4 shard_map.101.refs_4_
  1092.6 3.0 shard_map.102.refs_4_
  1095.6 2.3 shard_map.103
  (327 shorter events, 109.2 us)
Async XLA Ops:
  698.5 29.8 %collective-permute-start.27 = (bf16[384,768]{1,0:T(8,128)(2,1)}, bf16[384,768]{1,0:T(8,128)(2,1)S(1)}, u32[]{:S(2)}, u32[]{:S(2)}) collective-permute-start(bf16[384,768]{1,0:T(8,128)(2,1)} %get-tuple-element.87.refs_6_), channel_id=1, source_target_pairs={{0,4},{1,5},{2,6},{3,7},{4,0},{5,1},{6,2},{7,3}} | collective-permute-start | bytes 1769480 | tf_op jit(solution)/shard_map/ppermute | solution.py:338
  700.0 28.3 %collective-permute-start.67 = (bf16[384,768]{1,0:T(8,128)(2,1)}, bf16[384,768]{1,0:T(8,128)(2,1)S(1)}, u32[]{:S(2)}, u32[]{:S(2)}) collective-permute-start(bf16[384,768]{1,0:T(8,128)(2,1)} %get-tuple-element.87.refs_6_), channel_id=1, source_target_pairs={{0,2},{1,3},{2,0},{3,1},{4,6},{5,7},{6,4},{7,5}} | collective-permute-start | bytes 1769480 | tf_op jit(solution)/shard_map/ppermute | solution.py:338
  786.2 63.4 %collective-permute-start.51 = (bf16[960,768]{1,0:T(8,128)(2,1)S(1)}, bf16[960,768]{1,0:T(8,128)(2,1)S(1)}, u32[]{:S(2)}, u32[]{:S(2)}) collective-permute-start(bf16[960,768]{1,0:T(8,128)(2,1)S(1)} %copy-done.11), channel_id=1, source_target_pairs={{0,2},{1,3},{2,0},{3,1},{4,6},{5,7},{6,4},{7,5}} | collective-permute-start | bytes 4423688 | tf_op jit(solution)/shard_map/ppermute | solution.py:338
  788.5 61.2 %collective-permute-start.15 = (bf16[960,768]{1,0:T(8,128)(2,1)S(1)}, bf16[960,768]{1,0:T(8,128)(2,1)S(1)}, u32[]{:S(2)}, u32[]{:S(2)}) collective-permute-start(bf16[960,768]{1,0:T(8,128)(2,1)S(1)} %copy-done.11), channel_id=1, source_target_pairs={{0,4},{1,5},{2,6},{3,7},{4,0},{5,1},{6,2},{7,3}} | collective-permute-start | bytes 4423688 | tf_op jit(solution)/shard_map/ppermute | solution.py:338
  791.5 42.5 %collective-permute-start.28 = (bf16[384,768]{1,0:T(8,128)(2,1)S(1)}, bf16[384,768]{1,0:T(8,128)(2,1)S(1)}, u32[]{:S(2)}, u32[]{:S(2)}) collective-permute-start(bf16[384,768]{1,0:T(8,128)(2,1)S(1)} %collective-permute-done.27.refs_10_), channel_id=1, source_target_pairs={{0,2},{1,3},{2,0},{3,1},{4,6},{5,7},{6,4},{7,5}} | collective-permute-start | bytes 1769480 | tf_op jit(solution)/shard_map/ppermute | solution.py:338
  794.3 41.6 %collective-permute-start.25 = (bf16[384,768]{1,0:T(8,128)(2,1)S(1)}, bf16[384,768]{1,0:T(8,128)(2,1)S(1)}, u32[]{:S(2)}, u32[]{:S(2)}) collective-permute-start(bf16[384,768]{1,0:T(8,128)(2,1)S(1)} %collective-permute-done.24.refs_2_), channel_id=1, source_target_pairs={{0,4},{1,5},{2,6},{3,7},{4,0},{5,1},{6,2},{7,3}} | collective-permute-start | bytes 1769480 | tf_op jit(solution)/shard_map/ppermute | solution.py:338
  796.9 49.4 %collective-permute-start.10 = (bf16[384,768]{1,0:T(8,128)(2,1)S(1)}, bf16[384,768]{1,0:T(8,128)(2,1)}, u32[]{:S(2)}, u32[]{:S(2)}) collective-permute-start(bf16[384,768]{1,0:T(8,128)(2,1)S(1)} %collective-permute-done.9.refs_10_), channel_id=1, source_target_pairs={{0,2},{1,3},{2,0},{3,1},{4,6},{5,7},{6,4},{7,5}} | collective-permute-start | bytes 1769480 | tf_op jit(solution)/shard_map/ppermute | solution.py:338
  846.3 35.2 %collective-permute-start.12 = (bf16[960,768]{1,0:T(8,128)(2,1)S(1)}, bf16[960,768]{1,0:T(8,128)(2,1)S(1)}, u32[]{:S(2)}, u32[]{:S(2)}) collective-permute-start(bf16[960,768]{1,0:T(8,128)(2,1)S(1)} %copy-done.10), channel_id=1, source_target_pairs={{0,2},{1,3},{2,0},{3,1},{4,6},{5,7},{6,4},{7,5}} | collective-permute-start | bytes 4423688 | tf_op jit(solution)/shard_map/ppermute | solution.py:338
  848.5 35.2 %collective-permute-start.48 = (bf16[960,768]{1,0:T(8,128)(2,1)S(1)}, bf16[960,768]{1,0:T(8,128)(2,1)S(1)}, u32[]{:S(2)}, u32[]{:S(2)}) collective-permute-start(bf16[960,768]{1,0:T(8,128)(2,1)S(1)} %copy-done.10), channel_id=1, source_target_pairs={{0,4},{1,5},{2,6},{3,7},{4,0},{5,1},{6,2},{7,3}} | collective-permute-start | bytes 4423688 | tf_op jit(solution)/shard_map/ppermute | solution.py:338
  849.6 35.5 %collective-permute-start.46 = (bf16[960,768]{1,0:T(8,128)(2,1)S(1)}, bf16[960,768]{1,0:T(8,128)(2,1)S(1)}, u32[]{:S(2)}, u32[]{:S(2)}) collective-permute-start(bf16[960,768]{1,0:T(8,128)(2,1)S(1)} %copy-done.10), channel_id=1, source_target_pairs={{0,1},{1,0},{2,3},{3,2},{4,5},{5,4},{6,7},{7,6}} | collective-permute-start | bytes 4423688 | tf_op jit(solution)/shard_map/ppermute | solution.py:338
  849.7 69.7 %collective-permute-start.59 = (bf16[1152,768]{1,0:T(8,128)(2,1)S(1)}, bf16[1152,768]{1,0:T(8,128)(2,1)S(1)}, u32[]{:S(2)}, u32[]{:S(2)}) collective-permute-start(bf16[1152,768]{1,0:T(8,128)(2,1)S(1)} %copy-done.9), channel_id=1, source_target_pairs={{0,2},{1,3},{2,0},{3,1},{4,6},{5,7},{6,4},{7,5}} | collective-permute-start | bytes 5308424 | tf_op jit(solution)/shard_map/ppermute | solution.py:338
  850.6 71.0 %collective-permute-start.21 = (bf16[1152,768]{1,0:T(8,128)(2,1)S(1)}, bf16[1152,768]{1,0:T(8,128)(2,1)S(1)}, u32[]{:S(2)}, u32[]{:S(2)}) collective-permute-start(bf16[1152,768]{1,0:T(8,128)(2,1)S(1)} %copy-done.9), channel_id=1, source_target_pairs={{0,4},{1,5},{2,6},{3,7},{4,0},{5,1},{6,2},{7,3}} | collective-permute-start | bytes 5308424 | tf_op jit(solution)/shard_map/ppermute | solution.py:338
  881.4 40.2 %collective-permute-start.58 = (bf16[1152,768]{1,0:T(8,128)(2,1)S(1)}, bf16[1152,768]{1,0:T(8,128)(2,1)S(1)}, u32[]{:S(2)}, u32[]{:S(2)}) collective-permute-start(bf16[1152,768]{1,0:T(8,128)(2,1)S(1)} %copy-done.9), channel_id=1, source_target_pairs={{0,1},{1,0},{2,3},{3,2},{4,5},{5,4},{6,7},{7,6}} | collective-permute-start | bytes 5308424 | tf_op jit(solution)/shard_map/ppermute | solution.py:338
  883.7 72.3 %collective-permute-start.18 = (bf16[1152,768]{1,0:T(8,128)(2,1)S(1)}, bf16[1152,768]{1,0:T(8,128)(2,1)S(1)}, u32[]{:S(2)}, u32[]{:S(2)}) collective-permute-start(bf16[1152,768]{1,0:T(8,128)(2,1)S(1)} %copy-done.8), channel_id=1, source_target_pairs={{0,2},{1,3},{2,0},{3,1},{4,6},{5,7},{6,4},{7,5}} | collective-permute-start | bytes 5308424 | tf_op jit(solution)/shard_map/ppermute | solution.py:338
  885.2 72.0 %collective-permute-start.56 = (bf16[1152,768]{1,0:T(8,128)(2,1)S(1)}, bf16[1152,768]{1,0:T(8,128)(2,1)S(1)}, u32[]{:S(2)}, u32[]{:S(2)}) collective-permute-start(bf16[1152,768]{1,0:T(8,128)(2,1)S(1)} %copy-done.8), channel_id=1, source_target_pairs={{0,4},{1,5},{2,6},{3,7},{4,0},{5,1},{6,2},{7,3}} | collective-permute-start | bytes 5308424 | tf_op jit(solution)/shard_map/ppermute | solution.py:338
  919.4 38.0 %collective-permute-start.54 = (bf16[1152,768]{1,0:T(8,128)(2,1)S(1)}, bf16[1152,768]{1,0:T(8,128)(2,1)S(1)}, u32[]{:S(2)}, u32[]{:S(2)}) collective-permute-start(bf16[1152,768]{1,0:T(8,128)(2,1)S(1)} %copy-done.8), channel_id=1, source_target_pairs={{0,1},{1,0},{2,3},{3,2},{4,5},{5,4},{6,7},{7,6}} | collective-permute-start | bytes 5308424 | tf_op jit(solution)/shard_map/ppermute | solution.py:338
  921.6 39.4 %collective-permute-start.52 = (bf16[960,768]{1,0:T(8,128)(2,1)S(1)}, bf16[960,768]{1,0:T(8,128)(2,1)S(1)}, u32[]{:S(2)}, u32[]{:S(2)}) collective-permute-start(bf16[960,768]{1,0:T(8,128)(2,1)S(1)} %collective-permute-done.51.refs_8_), channel_id=1, source_target_pairs={{0,1},{1,0},{2,3},{3,2},{4,5},{5,4},{6,7},{7,6}} | collective-permute-start | bytes 4423688 | tf_op jit(solution)/shard_map/ppermute | solution.py:338
  921.6 36.1 %collective-permute-start.29 = (bf16[384,768]{1,0:T(8,128)(2,1)S(1)}, bf16[384,768]{1,0:T(8,128)(2,1)S(1)}, u32[]{:S(2)}, u32[]{:S(2)}) collective-permute-start(bf16[384,768]{1,0:T(8,128)(2,1)S(1)} %collective-permute-done.28.refs_2_), channel_id=1, source_target_pairs={{0,1},{1,0},{2,3},{3,2},{4,5},{5,4},{6,7},{7,6}} | collective-permute-start | bytes 1769480 | tf_op jit(solution)/shard_map/ppermute | solution.py:338
  959.5 35.2 %collective-permute-start.16 = (bf16[960,768]{1,0:T(8,128)(2,1)S(1)}, bf16[960,768]{1,0:T(8,128)(2,1)S(1)}, u32[]{:S(2)}, u32[]{:S(2)}) collective-permute-start(bf16[960,768]{1,0:T(8,128)(2,1)S(1)} %collective-permute-done.15.refs_10_), channel_id=1, source_target_pairs={{0,2},{1,3},{2,0},{3,1},{4,6},{5,7},{6,4},{7,5}} | collective-permute-start | bytes 4423688 | tf_op jit(solution)/shard_map/ppermute | solution.py:338
  962.1 34.1 %collective-permute-start.13 = (bf16[960,768]{1,0:T(8,128)(2,1)S(1)}, bf16[960,768]{1,0:T(8,128)(2,1)}, u32[]{:S(2)}, u32[]{:S(2)}) collective-permute-start(bf16[960,768]{1,0:T(8,128)(2,1)S(1)} %collective-permute-done.12.refs_2_), channel_id=1, source_target_pairs={{0,4},{1,5},{2,6},{3,7},{4,0},{5,1},{6,2},{7,3}} | collective-permute-start | bytes 4423688 | tf_op jit(solution)/shard_map/ppermute | solution.py:338
  963.8 32.4 %collective-permute-start.60 = (bf16[1152,768]{1,0:T(8,128)(2,1)S(1)}, bf16[1152,768]{1,0:T(8,128)(2,1)S(1)}, u32[]{:S(2)}, u32[]{:S(2)}) collective-permute-start(bf16[1152,768]{1,0:T(8,128)(2,1)S(1)} %collective-permute-done.59.refs_8_), channel_id=1, source_target_pairs={{0,1},{1,0},{2,3},{3,2},{4,5},{5,4},{6,7},{7,6}} | collective-permute-start | bytes 5308424 | tf_op jit(solution)/shard_map/ppermute | solution.py:338
  964.9 31.8 %collective-permute-start.61 = (bf16[1152,768]{1,0:T(8,128)(2,1)S(1)}, bf16[1152,768]{1,0:T(8,128)(2,1)S(1)}, u32[]{:S(2)}, u32[]{:S(2)}) collective-permute-start(bf16[1152,768]{1,0:T(8,128)(2,1)S(1)} %collective-permute-done.21.refs_10_), channel_id=1, source_target_pairs={{0,1},{1,0},{2,3},{3,2},{4,5},{5,4},{6,7},{7,6}} | collective-permute-start | bytes 5308424 | tf_op jit(solution)/shard_map/ppermute | solution.py:338
  966.6 65.4 %collective-permute-start.22 = (bf16[1152,768]{1,0:T(8,128)(2,1)S(1)}, bf16[1152,768]{1,0:T(8,128)(2,1)S(1)}, u32[]{:S(2)}, u32[]{:S(2)}) collective-permute-start(bf16[1152,768]{1,0:T(8,128)(2,1)S(1)} %collective-permute-done.21.refs_10_), channel_id=1, source_target_pairs={{0,2},{1,3},{2,0},{3,1},{4,6},{5,7},{6,4},{7,5}} | collective-permute-start | bytes 5308424 | tf_op jit(solution)/shard_map/ppermute | solution.py:338
  994.7 39.5 %collective-permute-start.19 = (bf16[1152,768]{1,0:T(8,128)(2,1)S(1)}, bf16[1152,768]{1,0:T(8,128)(2,1)S(1)}, u32[]{:S(2)}, u32[]{:S(2)}) collective-permute-start(bf16[1152,768]{1,0:T(8,128)(2,1)S(1)} %collective-permute-done.18.refs_2_), channel_id=1, source_target_pairs={{0,4},{1,5},{2,6},{3,7},{4,0},{5,1},{6,2},{7,3}} | collective-permute-start | bytes 5308424 | tf_op jit(solution)/shard_map/ppermute | solution.py:338
  996.2 39.2 %collective-permute-start.55 = (bf16[1152,768]{1,0:T(8,128)(2,1)S(1)}, bf16[1152,768]{1,0:T(8,128)(2,1)S(1)}, u32[]{:S(2)}, u32[]{:S(2)}) collective-permute-start(bf16[1152,768]{1,0:T(8,128)(2,1)S(1)} %collective-permute-done.18.refs_2_), channel_id=1, source_target_pairs={{0,1},{1,0},{2,3},{3,2},{4,5},{5,4},{6,7},{7,6}} | collective-permute-start | bytes 5308424 | tf_op jit(solution)/shard_map/ppermute | solution.py:338
  996.2 39.7 %collective-permute-start.57 = (bf16[1152,768]{1,0:T(8,128)(2,1)S(1)}, bf16[1152,768]{1,0:T(8,128)(2,1)S(1)}, u32[]{:S(2)}, u32[]{:S(2)}) collective-permute-start(bf16[1152,768]{1,0:T(8,128)(2,1)S(1)} %collective-permute-done.56.refs_4_), channel_id=1, source_target_pairs={{0,1},{1,0},{2,3},{3,2},{4,5},{5,4},{6,7},{7,6}} | collective-permute-start | bytes 5308424 | tf_op jit(solution)/shard_map/ppermute | solution.py:338
  996.7 39.2 %collective-permute-start.17 = (bf16[960,768]{1,0:T(8,128)(2,1)S(1)}, bf16[960,768]{1,0:T(8,128)(2,1)S(1)}, u32[]{:S(2)}, u32[]{:S(2)}) collective-permute-start(bf16[960,768]{1,0:T(8,128)(2,1)S(1)} %collective-permute-done.16.refs_2_), channel_id=1, source_target_pairs={{0,1},{1,0},{2,3},{3,2},{4,5},{5,4},{6,7},{7,6}} | collective-permute-start | bytes 4423688 | tf_op jit(solution)/shard_map/ppermute | solution.py:338
  1035.4 52.2 %collective-permute-start.14 = (bf16[960,768]{1,0:T(8,128)(2,1)}, bf16[960,768]{1,0:T(8,128)(2,1)}, u32[]{:S(2)}, u32[]{:S(2)}) collective-permute-start(bf16[960,768]{1,0:T(8,128)(2,1)} %collective-permute-done.13.refs_0_), channel_id=1, source_target_pairs={{0,1},{1,0},{2,3},{3,2},{4,5},{5,4},{6,7},{7,6}} | collective-permute-start | bytes 4423688 | tf_op jit(solution)/shard_map/ppermute | solution.py:338
  1035.9 56.7 %collective-permute-start.11 = (bf16[384,768]{1,0:T(8,128)(2,1)}, bf16[384,768]{1,0:T(8,128)(2,1)}, u32[]{:S(2)}, u32[]{:S(2)}) collective-permute-start(bf16[384,768]{1,0:T(8,128)(2,1)} %collective-permute-done.10.refs_2_), channel_id=1, source_target_pairs={{0,1},{1,0},{2,3},{3,2},{4,5},{5,4},{6,7},{7,6}} | collective-permute-start | bytes 1769480 | tf_op jit(solution)/shard_map/ppermute | solution.py:338
  1037.0 55.5 %collective-permute-start.8 = (bf16[384,768]{1,0:T(8,128)(2,1)}, bf16[384,768]{1,0:T(8,128)(2,1)}, u32[]{:S(2)}, u32[]{:S(2)}) collective-permute-start(bf16[384,768]{1,0:T(8,128)(2,1)} %collective-permute-done.7.refs_0_), channel_id=1, source_target_pairs={{0,1},{1,0},{2,3},{3,2},{4,5},{5,4},{6,7},{7,6}} | collective-permute-start | bytes 1769480 | tf_op jit(solution)/shard_map/ppermute | solution.py:338
  1038.8 56.9 %collective-permute-start.5 = (bf16[192,768]{1,0:T(8,128)(2,1)}, bf16[192,768]{1,0:T(8,128)(2,1)}, u32[]{:S(2)}, u32[]{:S(2)}) collective-permute-start(bf16[192,768]{1,0:T(8,128)(2,1)} %collective-permute-done.4.refs_2_), channel_id=1, source_target_pairs={{0,1},{1,0},{2,3},{3,2},{4,5},{5,4},{6,7},{7,6}} | collective-permute-start | bytes 884744 | tf_op jit(solution)/shard_map/ppermute | solution.py:338
  1040.1 55.5 %collective-permute-start.2 = (bf16[192,768]{1,0:T(8,128)(2,1)}, bf16[192,768]{1,0:T(8,128)(2,1)}, u32[]{:S(2)}, u32[]{:S(2)}) collective-permute-start(bf16[192,768]{1,0:T(8,128)(2,1)} %collective-permute-done.1.refs_0_), channel_id=1, source_target_pairs={{0,1},{1,0},{2,3},{3,2},{4,5},{5,4},{6,7},{7,6}} | collective-permute-start | bytes 884744 | tf_op jit(solution)/shard_map/ppermute | solution.py:338
  (137 other events, 1415.6 us)

commit v4 on v3

--- a/solution.py
+++ b/solution.py
@@ -12,7 +12,8 @@
 DECAY_RANK = 64
 ADAM_STEP = 10
 MESH = pl.DeviceIdType.MESH
-TILE = 256
+TILE = 384
+PIECE = 128
 SLAB = 32
 ADAM_TILE = 192
 ADAM_SLAB = 32
@@ -62,8 +63,52 @@
     pl.semaphore_wait(barrier, len(partners))
 
 
-def reduce_kernel(shard, grads, total_ref, clip_ref, x_raw, y_raw, mate_raw,
-                  relay, blocks, x_sum, y_sum, finals, squares, norm_mine, norm_all,
+def update_slab(row, total_rows, rate, clip_scale, grad, master, first, second, put):
+    width = grad.shape[1]
+    run_starts, lr_values, decay_values = layout_runs(width, total_rows)
+    lr_factor = jnp.full(row.shape, lr_values[0], jnp.float32)
+    decay = jnp.full(row.shape, decay_values[0], jnp.float32)
+    for k in range(1, len(run_starts)):
+        later = row >= run_starts[k]
+        if lr_values[k] != lr_values[k - 1]:
+            lr_factor = jnp.where(later, lr_values[k], lr_factor)
+        if decay_values[k] != decay_values[k - 1]:
+            decay = jnp.where(later, decay_values[k], decay)
+    step_size = rate * lr_factor
+    for lane in range(width // 128):
+        cols = pl.ds(lane * 128, 128)
+        clipped = grad[:, cols] * clip_scale
+        old = master[:, cols]
+        next_first = 0.9 * first[:, cols] + 0.1 * clipped
+        next_second = 0.99 * second[:, cols] + 0.01 * (clipped * clipped)
+        first_hat = next_first / (1.0 - 0.9 ** ADAM_STEP)
+        second_hat = next_second / (1.0 - 0.99 ** ADAM_STEP)
+        value = old - step_size * (first_hat / (jnp.sqrt(second_hat) + 1e-8) + decay * old)
+        put(cols, value, next_first, next_second)
+
+
+def adam_kernel(first_row, shard, total_rows, rate_ref, clip_ref, grad, master, first, second, *refs):
+    new_master, new_first, new_second, rounded = refs[-4:]
+    start = lax.axis_index('dp') * shard + first_row + pl.program_id(0) * ADAM_TILE
+    rate = rate_ref[0]
+    clip_scale = clip_ref[0:1, 0:1]
+
+    @pl.loop(0, ADAM_TILE // ADAM_SLAB)
+    def _(slab):
+        at = pl.ds(pl.multiple_of(slab * ADAM_SLAB, ADAM_SLAB), ADAM_SLAB)
+        row = start + slab * ADAM_SLAB + lax.broadcasted_iota(jnp.int32, (ADAM_SLAB, 128), 0)
+
+        def put(cols, value, next_first, next_second):
+            new_first[at, cols] = next_first
+            new_second[at, cols] = next_second
+            new_master[at, cols] = value
+            rounded[at, cols] = value.astype(jnp.bfloat16)
+
+        update_slab(row, total_rows, rate, clip_scale, grad.at[at], master.at[at], first.at[at], second.at[at], put)
+
+
+def reduce_kernel(shard, rate_in, grads, master, first, second, total_ref, clip_out, rounded_ref, x_raw, y_raw, mate_raw,
+                  relay, blocks, x_sum, y_sum, finals, head_grad, head_state, head_rounded, head_sem, rate_ref, clip_ref, squares, norm_mine, norm_all,
                   x_sent, y_sent, mate_sent, xs_sent, ys_sent, x_got, y_got, mate_got, xs_got, ys_got,
                   load_sem, store_sem, norm_sent, norm_got):
     half = shard // 2
@@ -73,6 +118,8 @@
     x_peer, y_peer = x_chip * 2 + core, y_chip * 2 + core
     everyone = [mate, x_chip * 2, x_chip * 2 + 1, y_chip * 2, y_chip * 2 + 1, d_chip * 2, d_chip * 2 + 1]
     greet(everyone)
+    head = [pltpu.make_async_copy(state.at[pl.ds(0, TILE)], head_state.at[k], head_sem.at[k]) for k, state in enumerate((master, first, second))]
+    head.append(pltpu.make_async_copy(rate_in, rate_ref, head_sem.at[3]))
 
     def rows(tile):
         return pl.ds(pl.multiple_of(tile * TILE, TILE), TILE)
@@ -129,17 +176,22 @@
             for copy in copies[4 * part:4 * part + 4]:
                 copy.wait()
 
-            @pl.loop(0, TILE // SLAB)
-            def _(slab):
-                at = pl.ds(pl.multiple_of(slab * SLAB, SLAB), SLAB)
-                parts = [blocks[part, k, at, :].astype(jnp.float32) for k in range(4)]
-                relay[part, tile, at, :] = (parts[0] + parts[1]) + (parts[2] + parts[3])
-
-            if part == 0:
-                remote(relay.at[0, tile], y_sum.at[tile], ys_sent.at[tile], ys_got.at[tile], y_peer).start()
-            else:
-                remote(relay.at[1, tile], x_sum.at[tile], xs_sent.at[tile], xs_got.at[tile], x_peer).start()
-
+            for piece in range(TILE // PIECE):
+                here = pl.ds(piece * PIECE, PIECE)
+
+                @pl.loop(piece * PIECE // SLAB, (piece + 1) * PIECE // SLAB)
+                def _(slab):
+                    at = pl.ds(pl.multiple_of(slab * SLAB, SLAB), SLAB)
+                    parts = [blocks[part, k, at, :].astype(jnp.float32) for k in range(4)]
+                    relay[part, tile, at, :] = (parts[0] + parts[1]) + (parts[2] + parts[3])
+
+                if part == 0:
+                    remote(relay.at[0, tile, here], y_sum.at[tile, here], ys_sent.at[tile], ys_got.at[tile, piece], y_peer).start()
+                else:
+                    remote(relay.at[1, tile, here], x_sum.at[tile, here], xs_sent.at[tile], xs_got.at[tile, piece], x_peer).start()
+
+    for copy in head:
+        copy.start()
     squares[...] = jnp.zeros_like(squares)
 
     def total_tile(part, tile):
@@ -154,23 +206,26 @@
         for part in range(2):
             for copy in copies[4 * part:4 * part + 4]:
                 copy.wait()
-            if part == 0:
-                arrived(y_sum.at[tile], ys_got.at[tile])
-            else:
-                arrived(x_sum.at[tile], xs_got.at[tile])
-            far_sum = (y_sum, x_sum)[part]
+            far_sum, far_got = (y_sum, x_sum)[part], (ys_got, xs_got)[part]
 
             @pl.when(tile > 0)
             def _():
                 pltpu.make_async_copy(finals.at[part], total_tile(part, tile), store_sem.at[part]).wait()
 
-            @pl.loop(0, TILE // SLAB)
-            def _(slab):
-                at = pl.ds(pl.multiple_of(slab * SLAB, SLAB), SLAB)
-                parts = [blocks[part, k, at, :].astype(jnp.float32) for k in range(4)]
-                mean = ((parts[0] + parts[1]) + (parts[2] + parts[3]) + far_sum[tile, at, :]) * 0.125
-                finals[part, at, :] = mean
-                squares[...] += jnp.sum((mean * mean).reshape(SLAB // 8, 8, mean.shape[1]), axis=0)
+            for piece in range(TILE // PIECE):
+                arrived(far_sum.at[tile, pl.ds(piece * PIECE, PIECE)], far_got.at[tile, piece])
+
+                @pl.loop(piece * PIECE // SLAB, (piece + 1) * PIECE // SLAB)
+                def _(slab):
+                    at = pl.ds(pl.multiple_of(slab * SLAB, SLAB), SLAB)
+                    parts = [blocks[part, k, at, :].astype(jnp.float32) for k in range(4)]
+                    mean = ((parts[0] + parts[1]) + (parts[2] + parts[3]) + far_sum[tile, at, :]) * 0.125
+                    finals[part, at, :] = mean
+                    if part == 0:
+                        @pl.when(tile == 0)
+                        def _():
+                            head_grad[at, :] = mean
+                    squares[...] += jnp.sum((mean * mean).reshape(SLAB // 8, 8, mean.shape[1]), axis=0)
 
             pltpu.make_async_copy(finals.at[part], total_tile(part, tile), store_sem.at[part]).start()
 
@@ -180,17 +235,37 @@
         packed = packed + squares[:, lane * 128:lane * 128 + 128]
     norm_mine[...] = packed
     norm_all[me] = packed
+    for k, partner in enumerate(everyone):
+        remote(norm_mine, norm_all.at[me], norm_sent.at[k], norm_got.at[me], partner).start()
     for part in range(2):
         pltpu.make_async_copy(finals.at[part], total_tile(part, 0), store_sem.at[part]).wait()
-    for k, partner in enumerate(everyone):
-        remote(norm_mine, norm_all.at[me], norm_sent.at[k], norm_got.at[me], partner).start()
+    for copy in head:
+        copy.wait()
     for partner in everyone:
         arrived(norm_all.at[partner], norm_got.at[partner])
     squared = norm_all[0]
     for k in range(1, 8):
         squared = squared + norm_all[k]
-    norm = jnp.sqrt(jnp.sum(squared))
-    clip_ref[...] = jnp.broadcast_to(jnp.minimum(1.0, 1.0 / (norm + 1e-6)), clip_ref.shape)
+    norm = jnp.sqrt(jnp.sum(squared, keepdims=True))
+    clip_scale = jnp.minimum(1.0, 1.0 / (norm + 1e-6))
+    clip_ref[...] = jnp.broadcast_to(clip_scale, clip_ref.shape)
+    clip_copy = pltpu.make_async_copy(clip_ref, clip_out, head_sem.at[4])
+
+    def head_slab(slab):
+        at = pl.ds(pl.multiple_of(slab * ADAM_SLAB, ADAM_SLAB), ADAM_SLAB)
+        row = me * shard + slab * ADAM_SLAB + lax.broadcasted_iota(jnp.int32, (ADAM_SLAB, 128), 0)
+
+        def put(cols, value, next_first, next_second):
+            head_rounded[at, cols] = value.astype(jnp.bfloat16)
+
+        update_slab(row, 8 * shard, rate_ref[0], clip_ref[0:1, 0:1], head_grad.at[at], head_state.at[0, at], head_state.at[1, at], head_state.at[2, at], put)
+
+    for piece in range(TILE // PIECE):
+        pl.loop(piece * PIECE // ADAM_SLAB, (piece + 1) * PIECE // ADAM_SLAB)(head_slab)
+        if piece == 0:
+            clip_copy.start()
+        here = pl.ds(piece * PIECE, PIECE)
+        pltpu.make_async_copy(head_rounded.at[here], rounded_ref.at[here], head_sem.at[5 + piece]).start()
 
     for k, partner in enumerate(everyone):
         remote(norm_mine, norm_mine, norm_sent.at[k], norm_sent.at[k], partner).wait_send()
@@ -201,8 +276,14 @@
                          (x_sum.at[tile], xs_sent), (y_sum.at[tile], ys_sent)):
             remote(ref, ref, sem.at[tile], sem.at[tile], mate).wait_send()
 
-
-def reduce_grads(local_grads, shard):
+    clip_copy.wait()
+    for piece in range(TILE // PIECE):
+        here = pl.ds(piece * PIECE, PIECE)
+        pltpu.make_async_copy(head_rounded.at[here], rounded_ref.at[here], head_sem.at[5 + piece]).wait()
+
+
+def reduce_grads(rate, local_grads, master, first, second):
+    shard = master.shape[0]
     width = local_grads.shape[2]
     half = shard // 2
     tiles = half // TILE
@@ -214,65 +295,36 @@
         out_shape=[
             jax.ShapeDtypeStruct((shard, width), f32),
             jax.ShapeDtypeStruct((8, 128), f32),
+            jax.ShapeDtypeStruct((TILE, width), bf16),
             jax.ShapeDtypeStruct((2, 2, half, width), bf16),
             jax.ShapeDtypeStruct((2, 2, half, width), bf16),
             jax.ShapeDtypeStruct((4, half, width), bf16),
         ],
-        in_specs=[any_spec],
-        out_specs=[any_spec, pl.BlockSpec(memory_space=pltpu.VMEM)] + [any_spec] * 3,
+        in_specs=[any_spec] * 5,
+        out_specs=[any_spec] * 6,
         scratch_shapes=[
             pltpu.VMEM((2, tiles, TILE, width), f32),
             pltpu.VMEM((2, 4, TILE, width), bf16),
             pltpu.VMEM((tiles, TILE, width), f32),
             pltpu.VMEM((tiles, TILE, width), f32),
             pltpu.VMEM((2, TILE, width), f32),
+            pltpu.VMEM((TILE, width), f32),
+            pltpu.VMEM((3, TILE, width), f32),
+            pltpu.VMEM((TILE, width), bf16),
+            dma((5 + TILE // PIECE,)),
+            pltpu.SMEM((1,), f32),
+            pltpu.VMEM((8, 128), f32),
             pltpu.VMEM((8, width), f32),
             pltpu.VMEM((8, 128), f32),
             pltpu.VMEM((8, 8, 128), f32),
             dma((tiles,)), dma((tiles,)), dma((tiles,)), dma((tiles,)), dma((tiles,)),
-            dma((2, 2, tiles)), dma((2, 2, tiles)), dma((4, tiles)), dma((tiles,)), dma((tiles,)),
+            dma((2, 2, tiles)), dma((2, 2, tiles)), dma((4, tiles)), dma((tiles, TILE // PIECE)), dma((tiles, TILE // PIECE)),
             dma((2, 4)), dma((2,)), dma((7,)), dma((8,)),
         ],
         compiler_params=pltpu.CompilerParams(collective_id=0, has_side_effects=True, vmem_limit_bytes=56 * 2 ** 20),
         name='reduce_grads',
-    )(local_grads)
-    return outs[0], outs[1]
-
-
-def adam_kernel(first_row, shard, total_rows, rate_ref, clip_ref, grad, master, first, second, *refs):
-    new_master, new_first, new_second, rounded = refs[-4:]
-    width = grad.shape[1]
-    run_starts, lr_values, decay_values = layout_runs(width, total_rows)
-    start = lax.axis_index('dp') * shard + first_row + pl.program_id(0) * ADAM_TILE
-    rate = rate_ref[0]
-    clip_scale = clip_ref[0:1, 0:1]
-
-    @pl.loop(0, ADAM_TILE // ADAM_SLAB)
-    def _(slab):
-        at = pl.ds(pl.multiple_of(slab * ADAM_SLAB, ADAM_SLAB), ADAM_SLAB)
-        row = start + slab * ADAM_SLAB + lax.broadcasted_iota(jnp.int32, (ADAM_SLAB, 128), 0)
-        lr_factor = jnp.full((ADAM_SLAB, 128), lr_values[0], jnp.float32)
-        decay = jnp.full((ADAM_SLAB, 128), decay_values[0], jnp.float32)
-        for k in range(1, len(run_starts)):
-            later = row >= run_starts[k]
-            if lr_values[k] != lr_values[k - 1]:
-                lr_factor = jnp.where(later, lr_values[k], lr_factor)
-            if decay_values[k] != decay_values[k - 1]:
-                decay = jnp.where(later, decay_values[k], decay)
-        step_size = rate * lr_factor
-        for lane in range(width // 128):
-            cols = pl.ds(lane * 128, 128)
-            clipped = grad[at, cols] * clip_scale
-            old = master[at, cols]
-            next_first = 0.9 * first[at, cols] + 0.1 * clipped
-            next_second = 0.99 * second[at, cols] + 0.01 * (clipped * clipped)
-            first_hat = next_first / (1.0 - 0.9 ** ADAM_STEP)
-            second_hat = next_second / (1.0 - 0.99 ** ADAM_STEP)
-            value = old - step_size * (first_hat / (jnp.sqrt(second_hat) + 1e-8) + decay * old)
-            new_first[at, cols] = next_first
-            new_second[at, cols] = next_second
-            new_master[at, cols] = value
-            rounded[at, cols] = value.astype(jnp.bfloat16)
+    )(rate, local_grads, master, first, second)
+    return outs[:3]
 
 
 def adam_chunk(first_row, chunk, rate, clip, grad, states, previous, total_rows):
@@ -344,16 +396,16 @@
     def device_step(local_grads, master, mom_first, mom_second, learn_rate):
         shard = master.shape[0]
         total_rows = shard * dev_count
-        grad_shard, clip = reduce_grads(local_grads, shard)
         rate = learn_rate.reshape(1)
+        grad_shard, clip, head_rounded = reduce_grads(rate, local_grads, master, mom_first, mom_second)
         previous = []
         chunks = []
-        first_row = 0
-        for chunk in CHUNKS:
-            outs = adam_chunk(first_row, chunk, rate, clip, grad_shard, (master, mom_first, mom_second), previous, total_rows)
+        for index in (*range(1, len(CHUNKS)), 0):
+            first_row = sum(CHUNKS[:index])
+            outs = adam_chunk(first_row, CHUNKS[index], rate, clip, grad_shard, (master, mom_first, mom_second), previous, total_rows)
             previous = list(outs[:3])
             chunks.append((first_row, outs[3]))
-            first_row += chunk
+        chunks = [(0, head_rounded)] + chunks[:-1]
         near, far = [], []
         for index, (first_row, mine) in enumerate(chunks):
             from_x = swap(mine, 2)

time: 1100 us -> 1110 us (level)
  local copies, waits for them, and re-layouts: 55.2 us -> 76.8 us
    unnamed x198 -> x258, local copies, waits for them, and re-layouts: 55.2 us -> 76.8 us
  transfers between devices with their start and end apart: 70 -> 70, of which waited for: 24 -> 24; matrix products, arithmetic and copies ran while one was open for 0% -> 0% of each run, Pallas kernels for 3% -> 4%
where the time goes in v4:
time: 1110 us
  Pallas kernels  738 us (66%)
  waiting for transfers between devices  259 us (23%)
  local copies, waits for them, and re-layouts  76.8 us (7%)
  starting transfers between devices  36.2 us (3%)
    pallas_call x1, Pallas kernels, reduce_grads(): pl.pallas_call(functools.partial(reduce_kernel, shard), out_shape=[jax.Sh...  621 us
    ppermute x70, waiting for transfers between devices, swap(): return lax.ppermute(value, 'dp', [(i, i ^ bit) for i in range(8)])  259 us
    unnamed x258, local copies, waits for them, and re-layouts  76.8 us
    pallas_call x10, Pallas kernels, adam_chunk(): pl.pallas_call(functools.partial(adam_kernel, first_row, shard, total_row...  74.6 us
    pallas_call x10, Pallas kernels, place(): pl.pallas_call(functools.partial(place_kernel, spots, shard), out_shape=j...  42.3 us
    ppermute x70, starting transfers between devices, swap(): return lax.ppermute(value, 'dp', [(i, i ^ bit) for i in range(8)])  36.2 us
  transfers between devices with their start and end apart: 70, of which 24 were waited for; matrix products, arithmetic and copies ran while one was open for 0% of the time, Pallas kernels for 4%

profile of v4, /device:TPU:0, one launch (start us, length us, event | category | flops | bytes accessed | tf_op | source)
XLA Modules:
  0.0 1112.0 jit_solution(11513700886126487455)
XLA Ops:
  1.3 620.9 %reduce_grads.1 = (f32[6144,768]{1,0:T(8,128)}, f32[8,128]{1,0:T(8,128)}, bf16[384,768]{1,0:T(8,128)(2,1)}, bf16[2,2,3072,768]{3,2,1,0:T(8,128)(2,1)}, bf16[2,2,...) custom-call(f32[1]{0:T(128)} %bitcast.1.rate_in, bf16[1,49152,768]{2,1,0:T(8,128)(2,1)} %grads.1, ...), custom_call_target="tpu_custom_call" | custom-call | tf_op jit(solution)/shard_map/reduce_grads/pallas_call | solution.py:293
  622.2 4.7 shard_map.84
  626.9 12.4 %shard_map.85 = (f32[6144,768]{1,0:T(8,128)}, f32[6144,768]{1,0:T(8,128)}, f32[6144,768]{1,0:T(8,128)}, bf16[1152,768]{1,0:T(8,128)(2,1)}) custom-call(f32[1]{0:T(128)} %bitcast.3.rate_ref, f32[8,128]{1,0:T(8,128)} %get-tuple-element.46.clip_ref, f32[6144,768]{1,0:T(8,128)} %get-tuple-element.47.grad, ...), custom_call_target="tpu_custom_call", output_to_operand_aliasing={{0}: (6, {}), {1}: (7, {}), {2}: (8, {})} | custom-call | flops 53084160 | bytes 26542080 | tf_op jit(solution)/shard_map/pallas_call | solution.py:338
  639.3 12.4 %shard_map.86 = (f32[6144,768]{1,0:T(8,128)}, f32[6144,768]{1,0:T(8,128)}, f32[6144,768]{1,0:T(8,128)}, bf16[1152,768]{1,0:T(8,128)(2,1)}) custom-call(f32[1]{0:T(128)} %bitcast.4.rate_ref, f32[8,128]{1,0:T(8,128)} %get-tuple-element.46.clip_ref, f32[6144,768]{1,0:T(8,128)} %get-tuple-element.47.grad, ...), custom_call_target="tpu_custom_call", output_to_operand_aliasing={{0}: (6, {}), {1}: (7, {}), {2}: (8, {})} | custom-call | flops 53084160 | bytes 26542080 | tf_op jit(solution)/shard_map/pallas_call | solution.py:338
  651.7 11.6 %shard_map.87 = (f32[6144,768]{1,0:T(8,128)}, f32[6144,768]{1,0:T(8,128)}, f32[6144,768]{1,0:T(8,128)}, bf16[960,768]{1,0:T(8,128)(2,1)}) custom-call(f32[1]{0:T(128)} %bitcast.5.rate_ref, f32[8,128]{1,0:T(8,128)} %get-tuple-element.46.clip_ref, f32[6144,768]{1,0:T(8,128)} %get-tuple-element.47.grad, ...), custom_call_target="tpu_custom_call", output_to_operand_aliasing={{0}: (6, {}), {1}: (7, {}), {2}: (8, {})} | custom-call | flops 44236800 | bytes 22118400 | tf_op jit(solution)/shard_map/pallas_call | solution.py:338
  663.3 11.8 %shard_map.88 = (f32[6144,768]{1,0:T(8,128)}, f32[6144,768]{1,0:T(8,128)}, f32[6144,768]{1,0:T(8,128)}, bf16[960,768]{1,0:T(8,128)(2,1)}) custom-call(f32[1]{0:T(128)} %bitcast.6.rate_ref, f32[8,128]{1,0:T(8,128)} %get-tuple-element.46.clip_ref, f32[6144,768]{1,0:T(8,128)} %get-tuple-element.47.grad, ...), custom_call_target="tpu_custom_call", output_to_operand_aliasing={{0}: (6, {}), {1}: (7, {}), {2}: (8, {})} | custom-call | flops 44236800 | bytes 22118400 | tf_op jit(solution)/shard_map/pallas_call | solution.py:338
  675.1 4.7 shard_map.89
  679.7 4.8 shard_map.90
  684.6 3.7 shard_map.91
  688.3 3.8 shard_map.92
  696.2 6.0 collective-permute-done.35.refs_8_
  704.9 15.4 %collective-permute-done.refs_2_ = bf16[192,768]{1,0:T(8,128)(2,1)S(1)} collective-permute-done((bf16[192,768]{1,0:T(8,128)(2,1)S(1)}, bf16[192,768]{1,0:T(8,128)(2,1)S(1)}, u32[]{:S(2)}, u32[]{:S(2)}) %collective-permute-start) | collective-permute-done | bytes 294944 | tf_op jit(solution)/shard_map/ppermute | solution.py:390
  727.2 10.5 collective-permute-done.24.refs_2_
  741.8 8.5 collective-permute-done.43.refs_8_
  753.6 7.7 collective-permute-done.6.refs_2_
  772.0 5.2 collective-permute-done.4.refs_2_
  795.8 34.7 %collective-permute-done.28.refs_2_ = bf16[384,768]{1,0:T(8,128)(2,1)S(1)} collective-permute-done((bf16[384,768]{1,0:T(8,128)(2,1)S(1)}, bf16[384,768]{1,0:T(8,128)(2,1)S(1)}, u32[]{:S(2)}, u32[]{:S(2)}) %collective-permute-start.28) | collective-permute-done | bytes 589856 | tf_op jit(solution)/shard_map/ppermute | solution.py:390
  832.2 10.5 collective-permute-done.10.refs_2_
  849.7 28.4 %collective-permute-done.12.refs_2_ = bf16[960,768]{1,0:T(8,128)(2,1)S(1)} collective-permute-done((bf16[960,768]{1,0:T(8,128)(2,1)}, bf16[960,768]{1,0:T(8,128)(2,1)S(1)}, u32[]{:S(2)}, u32[]{:S(2)}) %collective-permute-start.12) | collective-permute-done | bytes 1474592 | tf_op jit(solution)/shard_map/ppermute | solution.py:390
  883.5 32.5 %collective-permute-done.59.refs_8_ = bf16[1152,768]{1,0:T(8,128)(2,1)S(1)} collective-permute-done((bf16[1152,768]{1,0:T(8,128)(2,1)S(1)}, bf16[1152,768]{1,0:T(8,128)(2,1)S(1)}, u32[]{:S(2)}, u32[]{:S(2)}) %collective-permute-start.59) | collective-permute-done | bytes 1769504 | tf_op jit(solution)/shard_map/ppermute | solution.py:390
  922.0 30.7 %collective-permute-done.18.refs_2_ = bf16[1152,768]{1,0:T(8,128)(2,1)S(1)} collective-permute-done((bf16[1152,768]{1,0:T(8,128)(2,1)S(1)}, bf16[1152,768]{1,0:T(8,128)(2,1)S(1)}, u32[]{:S(2)}, u32[]{:S(2)}) %collective-permute-start.18) | collective-permute-done | bytes 1769504 | tf_op jit(solution)/shard_map/ppermute | solution.py:390
  968.9 24.8 %collective-permute-done.16.refs_2_ = bf16[960,768]{1,0:T(8,128)(2,1)S(1)} collective-permute-done((bf16[960,768]{1,0:T(8,128)(2,1)S(1)}, bf16[960,768]{1,0:T(8,128)(2,1)S(1)}, u32[]{:S(2)}, u32[]{:S(2)}) %collective-permute-start.16) | collective-permute-done | bytes 1474592 | tf_op jit(solution)/shard_map/ppermute | solution.py:390
  994.6 2.7 collective-permute-done.13.refs_0_
  1003.9 27.1 %collective-permute-done.22.refs_2_ = bf16[1152,768]{1,0:T(8,128)(2,1)S(1)} collective-permute-done((bf16[1152,768]{1,0:T(8,128)(2,1)S(1)}, bf16[1152,768]{1,0:T(8,128)(2,1)S(1)}, u32[]{:S(2)}, u32[]{:S(2)}) %collective-permute-start.22) | collective-permute-done | bytes 1769504 | tf_op jit(solution)/shard_map/ppermute | solution.py:390
  1043.0 4.7 shard_map.93
  1058.4 3.7 shard_map.94.refs_12_
  1066.0 10.4 shard_map.95.refs_12_
  1078.9 8.2 shard_map.96.refs_12_
  1087.4 3.5 shard_map.97.refs_12_
  1098.3 3.4 shard_map.100.refs_4_
  1102.2 4.4 shard_map.101.refs_4_
  1106.7 3.0 shard_map.102.refs_4_
  (387 shorter events, 132.8 us)
Async XLA Ops:
  694.1 29.6 %collective-permute-start.27 = (bf16[384,768]{1,0:T(8,128)(2,1)S(1)}, bf16[384,768]{1,0:T(8,128)(2,1)S(1)}, u32[]{:S(2)}, u32[]{:S(2)}) collective-permute-start(bf16[384,768]{1,0:T(8,128)(2,1)S(1)} %copy-done.77), channel_id=1, source_target_pairs={{0,4},{1,5},{2,6},{3,7},{4,0},{5,1},{6,2},{7,3}} | collective-permute-start | bytes 1769480 | tf_op jit(solution)/shard_map/ppermute | solution.py:390
  695.6 28.1 %collective-permute-start.67 = (bf16[384,768]{1,0:T(8,128)(2,1)S(1)}, bf16[384,768]{1,0:T(8,128)(2,1)S(1)}, u32[]{:S(2)}, u32[]{:S(2)}) collective-permute-start(bf16[384,768]{1,0:T(8,128)(2,1)S(1)} %copy-done.77), channel_id=1, source_target_pairs={{0,2},{1,3},{2,0},{3,1},{4,6},{5,7},{6,4},{7,5}} | collective-permute-start | bytes 1769480 | tf_op jit(solution)/shard_map/ppermute | solution.py:390
  782.7 63.3 %collective-permute-start.51 = (bf16[960,768]{1,0:T(8,128)(2,1)S(1)}, bf16[960,768]{1,0:T(8,128)(2,1)S(1)}, u32[]{:S(2)}, u32[]{:S(2)}) collective-permute-start(bf16[960,768]{1,0:T(8,128)(2,1)S(1)} %copy-done.26), channel_id=1, source_target_pairs={{0,2},{1,3},{2,0},{3,1},{4,6},{5,7},{6,4},{7,5}} | collective-permute-start | bytes 4423688 | tf_op jit(solution)/shard_map/ppermute | solution.py:390
  785.0 60.9 %collective-permute-start.15 = (bf16[960,768]{1,0:T(8,128)(2,1)S(1)}, bf16[960,768]{1,0:T(8,128)(2,1)S(1)}, u32[]{:S(2)}, u32[]{:S(2)}) collective-permute-start(bf16[960,768]{1,0:T(8,128)(2,1)S(1)} %copy-done.26), channel_id=1, source_target_pairs={{0,4},{1,5},{2,6},{3,7},{4,0},{5,1},{6,2},{7,3}} | collective-permute-start | bytes 4423688 | tf_op jit(solution)/shard_map/ppermute | solution.py:390
  788.1 42.4 %collective-permute-start.28 = (bf16[384,768]{1,0:T(8,128)(2,1)S(1)}, bf16[384,768]{1,0:T(8,128)(2,1)S(1)}, u32[]{:S(2)}, u32[]{:S(2)}) collective-permute-start(bf16[384,768]{1,0:T(8,128)(2,1)S(1)} %collective-permute-done.27.refs_10_), channel_id=1, source_target_pairs={{0,2},{1,3},{2,0},{3,1},{4,6},{5,7},{6,4},{7,5}} | collective-permute-start | bytes 1769480 | tf_op jit(solution)/shard_map/ppermute | solution.py:390
  790.7 41.6 %collective-permute-start.25 = (bf16[384,768]{1,0:T(8,128)(2,1)S(1)}, bf16[384,768]{1,0:T(8,128)(2,1)S(1)}, u32[]{:S(2)}, u32[]{:S(2)}) collective-permute-start(bf16[384,768]{1,0:T(8,128)(2,1)S(1)} %collective-permute-done.24.refs_2_), channel_id=1, source_target_pairs={{0,4},{1,5},{2,6},{3,7},{4,0},{5,1},{6,2},{7,3}} | collective-permute-start | bytes 1769480 | tf_op jit(solution)/shard_map/ppermute | solution.py:390
  793.5 49.3 %collective-permute-start.10 = (bf16[384,768]{1,0:T(8,128)(2,1)S(1)}, bf16[384,768]{1,0:T(8,128)(2,1)}, u32[]{:S(2)}, u32[]{:S(2)}) collective-permute-start(bf16[384,768]{1,0:T(8,128)(2,1)S(1)} %collective-permute-done.9.refs_10_), channel_id=1, source_target_pairs={{0,2},{1,3},{2,0},{3,1},{4,6},{5,7},{6,4},{7,5}} | collective-permute-start | bytes 1769480 | tf_op jit(solution)/shard_map/ppermute | solution.py:390
  842.8 35.4 %collective-permute-start.12 = (bf16[960,768]{1,0:T(8,128)(2,1)}, bf16[960,768]{1,0:T(8,128)(2,1)S(1)}, u32[]{:S(2)}, u32[]{:S(2)}) collective-permute-start(bf16[960,768]{1,0:T(8,128)(2,1)} %get-tuple-element.82.refs_0_), channel_id=1, source_target_pairs={{0,2},{1,3},{2,0},{3,1},{4,6},{5,7},{6,4},{7,5}} | collective-permute-start | bytes 4423688 | tf_op jit(solution)/shard_map/ppermute | solution.py:390
  845.0 35.4 %collective-permute-start.48 = (bf16[960,768]{1,0:T(8,128)(2,1)}, bf16[960,768]{1,0:T(8,128)(2,1)S(1)}, u32[]{:S(2)}, u32[]{:S(2)}) collective-permute-start(bf16[960,768]{1,0:T(8,128)(2,1)} %get-tuple-element.82.refs_0_), channel_id=1, source_target_pairs={{0,4},{1,5},{2,6},{3,7},{4,0},{5,1},{6,2},{7,3}} | collective-permute-start | bytes 4423688 | tf_op jit(solution)/shard_map/ppermute | solution.py:390
  846.0 35.9 %collective-permute-start.46 = (bf16[960,768]{1,0:T(8,128)(2,1)}, bf16[960,768]{1,0:T(8,128)(2,1)S(1)}, u32[]{:S(2)}, u32[]{:S(2)}) collective-permute-start(bf16[960,768]{1,0:T(8,128)(2,1)} %get-tuple-element.82.refs_0_), channel_id=1, source_target_pairs={{0,1},{1,0},{2,3},{3,2},{4,5},{5,4},{6,7},{7,6}} | collective-permute-start | bytes 4423688 | tf_op jit(solution)/shard_map/ppermute | solution.py:390
  846.0 70.1 %collective-permute-start.59 = (bf16[1152,768]{1,0:T(8,128)(2,1)S(1)}, bf16[1152,768]{1,0:T(8,128)(2,1)S(1)}, u32[]{:S(2)}, u32[]{:S(2)}) collective-permute-start(bf16[1152,768]{1,0:T(8,128)(2,1)S(1)} %copy-done.9), channel_id=1, source_target_pairs={{0,2},{1,3},{2,0},{3,1},{4,6},{5,7},{6,4},{7,5}} | collective-permute-start | bytes 5308424 | tf_op jit(solution)/shard_map/ppermute | solution.py:390
  848.2 70.1 %collective-permute-start.21 = (bf16[1152,768]{1,0:T(8,128)(2,1)S(1)}, bf16[1152,768]{1,0:T(8,128)(2,1)S(1)}, u32[]{:S(2)}, u32[]{:S(2)}) collective-permute-start(bf16[1152,768]{1,0:T(8,128)(2,1)S(1)} %copy-done.9), channel_id=1, source_target_pairs={{0,4},{1,5},{2,6},{3,7},{4,0},{5,1},{6,2},{7,3}} | collective-permute-start | bytes 5308424 | tf_op jit(solution)/shard_map/ppermute | solution.py:390
  878.1 41.3 %collective-permute-start.58 = (bf16[1152,768]{1,0:T(8,128)(2,1)S(1)}, bf16[1152,768]{1,0:T(8,128)(2,1)S(1)}, u32[]{:S(2)}, u32[]{:S(2)}) collective-permute-start(bf16[1152,768]{1,0:T(8,128)(2,1)S(1)} %copy-done.9), channel_id=1, source_target_pairs={{0,1},{1,0},{2,3},{3,2},{4,5},{5,4},{6,7},{7,6}} | collective-permute-start | bytes 5308424 | tf_op jit(solution)/shard_map/ppermute | solution.py:390
  880.4 72.3 %collective-permute-start.18 = (bf16[1152,768]{1,0:T(8,128)(2,1)S(1)}, bf16[1152,768]{1,0:T(8,128)(2,1)S(1)}, u32[]{:S(2)}, u32[]{:S(2)}) collective-permute-start(bf16[1152,768]{1,0:T(8,128)(2,1)S(1)} %copy-done.8), channel_id=1, source_target_pairs={{0,2},{1,3},{2,0},{3,1},{4,6},{5,7},{6,4},{7,5}} | collective-permute-start | bytes 5308424 | tf_op jit(solution)/shard_map/ppermute | solution.py:390
  883.0 70.9 %collective-permute-start.56 = (bf16[1152,768]{1,0:T(8,128)(2,1)S(1)}, bf16[1152,768]{1,0:T(8,128)(2,1)S(1)}, u32[]{:S(2)}, u32[]{:S(2)}) collective-permute-start(bf16[1152,768]{1,0:T(8,128)(2,1)S(1)} %copy-done.8), channel_id=1, source_target_pairs={{0,4},{1,5},{2,6},{3,7},{4,0},{5,1},{6,2},{7,3}} | collective-permute-start | bytes 5308424 | tf_op jit(solution)/shard_map/ppermute | solution.py:390
  916.1 37.9 %collective-permute-start.54 = (bf16[1152,768]{1,0:T(8,128)(2,1)S(1)}, bf16[1152,768]{1,0:T(8,128)(2,1)S(1)}, u32[]{:S(2)}, u32[]{:S(2)}) collective-permute-start(bf16[1152,768]{1,0:T(8,128)(2,1)S(1)} %copy-done.8), channel_id=1, source_target_pairs={{0,1},{1,0},{2,3},{3,2},{4,5},{5,4},{6,7},{7,6}} | collective-permute-start | bytes 5308424 | tf_op jit(solution)/shard_map/ppermute | solution.py:390
  918.3 42.8 %collective-permute-start.52 = (bf16[960,768]{1,0:T(8,128)(2,1)S(1)}, bf16[960,768]{1,0:T(8,128)(2,1)S(1)}, u32[]{:S(2)}, u32[]{:S(2)}) collective-permute-start(bf16[960,768]{1,0:T(8,128)(2,1)S(1)} %collective-permute-done.51.refs_8_), channel_id=1, source_target_pairs={{0,1},{1,0},{2,3},{3,2},{4,5},{5,4},{6,7},{7,6}} | collective-permute-start | bytes 4423688 | tf_op jit(solution)/shard_map/ppermute | solution.py:390
  920.7 35.0 %collective-permute-start.29 = (bf16[384,768]{1,0:T(8,128)(2,1)S(1)}, bf16[384,768]{1,0:T(8,128)(2,1)S(1)}, u32[]{:S(2)}, u32[]{:S(2)}) collective-permute-start(bf16[384,768]{1,0:T(8,128)(2,1)S(1)} %collective-permute-done.28.refs_2_), channel_id=1, source_target_pairs={{0,1},{1,0},{2,3},{3,2},{4,5},{5,4},{6,7},{7,6}} | collective-permute-start | bytes 1769480 | tf_op jit(solution)/shard_map/ppermute | solution.py:390
  958.5 35.2 %collective-permute-start.16 = (bf16[960,768]{1,0:T(8,128)(2,1)S(1)}, bf16[960,768]{1,0:T(8,128)(2,1)S(1)}, u32[]{:S(2)}, u32[]{:S(2)}) collective-permute-start(bf16[960,768]{1,0:T(8,128)(2,1)S(1)} %collective-permute-done.15.refs_10_), channel_id=1, source_target_pairs={{0,2},{1,3},{2,0},{3,1},{4,6},{5,7},{6,4},{7,5}} | collective-permute-start | bytes 4423688 | tf_op jit(solution)/shard_map/ppermute | solution.py:390
  962.3 35.1 %collective-permute-start.13 = (bf16[960,768]{1,0:T(8,128)(2,1)S(1)}, bf16[960,768]{1,0:T(8,128)(2,1)}, u32[]{:S(2)}, u32[]{:S(2)}) collective-permute-start(bf16[960,768]{1,0:T(8,128)(2,1)S(1)} %collective-permute-done.12.refs_2_), channel_id=1, source_target_pairs={{0,4},{1,5},{2,6},{3,7},{4,0},{5,1},{6,2},{7,3}} | collective-permute-start | bytes 4423688 | tf_op jit(solution)/shard_map/ppermute | solution.py:390
  965.1 33.5 %collective-permute-start.60 = (bf16[1152,768]{1,0:T(8,128)(2,1)S(1)}, bf16[1152,768]{1,0:T(8,128)(2,1)S(1)}, u32[]{:S(2)}, u32[]{:S(2)}) collective-permute-start(bf16[1152,768]{1,0:T(8,128)(2,1)S(1)} %collective-permute-done.59.refs_8_), channel_id=1, source_target_pairs={{0,1},{1,0},{2,3},{3,2},{4,5},{5,4},{6,7},{7,6}} | collective-permute-start | bytes 5308424 | tf_op jit(solution)/shard_map/ppermute | solution.py:390
  966.3 35.2 %collective-permute-start.61 = (bf16[1152,768]{1,0:T(8,128)(2,1)S(1)}, bf16[1152,768]{1,0:T(8,128)(2,1)S(1)}, u32[]{:S(2)}, u32[]{:S(2)}) collective-permute-start(bf16[1152,768]{1,0:T(8,128)(2,1)S(1)} %collective-permute-done.21.refs_10_), channel_id=1, source_target_pairs={{0,1},{1,0},{2,3},{3,2},{4,5},{5,4},{6,7},{7,6}} | collective-permute-start | bytes 5308424 | tf_op jit(solution)/shard_map/ppermute | solution.py:390
  967.9 63.1 %collective-permute-start.22 = (bf16[1152,768]{1,0:T(8,128)(2,1)S(1)}, bf16[1152,768]{1,0:T(8,128)(2,1)S(1)}, u32[]{:S(2)}, u32[]{:S(2)}) collective-permute-start(bf16[1152,768]{1,0:T(8,128)(2,1)S(1)} %collective-permute-done.21.refs_10_), channel_id=1, source_target_pairs={{0,2},{1,3},{2,0},{3,1},{4,6},{5,7},{6,4},{7,5}} | collective-permute-start | bytes 5308424 | tf_op jit(solution)/shard_map/ppermute | solution.py:390
  993.7 40.5 %collective-permute-start.19 = (bf16[1152,768]{1,0:T(8,128)(2,1)S(1)}, bf16[1152,768]{1,0:T(8,128)(2,1)S(1)}, u32[]{:S(2)}, u32[]{:S(2)}) collective-permute-start(bf16[1152,768]{1,0:T(8,128)(2,1)S(1)} %collective-permute-done.18.refs_2_), channel_id=1, source_target_pairs={{0,4},{1,5},{2,6},{3,7},{4,0},{5,1},{6,2},{7,3}} | collective-permute-start | bytes 5308424 | tf_op jit(solution)/shard_map/ppermute | solution.py:390
  997.4 38.1 %collective-permute-start.55 = (bf16[1152,768]{1,0:T(8,128)(2,1)S(1)}, bf16[1152,768]{1,0:T(8,128)(2,1)S(1)}, u32[]{:S(2)}, u32[]{:S(2)}) collective-permute-start(bf16[1152,768]{1,0:T(8,128)(2,1)S(1)} %collective-permute-done.18.refs_2_), channel_id=1, source_target_pairs={{0,1},{1,0},{2,3},{3,2},{4,5},{5,4},{6,7},{7,6}} | collective-permute-start | bytes 5308424 | tf_op jit(solution)/shard_map/ppermute | solution.py:390
  999.8 37.3 %collective-permute-start.57 = (bf16[1152,768]{1,0:T(8,128)(2,1)S(1)}, bf16[1152,768]{1,0:T(8,128)(2,1)S(1)}, u32[]{:S(2)}, u32[]{:S(2)}) collective-permute-start(bf16[1152,768]{1,0:T(8,128)(2,1)S(1)} %collective-permute-done.56.refs_4_), channel_id=1, source_target_pairs={{0,1},{1,0},{2,3},{3,2},{4,5},{5,4},{6,7},{7,6}} | collective-permute-start | bytes 5308424 | tf_op jit(solution)/shard_map/ppermute | solution.py:390
  1002.8 35.7 %collective-permute-start.17 = (bf16[960,768]{1,0:T(8,128)(2,1)S(1)}, bf16[960,768]{1,0:T(8,128)(2,1)S(1)}, u32[]{:S(2)}, u32[]{:S(2)}) collective-permute-start(bf16[960,768]{1,0:T(8,128)(2,1)S(1)} %collective-permute-done.16.refs_2_), channel_id=1, source_target_pairs={{0,1},{1,0},{2,3},{3,2},{4,5},{5,4},{6,7},{7,6}} | collective-permute-start | bytes 4423688 | tf_op jit(solution)/shard_map/ppermute | solution.py:390
  1036.7 65.0 %collective-permute-start.14 = (bf16[960,768]{1,0:T(8,128)(2,1)}, bf16[960,768]{1,0:T(8,128)(2,1)}, u32[]{:S(2)}, u32[]{:S(2)}) collective-permute-start(bf16[960,768]{1,0:T(8,128)(2,1)} %collective-permute-done.13.refs_0_), channel_id=1, source_target_pairs={{0,1},{1,0},{2,3},{3,2},{4,5},{5,4},{6,7},{7,6}} | collective-permute-start | bytes 4423688 | tf_op jit(solution)/shard_map/ppermute | solution.py:390
  1038.4 68.2 %collective-permute-start.11 = (bf16[384,768]{1,0:T(8,128)(2,1)}, bf16[384,768]{1,0:T(8,128)(2,1)}, u32[]{:S(2)}, u32[]{:S(2)}) collective-permute-start(bf16[384,768]{1,0:T(8,128)(2,1)} %collective-permute-done.10.refs_2_), channel_id=1, source_target_pairs={{0,1},{1,0},{2,3},{3,2},{4,5},{5,4},{6,7},{7,6}} | collective-permute-start | bytes 1769480 | tf_op jit(solution)/shard_map/ppermute | solution.py:390
  1039.5 67.1 %collective-permute-start.8 = (bf16[384,768]{1,0:T(8,128)(2,1)}, bf16[384,768]{1,0:T(8,128)(2,1)}, u32[]{:S(2)}, u32[]{:S(2)}) collective-permute-start(bf16[384,768]{1,0:T(8,128)(2,1)} %collective-permute-done.7.refs_0_), channel_id=1, source_target_pairs={{0,1},{1,0},{2,3},{3,2},{4,5},{5,4},{6,7},{7,6}} | collective-permute-start | bytes 1769480 | tf_op jit(solution)/shard_map/ppermute | solution.py:390
  1041.3 68.4 %collective-permute-start.5 = (bf16[192,768]{1,0:T(8,128)(2,1)}, bf16[192,768]{1,0:T(8,128)(2,1)}, u32[]{:S(2)}, u32[]{:S(2)}) collective-permute-start(bf16[192,768]{1,0:T(8,128)(2,1)} %collective-permute-done.4.refs_2_), channel_id=1, source_target_pairs={{0,1},{1,0},{2,3},{3,2},{4,5},{5,4},{6,7},{7,6}} | collective-permute-start | bytes 884744 | tf_op jit(solution)/shard_map/ppermute | solution.py:390
  1042.5 67.2 %collective-permute-start.2 = (bf16[192,768]{1,0:T(8,128)(2,1)}, bf16[192,768]{1,0:T(8,128)(2,1)}, u32[]{:S(2)}, u32[]{:S(2)}) collective-permute-start(bf16[192,768]{1,0:T(8,128)(2,1)} %collective-permute-done.1.refs_0_), channel_id=1, source_target_pairs={{0,1},{1,0},{2,3},{3,2},{4,5},{5,4},{6,7},{7,6}} | collective-permute-start | bytes 884744 | tf_op jit(solution)/shard_map/ppermute | solution.py:390
  (167 other events, 1470.9 us)

commit v5 on v4

--- a/solution.py
+++ b/solution.py
@@ -12,6 +12,7 @@
 DECAY_RANK = 64
 ADAM_STEP = 10
 MESH = pl.DeviceIdType.MESH
+RAW = 1536
 TILE = 384
 PIECE = 128
 SLAB = 32
@@ -81,8 +82,8 @@
         old = master[:, cols]
         next_first = 0.9 * first[:, cols] + 0.1 * clipped
         next_second = 0.99 * second[:, cols] + 0.01 * (clipped * clipped)
-        first_hat = next_first / (1.0 - 0.9 ** ADAM_STEP)
-        second_hat = next_second / (1.0 - 0.99 ** ADAM_STEP)
+        first_hat = next_first * (1.0 / (1.0 - 0.9 ** ADAM_STEP))
+        second_hat = next_second * (1.0 / (1.0 - 0.99 ** ADAM_STEP))
         value = old - step_size * (first_hat / (jnp.sqrt(second_hat) + 1e-8) + decay * old)
         put(cols, value, next_first, next_second)
 
@@ -130,26 +131,35 @@
     def remote(src, dst, sent, got, device):
         return pltpu.make_async_remote_copy(src_ref=src, dst_ref=dst, send_sem=sent, recv_sem=got, device_id=(device,), device_id_type=MESH)
 
-    def send_raw(stage, tile):
+    def raw_rows(block):
+        return pl.ds(pl.multiple_of(block * RAW, RAW), RAW)
+
+    def grad_block(owner, part, block):
+        return grads.at[0, pl.ds(pl.multiple_of(owner * shard + part * half + block * RAW, TILE), RAW), :]
+
+    def send_raw(stage, block):
         x_owner = d_chip if stage == 0 else x_chip
         y_owner = d_chip if stage == 0 else y_chip
         for dest in range(2):
-            remote(grad_tile(x_owner * 2 + dest, 0, tile), x_raw.at[stage, core, rows(tile)], x_sent.at[tile], x_got.at[stage, core, tile], x_chip * 2 + dest).start()
-            remote(grad_tile(y_owner * 2 + dest, 1, tile), y_raw.at[stage, core, rows(tile)], y_sent.at[tile], y_got.at[stage, core, tile], y_chip * 2 + dest).start()
+            remote(grad_block(x_owner * 2 + dest, 0, block), x_raw.at[stage, core, raw_rows(block)], x_sent.at[block], x_got.at[stage, core, block], x_chip * 2 + dest).start()
+            remote(grad_block(y_owner * 2 + dest, 1, block), y_raw.at[stage, core, raw_rows(block)], y_sent.at[block], y_got.at[stage, core, block], y_chip * 2 + dest).start()
         first = y_chip * 2 + mate_core if stage == 0 else mate
         second = x_chip * 2 + mate_core if stage == 0 else mate
-        remote(grad_tile(first, 0, tile), mate_raw.at[2 * stage, rows(tile)], mate_sent.at[tile], mate_got.at[2 * stage, tile], mate).start()
-        remote(grad_tile(second, 1, tile), mate_raw.at[2 * stage + 1, rows(tile)], mate_sent.at[tile], mate_got.at[2 * stage + 1, tile], mate).start()
+        remote(grad_block(first, 0, block), mate_raw.at[2 * stage, raw_rows(block)], mate_sent.at[block], mate_got.at[2 * stage, block], mate).start()
+        remote(grad_block(second, 1, block), mate_raw.at[2 * stage + 1, raw_rows(block)], mate_sent.at[block], mate_got.at[2 * stage + 1, block], mate).start()
 
     def arrived(ref, sem):
         remote(ref, ref, sem, sem, mate).wait_recv()
 
     def wait_raw(stage, tile):
-        for source in range(2):
-            arrived(x_raw.at[stage, source, rows(tile)], x_got.at[stage, source, tile])
-            arrived(y_raw.at[stage, source, rows(tile)], y_got.at[stage, source, tile])
-        for part in range(2):
-            arrived(mate_raw.at[2 * stage + part, rows(tile)], mate_got.at[2 * stage + part, tile])
+        @pl.when(tile % (RAW // TILE) == 0)
+        def _():
+            block = tile // (RAW // TILE)
+            for source in range(2):
+                arrived(x_raw.at[stage, source, raw_rows(block)], x_got.at[stage, source, block])
+                arrived(y_raw.at[stage, source, raw_rows(block)], y_got.at[stage, source, block])
+            for part in range(2):
+                arrived(mate_raw.at[2 * stage + part, raw_rows(block)], mate_got.at[2 * stage + part, block])
 
     def loads(stage, tile):
         owners = (y_peer, x_peer) if stage == 0 else (me, me)
@@ -161,24 +171,25 @@
                 out.append(pltpu.make_async_copy(source, blocks.at[part, k], load_sem.at[part, k]))
         return out
 
+    @pl.loop(0, half // RAW)
+    def _(block):
+        send_raw(0, block)
+
     @pl.loop(0, tiles)
     def _(tile):
-        send_raw(0, tile)
-
-    @pl.loop(0, tiles)
-    def _(tile):
-        send_raw(1, tile)
+        @pl.when(tile % (RAW // TILE) == 0)
+        def _():
+            send_raw(1, tile // (RAW // TILE))
+
         wait_raw(0, tile)
         copies = loads(0, tile)
         for copy in copies:
             copy.start()
-        for part in range(2):
-            for copy in copies[4 * part:4 * part + 4]:
-                copy.wait()
-
-            for piece in range(TILE // PIECE):
-                here = pl.ds(piece * PIECE, PIECE)
-
+        for copy in copies:
+            copy.wait()
+        for piece in range(TILE // PIECE):
+            here = pl.ds(piece * PIECE, PIECE)
+            for part in range(2):
                 @pl.loop(piece * PIECE // SLAB, (piece + 1) * PIECE // SLAB)
                 def _(slab):
                     at = pl.ds(pl.multiple_of(slab * SLAB, SLAB), SLAB)
@@ -203,16 +214,17 @@
         copies = loads(1, tile)
         for copy in copies:
             copy.start()
-        for part in range(2):
-            for copy in copies[4 * part:4 * part + 4]:
-                copy.wait()
-            far_sum, far_got = (y_sum, x_sum)[part], (ys_got, xs_got)[part]
-
-            @pl.when(tile > 0)
-            def _():
+        for copy in copies:
+            copy.wait()
+
+        @pl.when(tile > 0)
+        def _():
+            for part in range(2):
                 pltpu.make_async_copy(finals.at[part], total_tile(part, tile), store_sem.at[part]).wait()
 
-            for piece in range(TILE // PIECE):
+        for piece in range(TILE // PIECE):
+            for part in range(2):
+                far_sum, far_got = (y_sum, x_sum)[part], (ys_got, xs_got)[part]
                 arrived(far_sum.at[tile, pl.ds(piece * PIECE, PIECE)], far_got.at[tile, piece])
 
                 @pl.loop(piece * PIECE // SLAB, (piece + 1) * PIECE // SLAB)
@@ -227,6 +239,7 @@
                             head_grad[at, :] = mean
                     squares[...] += jnp.sum((mean * mean).reshape(SLAB // 8, 8, mean.shape[1]), axis=0)
 
+        for part in range(2):
             pltpu.make_async_copy(finals.at[part], total_tile(part, tile), store_sem.at[part]).start()
 
     width = squares.shape[1]
@@ -270,10 +283,14 @@
     for k, partner in enumerate(everyone):
         remote(norm_mine, norm_mine, norm_sent.at[k], norm_sent.at[k], partner).wait_send()
 
+    @pl.loop(0, half // RAW)
+    def _(block):
+        for ref, sem in ((x_raw.at[:, :, raw_rows(block)], x_sent), (y_raw.at[:, :, raw_rows(block)], y_sent), (mate_raw.at[:, raw_rows(block)], mate_sent)):
+            remote(ref, ref, sem.at[block], sem.at[block], mate).wait_send()
+
     @pl.loop(0, tiles)
     def _(tile):
-        for ref, sem in ((x_raw.at[:, :, rows(tile)], x_sent), (y_raw.at[:, :, rows(tile)], y_sent), (mate_raw.at[:, rows(tile)], mate_sent),
-                         (x_sum.at[tile], xs_sent), (y_sum.at[tile], ys_sent)):
+        for ref, sem in ((x_sum.at[tile], xs_sent), (y_sum.at[tile], ys_sent)):
             remote(ref, ref, sem.at[tile], sem.at[tile], mate).wait_send()
 
     clip_copy.wait()
@@ -287,6 +304,7 @@
     width = local_grads.shape[2]
     half = shard // 2
     tiles = half // TILE
+    blocks = half // RAW
     any_spec = pl.BlockSpec(memory_space=pl.ANY)
     bf16, f32 = jnp.bfloat16, jnp.float32
     dma = pltpu.SemaphoreType.DMA
@@ -317,8 +335,8 @@
             pltpu.VMEM((8, width), f32),
             pltpu.VMEM((8, 128), f32),
             pltpu.VMEM((8, 8, 128), f32),
-            dma((tiles,)), dma((tiles,)), dma((tiles,)), dma((tiles,)), dma((tiles,)),
-            dma((2, 2, tiles)), dma((2, 2, tiles)), dma((4, tiles)), dma((tiles, TILE // PIECE)), dma((tiles, TILE // PIECE)),
+            dma((blocks,)), dma((blocks,)), dma((blocks,)), dma((tiles,)), dma((tiles,)),
+            dma((2, 2, blocks)), dma((2, 2, blocks)), dma((4, blocks)), dma((tiles, TILE // PIECE)), dma((tiles, TILE // PIECE)),
             dma((2, 4)), dma((2,)), dma((7,)), dma((8,)),
         ],
         compiler_params=pltpu.CompilerParams(collective_id=0, has_side_effects=True, vmem_limit_bytes=56 * 2 ** 20),
@@ -418,8 +436,11 @@
         target = None
         for pair in range(len(CHUNKS) // 2):
             target = place(shard, near[12 * pair:12 * pair + 12], target, total_rows)
-        for pair in range(len(CHUNKS) // 2):
+        last = len(CHUNKS) // 2 - 1
+        for pair in range(last):
             target = place(shard, far[4 * pair:4 * pair + 4], target, total_rows)
+        target = place(shard, far[4 * last::2], target, total_rows)
+        target = place(shard, far[4 * last + 1::2], target, total_rows)
         return (*previous, target)
 
     return jax.shard_map(device_step, mesh=mesh, in_specs=(P('dp', None, None), P('dp', None), P('dp', None), P('dp', None), P()), out_specs=(P('dp', None), P('dp', None), P('dp', None), P(None, None)), check_vma=False)

time: 1110 us -> 1110 us (level)
    pallas_call x10 -> x11, Pallas kernels: 42.3 us -> 43.8 us  [place(): pl.pallas_call(functools.partial(place_kernel, spots, shard), out_shape=j...]
where the time goes in v5:
time: 1110 us
  Pallas kernels  738 us (66%)
  waiting for transfers between devices  258 us (23%)
  local copies, waits for them, and re-layouts  76.8 us (7%)
  starting transfers between devices  37.7 us (3%)
    pallas_call x1, Pallas kernels, reduce_grads(): pl.pallas_call(functools.partial(reduce_kernel, shard), out_shape=[jax.Sh...  620 us
    ppermute x70, waiting for transfers between devices, swap(): return lax.ppermute(value, 'dp', [(i, i ^ bit) for i in range(8)])  258 us
    unnamed x258, local copies, waits for them, and re-layouts  76.8 us
    pallas_call x10, Pallas kernels, adam_chunk(): pl.pallas_call(functools.partial(adam_kernel, first_row, shard, total_row...  74.6 us
    pallas_call x11, Pallas kernels, place(): pl.pallas_call(functools.partial(place_kernel, spots, shard), out_shape=j...  43.8 us
    ppermute x70, starting transfers between devices, swap(): return lax.ppermute(value, 'dp', [(i, i ^ bit) for i in range(8)])  37.7 us
  transfers between devices with their start and end apart: 70, of which 24 were waited for; matrix products, arithmetic and copies ran while one was open for 0% of the time, Pallas kernels for 4%

profile of v5, /device:TPU:0, one launch (start us, length us, event | category | flops | bytes accessed | tf_op | source)
XLA Modules:
  0.0 1112.3 jit_solution(16631867315271775146)
XLA Ops:
  1.3 619.7 %reduce_grads.1 = (f32[6144,768]{1,0:T(8,128)}, f32[8,128]{1,0:T(8,128)}, bf16[384,768]{1,0:T(8,128)(2,1)}, bf16[2,2,3072,768]{3,2,1,0:T(8,128)(2,1)}, bf16[2,2,...) custom-call(f32[1]{0:T(128)} %bitcast.1.rate_in, bf16[1,49152,768]{2,1,0:T(8,128)(2,1)} %grads.1, ...), custom_call_target="tpu_custom_call" | custom-call | tf_op jit(solution)/shard_map/reduce_grads/pallas_call | solution.py:311
  621.0 4.7 shard_map.84
  625.7 12.4 %shard_map.85 = (f32[6144,768]{1,0:T(8,128)}, f32[6144,768]{1,0:T(8,128)}, f32[6144,768]{1,0:T(8,128)}, bf16[1152,768]{1,0:T(8,128)(2,1)}) custom-call(f32[1]{0:T(128)} %bitcast.3.rate_ref, f32[8,128]{1,0:T(8,128)} %get-tuple-element.46.clip_ref, f32[6144,768]{1,0:T(8,128)} %get-tuple-element.47.grad, ...), custom_call_target="tpu_custom_call", output_to_operand_aliasing={{0}: (6, {}), {1}: (7, {}), {2}: (8, {})} | custom-call | flops 53084160 | bytes 26542080 | tf_op jit(solution)/shard_map/pallas_call | solution.py:356
  638.1 12.4 %shard_map.86 = (f32[6144,768]{1,0:T(8,128)}, f32[6144,768]{1,0:T(8,128)}, f32[6144,768]{1,0:T(8,128)}, bf16[1152,768]{1,0:T(8,128)(2,1)}) custom-call(f32[1]{0:T(128)} %bitcast.4.rate_ref, f32[8,128]{1,0:T(8,128)} %get-tuple-element.46.clip_ref, f32[6144,768]{1,0:T(8,128)} %get-tuple-element.47.grad, ...), custom_call_target="tpu_custom_call", output_to_operand_aliasing={{0}: (6, {}), {1}: (7, {}), {2}: (8, {})} | custom-call | flops 53084160 | bytes 26542080 | tf_op jit(solution)/shard_map/pallas_call | solution.py:356
  650.5 11.6 %shard_map.87 = (f32[6144,768]{1,0:T(8,128)}, f32[6144,768]{1,0:T(8,128)}, f32[6144,768]{1,0:T(8,128)}, bf16[960,768]{1,0:T(8,128)(2,1)}) custom-call(f32[1]{0:T(128)} %bitcast.5.rate_ref, f32[8,128]{1,0:T(8,128)} %get-tuple-element.46.clip_ref, f32[6144,768]{1,0:T(8,128)} %get-tuple-element.47.grad, ...), custom_call_target="tpu_custom_call", output_to_operand_aliasing={{0}: (6, {}), {1}: (7, {}), {2}: (8, {})} | custom-call | flops 44236800 | bytes 22118400 | tf_op jit(solution)/shard_map/pallas_call | solution.py:356
  662.1 11.8 %shard_map.88 = (f32[6144,768]{1,0:T(8,128)}, f32[6144,768]{1,0:T(8,128)}, f32[6144,768]{1,0:T(8,128)}, bf16[960,768]{1,0:T(8,128)(2,1)}) custom-call(f32[1]{0:T(128)} %bitcast.6.rate_ref, f32[8,128]{1,0:T(8,128)} %get-tuple-element.46.clip_ref, f32[6144,768]{1,0:T(8,128)} %get-tuple-element.47.grad, ...), custom_call_target="tpu_custom_call", output_to_operand_aliasing={{0}: (6, {}), {1}: (7, {}), {2}: (8, {})} | custom-call | flops 44236800 | bytes 22118400 | tf_op jit(solution)/shard_map/pallas_call | solution.py:356
  673.9 4.7 shard_map.89
  678.6 4.8 shard_map.90
  683.4 3.7 shard_map.91
  687.1 3.8 shard_map.92
  695.0 6.0 collective-permute-done.35.refs_8_
  703.8 15.4 %collective-permute-done.refs_2_ = bf16[192,768]{1,0:T(8,128)(2,1)S(1)} collective-permute-done((bf16[192,768]{1,0:T(8,128)(2,1)S(1)}, bf16[192,768]{1,0:T(8,128)(2,1)S(1)}, u32[]{:S(2)}, u32[]{:S(2)}) %collective-permute-start) | collective-permute-done | bytes 294944 | tf_op jit(solution)/shard_map/ppermute | solution.py:408
  726.0 10.5 collective-permute-done.24.refs_2_
  740.7 8.5 collective-permute-done.43.refs_8_
  752.5 7.7 collective-permute-done.6.refs_2_
  771.2 4.8 collective-permute-done.4.refs_1_
  794.6 34.7 %collective-permute-done.28.refs_2_ = bf16[384,768]{1,0:T(8,128)(2,1)S(1)} collective-permute-done((bf16[384,768]{1,0:T(8,128)(2,1)S(1)}, bf16[384,768]{1,0:T(8,128)(2,1)S(1)}, u32[]{:S(2)}, u32[]{:S(2)}) %collective-permute-start.28) | collective-permute-done | bytes 589856 | tf_op jit(solution)/shard_map/ppermute | solution.py:408
  831.4 10.2 collective-permute-done.10.refs_2_
  848.6 28.4 %collective-permute-done.12.refs_2_ = bf16[960,768]{1,0:T(8,128)(2,1)S(1)} collective-permute-done((bf16[960,768]{1,0:T(8,128)(2,1)}, bf16[960,768]{1,0:T(8,128)(2,1)S(1)}, u32[]{:S(2)}, u32[]{:S(2)}) %collective-permute-start.12) | collective-permute-done | bytes 1474592 | tf_op jit(solution)/shard_map/ppermute | solution.py:408
  882.4 32.5 %collective-permute-done.59.refs_8_ = bf16[1152,768]{1,0:T(8,128)(2,1)S(1)} collective-permute-done((bf16[1152,768]{1,0:T(8,128)(2,1)S(1)}, bf16[1152,768]{1,0:T(8,128)(2,1)S(1)}, u32[]{:S(2)}, u32[]{:S(2)}) %collective-permute-start.59) | collective-permute-done | bytes 1769504 | tf_op jit(solution)/shard_map/ppermute | solution.py:408
  920.8 30.7 %collective-permute-done.18.refs_2_ = bf16[1152,768]{1,0:T(8,128)(2,1)S(1)} collective-permute-done((bf16[1152,768]{1,0:T(8,128)(2,1)S(1)}, bf16[1152,768]{1,0:T(8,128)(2,1)S(1)}, u32[]{:S(2)}, u32[]{:S(2)}) %collective-permute-start.18) | collective-permute-done | bytes 1769504 | tf_op jit(solution)/shard_map/ppermute | solution.py:408
  968.0 24.5 %collective-permute-done.16.refs_2_ = bf16[960,768]{1,0:T(8,128)(2,1)S(1)} collective-permute-done((bf16[960,768]{1,0:T(8,128)(2,1)S(1)}, bf16[960,768]{1,0:T(8,128)(2,1)S(1)}, u32[]{:S(2)}, u32[]{:S(2)}) %collective-permute-start.16) | collective-permute-done | bytes 1474592 | tf_op jit(solution)/shard_map/ppermute | solution.py:408
  993.8 2.4 collective-permute-done.13.refs_0_
  1002.7 27.1 %collective-permute-done.22.refs_2_ = bf16[1152,768]{1,0:T(8,128)(2,1)S(1)} collective-permute-done((bf16[1152,768]{1,0:T(8,128)(2,1)S(1)}, bf16[1152,768]{1,0:T(8,128)(2,1)S(1)}, u32[]{:S(2)}, u32[]{:S(2)}) %collective-permute-start.22) | collective-permute-done | bytes 1769504 | tf_op jit(solution)/shard_map/ppermute | solution.py:408
  1041.9 4.7 shard_map.93
  1057.3 3.7 shard_map.94.refs_12_
  1064.9 10.4 shard_map.95.refs_12_
  1077.8 8.2 shard_map.96.refs_12_
  1086.2 3.5 shard_map.97.refs_12_
  1097.1 3.4 shard_map.100.refs_4_
  1101.0 4.4 shard_map.101.refs_4_
  1105.5 3.0 shard_map.102.refs_2_
  (388 shorter events, 135.7 us)
Async XLA Ops:
  693.0 29.9 %collective-permute-start.27 = (bf16[384,768]{1,0:T(8,128)(2,1)S(1)}, bf16[384,768]{1,0:T(8,128)(2,1)S(1)}, u32[]{:S(2)}, u32[]{:S(2)}) collective-permute-start(bf16[384,768]{1,0:T(8,128)(2,1)S(1)} %copy-done.77), channel_id=1, source_target_pairs={{0,4},{1,5},{2,6},{3,7},{4,0},{5,1},{6,2},{7,3}} | collective-permute-start | bytes 1769480 | tf_op jit(solution)/shard_map/ppermute | solution.py:408
  694.4 28.5 %collective-permute-start.67 = (bf16[384,768]{1,0:T(8,128)(2,1)S(1)}, bf16[384,768]{1,0:T(8,128)(2,1)S(1)}, u32[]{:S(2)}, u32[]{:S(2)}) collective-permute-start(bf16[384,768]{1,0:T(8,128)(2,1)S(1)} %copy-done.77), channel_id=1, source_target_pairs={{0,2},{1,3},{2,0},{3,1},{4,6},{5,7},{6,4},{7,5}} | collective-permute-start | bytes 1769480 | tf_op jit(solution)/shard_map/ppermute | solution.py:408
  781.5 63.6 %collective-permute-start.51 = (bf16[960,768]{1,0:T(8,128)(2,1)S(1)}, bf16[960,768]{1,0:T(8,128)(2,1)S(1)}, u32[]{:S(2)}, u32[]{:S(2)}) collective-permute-start(bf16[960,768]{1,0:T(8,128)(2,1)S(1)} %copy-done.26), channel_id=1, source_target_pairs={{0,2},{1,3},{2,0},{3,1},{4,6},{5,7},{6,4},{7,5}} | collective-permute-start | bytes 4423688 | tf_op jit(solution)/shard_map/ppermute | solution.py:408
  783.8 61.3 %collective-permute-start.15 = (bf16[960,768]{1,0:T(8,128)(2,1)S(1)}, bf16[960,768]{1,0:T(8,128)(2,1)S(1)}, u32[]{:S(2)}, u32[]{:S(2)}) collective-permute-start(bf16[960,768]{1,0:T(8,128)(2,1)S(1)} %copy-done.26), channel_id=1, source_target_pairs={{0,4},{1,5},{2,6},{3,7},{4,0},{5,1},{6,2},{7,3}} | collective-permute-start | bytes 4423688 | tf_op jit(solution)/shard_map/ppermute | solution.py:408
  786.9 42.4 %collective-permute-start.28 = (bf16[384,768]{1,0:T(8,128)(2,1)S(1)}, bf16[384,768]{1,0:T(8,128)(2,1)S(1)}, u32[]{:S(2)}, u32[]{:S(2)}) collective-permute-start(bf16[384,768]{1,0:T(8,128)(2,1)S(1)} %collective-permute-done.27.refs_10_), channel_id=1, source_target_pairs={{0,2},{1,3},{2,0},{3,1},{4,6},{5,7},{6,4},{7,5}} | collective-permute-start | bytes 1769480 | tf_op jit(solution)/shard_map/ppermute | solution.py:408
  789.8 41.6 %collective-permute-start.25 = (bf16[384,768]{1,0:T(8,128)(2,1)S(1)}, bf16[384,768]{1,0:T(8,128)(2,1)S(1)}, u32[]{:S(2)}, u32[]{:S(2)}) collective-permute-start(bf16[384,768]{1,0:T(8,128)(2,1)S(1)} %collective-permute-done.24.refs_2_), channel_id=1, source_target_pairs={{0,4},{1,5},{2,6},{3,7},{4,0},{5,1},{6,2},{7,3}} | collective-permute-start | bytes 1769480 | tf_op jit(solution)/shard_map/ppermute | solution.py:408
  792.3 49.3 %collective-permute-start.10 = (bf16[384,768]{1,0:T(8,128)(2,1)S(1)}, bf16[384,768]{1,0:T(8,128)(2,1)}, u32[]{:S(2)}, u32[]{:S(2)}) collective-permute-start(bf16[384,768]{1,0:T(8,128)(2,1)S(1)} %collective-permute-done.9.refs_10_), channel_id=1, source_target_pairs={{0,2},{1,3},{2,0},{3,1},{4,6},{5,7},{6,4},{7,5}} | collective-permute-start | bytes 1769480 | tf_op jit(solution)/shard_map/ppermute | solution.py:408
  841.6 35.4 %collective-permute-start.12 = (bf16[960,768]{1,0:T(8,128)(2,1)}, bf16[960,768]{1,0:T(8,128)(2,1)S(1)}, u32[]{:S(2)}, u32[]{:S(2)}) collective-permute-start(bf16[960,768]{1,0:T(8,128)(2,1)} %get-tuple-element.82.refs_0_), channel_id=1, source_target_pairs={{0,2},{1,3},{2,0},{3,1},{4,6},{5,7},{6,4},{7,5}} | collective-permute-start | bytes 4423688 | tf_op jit(solution)/shard_map/ppermute | solution.py:408
  843.9 35.4 %collective-permute-start.48 = (bf16[960,768]{1,0:T(8,128)(2,1)}, bf16[960,768]{1,0:T(8,128)(2,1)S(1)}, u32[]{:S(2)}, u32[]{:S(2)}) collective-permute-start(bf16[960,768]{1,0:T(8,128)(2,1)} %get-tuple-element.82.refs_0_), channel_id=1, source_target_pairs={{0,4},{1,5},{2,6},{3,7},{4,0},{5,1},{6,2},{7,3}} | collective-permute-start | bytes 4423688 | tf_op jit(solution)/shard_map/ppermute | solution.py:408
  845.1 35.6 %collective-permute-start.46 = (bf16[960,768]{1,0:T(8,128)(2,1)}, bf16[960,768]{1,0:T(8,128)(2,1)S(1)}, u32[]{:S(2)}, u32[]{:S(2)}) collective-permute-start(bf16[960,768]{1,0:T(8,128)(2,1)} %get-tuple-element.82.refs_0_), channel_id=1, source_target_pairs={{0,1},{1,0},{2,3},{3,2},{4,5},{5,4},{6,7},{7,6}} | collective-permute-start | bytes 4423688 | tf_op jit(solution)/shard_map/ppermute | solution.py:408
  845.2 69.7 %collective-permute-start.59 = (bf16[1152,768]{1,0:T(8,128)(2,1)S(1)}, bf16[1152,768]{1,0:T(8,128)(2,1)S(1)}, u32[]{:S(2)}, u32[]{:S(2)}) collective-permute-start(bf16[1152,768]{1,0:T(8,128)(2,1)S(1)} %copy-done.9), channel_id=1, source_target_pairs={{0,2},{1,3},{2,0},{3,1},{4,6},{5,7},{6,4},{7,5}} | collective-permute-start | bytes 5308424 | tf_op jit(solution)/shard_map/ppermute | solution.py:408
  847.1 70.1 %collective-permute-start.21 = (bf16[1152,768]{1,0:T(8,128)(2,1)S(1)}, bf16[1152,768]{1,0:T(8,128)(2,1)S(1)}, u32[]{:S(2)}, u32[]{:S(2)}) collective-permute-start(bf16[1152,768]{1,0:T(8,128)(2,1)S(1)} %copy-done.9), channel_id=1, source_target_pairs={{0,4},{1,5},{2,6},{3,7},{4,0},{5,1},{6,2},{7,3}} | collective-permute-start | bytes 5308424 | tf_op jit(solution)/shard_map/ppermute | solution.py:408
  877.0 41.3 %collective-permute-start.58 = (bf16[1152,768]{1,0:T(8,128)(2,1)S(1)}, bf16[1152,768]{1,0:T(8,128)(2,1)S(1)}, u32[]{:S(2)}, u32[]{:S(2)}) collective-permute-start(bf16[1152,768]{1,0:T(8,128)(2,1)S(1)} %copy-done.9), channel_id=1, source_target_pairs={{0,1},{1,0},{2,3},{3,2},{4,5},{5,4},{6,7},{7,6}} | collective-permute-start | bytes 5308424 | tf_op jit(solution)/shard_map/ppermute | solution.py:408
  879.2 72.3 %collective-permute-start.18 = (bf16[1152,768]{1,0:T(8,128)(2,1)S(1)}, bf16[1152,768]{1,0:T(8,128)(2,1)S(1)}, u32[]{:S(2)}, u32[]{:S(2)}) collective-permute-start(bf16[1152,768]{1,0:T(8,128)(2,1)S(1)} %copy-done.8), channel_id=1, source_target_pairs={{0,2},{1,3},{2,0},{3,1},{4,6},{5,7},{6,4},{7,5}} | collective-permute-start | bytes 5308424 | tf_op jit(solution)/shard_map/ppermute | solution.py:408
  881.8 70.9 %collective-permute-start.56 = (bf16[1152,768]{1,0:T(8,128)(2,1)S(1)}, bf16[1152,768]{1,0:T(8,128)(2,1)S(1)}, u32[]{:S(2)}, u32[]{:S(2)}) collective-permute-start(bf16[1152,768]{1,0:T(8,128)(2,1)S(1)} %copy-done.8), channel_id=1, source_target_pairs={{0,4},{1,5},{2,6},{3,7},{4,0},{5,1},{6,2},{7,3}} | collective-permute-start | bytes 5308424 | tf_op jit(solution)/shard_map/ppermute | solution.py:408
  914.9 37.9 %collective-permute-start.54 = (bf16[1152,768]{1,0:T(8,128)(2,1)S(1)}, bf16[1152,768]{1,0:T(8,128)(2,1)S(1)}, u32[]{:S(2)}, u32[]{:S(2)}) collective-permute-start(bf16[1152,768]{1,0:T(8,128)(2,1)S(1)} %copy-done.8), channel_id=1, source_target_pairs={{0,1},{1,0},{2,3},{3,2},{4,5},{5,4},{6,7},{7,6}} | collective-permute-start | bytes 5308424 | tf_op jit(solution)/shard_map/ppermute | solution.py:408
  917.2 42.8 %collective-permute-start.52 = (bf16[960,768]{1,0:T(8,128)(2,1)S(1)}, bf16[960,768]{1,0:T(8,128)(2,1)S(1)}, u32[]{:S(2)}, u32[]{:S(2)}) collective-permute-start(bf16[960,768]{1,0:T(8,128)(2,1)S(1)} %collective-permute-done.51.refs_8_), channel_id=1, source_target_pairs={{0,1},{1,0},{2,3},{3,2},{4,5},{5,4},{6,7},{7,6}} | collective-permute-start | bytes 4423688 | tf_op jit(solution)/shard_map/ppermute | solution.py:408
  919.5 35.0 %collective-permute-start.29 = (bf16[384,768]{1,0:T(8,128)(2,1)S(1)}, bf16[384,768]{1,0:T(8,128)(2,1)S(1)}, u32[]{:S(2)}, u32[]{:S(2)}) collective-permute-start(bf16[384,768]{1,0:T(8,128)(2,1)S(1)} %collective-permute-done.28.refs_2_), channel_id=1, source_target_pairs={{0,1},{1,0},{2,3},{3,2},{4,5},{5,4},{6,7},{7,6}} | collective-permute-start | bytes 1769480 | tf_op jit(solution)/shard_map/ppermute | solution.py:408
  957.4 35.2 %collective-permute-start.16 = (bf16[960,768]{1,0:T(8,128)(2,1)S(1)}, bf16[960,768]{1,0:T(8,128)(2,1)S(1)}, u32[]{:S(2)}, u32[]{:S(2)}) collective-permute-start(bf16[960,768]{1,0:T(8,128)(2,1)S(1)} %collective-permute-done.15.refs_10_), channel_id=1, source_target_pairs={{0,2},{1,3},{2,0},{3,1},{4,6},{5,7},{6,4},{7,5}} | collective-permute-start | bytes 4423688 | tf_op jit(solution)/shard_map/ppermute | solution.py:408
  961.1 35.1 %collective-permute-start.13 = (bf16[960,768]{1,0:T(8,128)(2,1)S(1)}, bf16[960,768]{1,0:T(8,128)(2,1)}, u32[]{:S(2)}, u32[]{:S(2)}) collective-permute-start(bf16[960,768]{1,0:T(8,128)(2,1)S(1)} %collective-permute-done.12.refs_2_), channel_id=1, source_target_pairs={{0,4},{1,5},{2,6},{3,7},{4,0},{5,1},{6,2},{7,3}} | collective-permute-start | bytes 4423688 | tf_op jit(solution)/shard_map/ppermute | solution.py:408
  963.9 33.5 %collective-permute-start.60 = (bf16[1152,768]{1,0:T(8,128)(2,1)S(1)}, bf16[1152,768]{1,0:T(8,128)(2,1)S(1)}, u32[]{:S(2)}, u32[]{:S(2)}) collective-permute-start(bf16[1152,768]{1,0:T(8,128)(2,1)S(1)} %collective-permute-done.59.refs_8_), channel_id=1, source_target_pairs={{0,1},{1,0},{2,3},{3,2},{4,5},{5,4},{6,7},{7,6}} | collective-permute-start | bytes 5308424 | tf_op jit(solution)/shard_map/ppermute | solution.py:408
  965.1 35.2 %collective-permute-start.61 = (bf16[1152,768]{1,0:T(8,128)(2,1)S(1)}, bf16[1152,768]{1,0:T(8,128)(2,1)S(1)}, u32[]{:S(2)}, u32[]{:S(2)}) collective-permute-start(bf16[1152,768]{1,0:T(8,128)(2,1)S(1)} %collective-permute-done.21.refs_10_), channel_id=1, source_target_pairs={{0,1},{1,0},{2,3},{3,2},{4,5},{5,4},{6,7},{7,6}} | collective-permute-start | bytes 5308424 | tf_op jit(solution)/shard_map/ppermute | solution.py:408
  966.8 63.1 %collective-permute-start.22 = (bf16[1152,768]{1,0:T(8,128)(2,1)S(1)}, bf16[1152,768]{1,0:T(8,128)(2,1)S(1)}, u32[]{:S(2)}, u32[]{:S(2)}) collective-permute-start(bf16[1152,768]{1,0:T(8,128)(2,1)S(1)} %collective-permute-done.21.refs_10_), channel_id=1, source_target_pairs={{0,2},{1,3},{2,0},{3,1},{4,6},{5,7},{6,4},{7,5}} | collective-permute-start | bytes 5308424 | tf_op jit(solution)/shard_map/ppermute | solution.py:408
  992.5 40.5 %collective-permute-start.19 = (bf16[1152,768]{1,0:T(8,128)(2,1)S(1)}, bf16[1152,768]{1,0:T(8,128)(2,1)S(1)}, u32[]{:S(2)}, u32[]{:S(2)}) collective-permute-start(bf16[1152,768]{1,0:T(8,128)(2,1)S(1)} %collective-permute-done.18.refs_2_), channel_id=1, source_target_pairs={{0,4},{1,5},{2,6},{3,7},{4,0},{5,1},{6,2},{7,3}} | collective-permute-start | bytes 5308424 | tf_op jit(solution)/shard_map/ppermute | solution.py:408
  996.2 38.1 %collective-permute-start.55 = (bf16[1152,768]{1,0:T(8,128)(2,1)S(1)}, bf16[1152,768]{1,0:T(8,128)(2,1)S(1)}, u32[]{:S(2)}, u32[]{:S(2)}) collective-permute-start(bf16[1152,768]{1,0:T(8,128)(2,1)S(1)} %collective-permute-done.18.refs_2_), channel_id=1, source_target_pairs={{0,1},{1,0},{2,3},{3,2},{4,5},{5,4},{6,7},{7,6}} | collective-permute-start | bytes 5308424 | tf_op jit(solution)/shard_map/ppermute | solution.py:408
  998.7 37.3 %collective-permute-start.57 = (bf16[1152,768]{1,0:T(8,128)(2,1)S(1)}, bf16[1152,768]{1,0:T(8,128)(2,1)S(1)}, u32[]{:S(2)}, u32[]{:S(2)}) collective-permute-start(bf16[1152,768]{1,0:T(8,128)(2,1)S(1)} %collective-permute-done.56.refs_4_), channel_id=1, source_target_pairs={{0,1},{1,0},{2,3},{3,2},{4,5},{5,4},{6,7},{7,6}} | collective-permute-start | bytes 5308424 | tf_op jit(solution)/shard_map/ppermute | solution.py:408
  1001.6 35.7 %collective-permute-start.17 = (bf16[960,768]{1,0:T(8,128)(2,1)S(1)}, bf16[960,768]{1,0:T(8,128)(2,1)S(1)}, u32[]{:S(2)}, u32[]{:S(2)}) collective-permute-start(bf16[960,768]{1,0:T(8,128)(2,1)S(1)} %collective-permute-done.16.refs_2_), channel_id=1, source_target_pairs={{0,1},{1,0},{2,3},{3,2},{4,5},{5,4},{6,7},{7,6}} | collective-permute-start | bytes 4423688 | tf_op jit(solution)/shard_map/ppermute | solution.py:408
  1035.5 65.0 %collective-permute-start.14 = (bf16[960,768]{1,0:T(8,128)(2,1)}, bf16[960,768]{1,0:T(8,128)(2,1)}, u32[]{:S(2)}, u32[]{:S(2)}) collective-permute-start(bf16[960,768]{1,0:T(8,128)(2,1)} %collective-permute-done.13.refs_0_), channel_id=1, source_target_pairs={{0,1},{1,0},{2,3},{3,2},{4,5},{5,4},{6,7},{7,6}} | collective-permute-start | bytes 4423688 | tf_op jit(solution)/shard_map/ppermute | solution.py:408
  1037.2 68.2 %collective-permute-start.11 = (bf16[384,768]{1,0:T(8,128)(2,1)}, bf16[384,768]{1,0:T(8,128)(2,1)}, u32[]{:S(2)}, u32[]{:S(2)}) collective-permute-start(bf16[384,768]{1,0:T(8,128)(2,1)} %collective-permute-done.10.refs_2_), channel_id=1, source_target_pairs={{0,1},{1,0},{2,3},{3,2},{4,5},{5,4},{6,7},{7,6}} | collective-permute-start | bytes 1769480 | tf_op jit(solution)/shard_map/ppermute | solution.py:408
  1038.4 67.1 %collective-permute-start.8 = (bf16[384,768]{1,0:T(8,128)(2,1)}, bf16[384,768]{1,0:T(8,128)(2,1)}, u32[]{:S(2)}, u32[]{:S(2)}) collective-permute-start(bf16[384,768]{1,0:T(8,128)(2,1)} %collective-permute-done.7.refs_0_), channel_id=1, source_target_pairs={{0,1},{1,0},{2,3},{3,2},{4,5},{5,4},{6,7},{7,6}} | collective-permute-start | bytes 1769480 | tf_op jit(solution)/shard_map/ppermute | solution.py:408
  1040.1 70.3 %collective-permute-start.5 = (bf16[192,768]{1,0:T(8,128)(2,1)}, bf16[192,768]{1,0:T(8,128)(2,1)}, u32[]{:S(2)}, u32[]{:S(2)}) collective-permute-start(bf16[192,768]{1,0:T(8,128)(2,1)} %collective-permute-done.4.refs_1_), channel_id=1, source_target_pairs={{0,1},{1,0},{2,3},{3,2},{4,5},{5,4},{6,7},{7,6}} | collective-permute-start | bytes 884744 | tf_op jit(solution)/shard_map/ppermute | solution.py:408
  1041.3 69.1 %collective-permute-start.2 = (bf16[192,768]{1,0:T(8,128)(2,1)}, bf16[192,768]{1,0:T(8,128)(2,1)}, u32[]{:S(2)}, u32[]{:S(2)}) collective-permute-start(bf16[192,768]{1,0:T(8,128)(2,1)} %collective-permute-done.1.refs_0_), channel_id=1, source_target_pairs={{0,1},{1,0},{2,3},{3,2},{4,5},{5,4},{6,7},{7,6}} | collective-permute-start | bytes 884744 | tf_op jit(solution)/shard_map/ppermute | solution.py:408
  (167 other events, 1470.9 us)

commit v6 on v5

--- a/solution.py
+++ b/solution.py
@@ -12,12 +12,12 @@
 DECAY_RANK = 64
 ADAM_STEP = 10
 MESH = pl.DeviceIdType.MESH
-RAW = 1536
+RAW = 3072
 TILE = 384
-PIECE = 128
-SLAB = 32
+PIECE = 192
+SLAB = 64
 ADAM_TILE = 192
-ADAM_SLAB = 32
+ADAM_SLAB = 96
 CHUNKS = (384, 384, 1152, 1152, 960, 960, 384, 384, 192, 192)
 ADAM_FLOPS = 60
 PLACE_FLOPS = 16
@@ -117,7 +117,7 @@
     me, core, mate, x_chip, y_chip, d_chip = places()
     mate_core = 1 - core
     x_peer, y_peer = x_chip * 2 + core, y_chip * 2 + core
-    everyone = [mate, x_chip * 2, x_chip * 2 + 1, y_chip * 2, y_chip * 2 + 1, d_chip * 2, d_chip * 2 + 1]
+    everyone = [d_chip * 2, d_chip * 2 + 1, x_chip * 2, x_chip * 2 + 1, y_chip * 2, y_chip * 2 + 1, mate]
     greet(everyone)
     head = [pltpu.make_async_copy(state.at[pl.ds(0, TILE)], head_state.at[k], head_sem.at[k]) for k, state in enumerate((master, first, second))]
     head.append(pltpu.make_async_copy(rate_in, rate_ref, head_sem.at[3]))

time: 1110 us -> 1110 us (level)
  no operation moved by 1% of the time
where the time goes in v6:
time: 1110 us
  Pallas kernels  738 us (66%)
  waiting for transfers between devices  258 us (23%)
  local copies, waits for them, and re-layouts  76.8 us (7%)
  starting transfers between devices  37.4 us (3%)
    pallas_call x1, Pallas kernels, reduce_grads(): pl.pallas_call(functools.partial(reduce_kernel, shard), out_shape=[jax.Sh...  619 us
    ppermute x70, waiting for transfers between devices, swap(): return lax.ppermute(value, 'dp', [(i, i ^ bit) for i in range(8)])  258 us
    unnamed x258, local copies, waits for them, and re-layouts  76.8 us
    pallas_call x10, Pallas kernels, adam_chunk(): pl.pallas_call(functools.partial(adam_kernel, first_row, shard, total_row...  74.7 us
    pallas_call x11, Pallas kernels, place(): pl.pallas_call(functools.partial(place_kernel, spots, shard), out_shape=j...  43.8 us
    ppermute x70, starting transfers between devices, swap(): return lax.ppermute(value, 'dp', [(i, i ^ bit) for i in range(8)])  37.4 us
  transfers between devices with their start and end apart: 70, of which 24 were waited for; matrix products, arithmetic and copies ran while one was open for 0% of the time, Pallas kernels for 4%

profile of v6, /device:TPU:0, one launch (start us, length us, event | category | flops | bytes accessed | tf_op | source)
XLA Modules:
  0.0 1112.1 jit_solution(1989153420286978219)
XLA Ops:
  1.3 619.5 %reduce_grads.1 = (f32[6144,768]{1,0:T(8,128)}, f32[8,128]{1,0:T(8,128)}, bf16[384,768]{1,0:T(8,128)(2,1)}, bf16[2,2,3072,768]{3,2,1,0:T(8,128)(2,1)}, bf16[2,2,...) custom-call(f32[1]{0:T(128)} %bitcast.1.rate_in, bf16[1,49152,768]{2,1,0:T(8,128)(2,1)} %grads.1, ...), custom_call_target="tpu_custom_call" | custom-call | tf_op jit(solution)/shard_map/reduce_grads/pallas_call | solution.py:311
  620.8 4.7 shard_map.84
  625.5 12.4 %shard_map.85 = (f32[6144,768]{1,0:T(8,128)}, f32[6144,768]{1,0:T(8,128)}, f32[6144,768]{1,0:T(8,128)}, bf16[1152,768]{1,0:T(8,128)(2,1)}) custom-call(f32[1]{0:T(128)} %bitcast.3.rate_ref, f32[8,128]{1,0:T(8,128)} %get-tuple-element.46.clip_ref, f32[6144,768]{1,0:T(8,128)} %get-tuple-element.47.grad, ...), custom_call_target="tpu_custom_call", output_to_operand_aliasing={{0}: (6, {}), {1}: (7, {}), {2}: (8, {})} | custom-call | flops 53084160 | bytes 26542080 | tf_op jit(solution)/shard_map/pallas_call | solution.py:356
  637.9 12.4 %shard_map.86 = (f32[6144,768]{1,0:T(8,128)}, f32[6144,768]{1,0:T(8,128)}, f32[6144,768]{1,0:T(8,128)}, bf16[1152,768]{1,0:T(8,128)(2,1)}) custom-call(f32[1]{0:T(128)} %bitcast.4.rate_ref, f32[8,128]{1,0:T(8,128)} %get-tuple-element.46.clip_ref, f32[6144,768]{1,0:T(8,128)} %get-tuple-element.47.grad, ...), custom_call_target="tpu_custom_call", output_to_operand_aliasing={{0}: (6, {}), {1}: (7, {}), {2}: (8, {})} | custom-call | flops 53084160 | bytes 26542080 | tf_op jit(solution)/shard_map/pallas_call | solution.py:356
  650.3 11.6 %shard_map.87 = (f32[6144,768]{1,0:T(8,128)}, f32[6144,768]{1,0:T(8,128)}, f32[6144,768]{1,0:T(8,128)}, bf16[960,768]{1,0:T(8,128)(2,1)}) custom-call(f32[1]{0:T(128)} %bitcast.5.rate_ref, f32[8,128]{1,0:T(8,128)} %get-tuple-element.46.clip_ref, f32[6144,768]{1,0:T(8,128)} %get-tuple-element.47.grad, ...), custom_call_target="tpu_custom_call", output_to_operand_aliasing={{0}: (6, {}), {1}: (7, {}), {2}: (8, {})} | custom-call | flops 44236800 | bytes 22118400 | tf_op jit(solution)/shard_map/pallas_call | solution.py:356
  661.9 11.8 %shard_map.88 = (f32[6144,768]{1,0:T(8,128)}, f32[6144,768]{1,0:T(8,128)}, f32[6144,768]{1,0:T(8,128)}, bf16[960,768]{1,0:T(8,128)(2,1)}) custom-call(f32[1]{0:T(128)} %bitcast.6.rate_ref, f32[8,128]{1,0:T(8,128)} %get-tuple-element.46.clip_ref, f32[6144,768]{1,0:T(8,128)} %get-tuple-element.47.grad, ...), custom_call_target="tpu_custom_call", output_to_operand_aliasing={{0}: (6, {}), {1}: (7, {}), {2}: (8, {})} | custom-call | flops 44236800 | bytes 22118400 | tf_op jit(solution)/shard_map/pallas_call | solution.py:356
  673.7 4.7 shard_map.89
  678.4 4.8 shard_map.90
  683.3 3.7 shard_map.91
  687.0 3.8 shard_map.92
  694.8 6.0 collective-permute-done.35.refs_8_
  703.6 15.3 %collective-permute-done.refs_2_ = bf16[192,768]{1,0:T(8,128)(2,1)S(1)} collective-permute-done((bf16[192,768]{1,0:T(8,128)(2,1)S(1)}, bf16[192,768]{1,0:T(8,128)(2,1)S(1)}, u32[]{:S(2)}, u32[]{:S(2)}) %collective-permute-start) | collective-permute-done | bytes 294944 | tf_op jit(solution)/shard_map/ppermute | solution.py:408
  725.8 10.5 collective-permute-done.24.refs_2_
  740.5 8.4 collective-permute-done.43.refs_8_
  752.2 7.7 collective-permute-done.6.refs_2_
  770.8 4.9 collective-permute-done.4.refs_1_
  794.4 34.7 %collective-permute-done.28.refs_2_ = bf16[384,768]{1,0:T(8,128)(2,1)S(1)} collective-permute-done((bf16[384,768]{1,0:T(8,128)(2,1)S(1)}, bf16[384,768]{1,0:T(8,128)(2,1)S(1)}, u32[]{:S(2)}, u32[]{:S(2)}) %collective-permute-start.28) | collective-permute-done | bytes 589856 | tf_op jit(solution)/shard_map/ppermute | solution.py:408
  831.1 10.3 collective-permute-done.10.refs_2_
  848.3 28.5 %collective-permute-done.12.refs_2_ = bf16[960,768]{1,0:T(8,128)(2,1)S(1)} collective-permute-done((bf16[960,768]{1,0:T(8,128)(2,1)}, bf16[960,768]{1,0:T(8,128)(2,1)S(1)}, u32[]{:S(2)}, u32[]{:S(2)}) %collective-permute-start.12) | collective-permute-done | bytes 1474592 | tf_op jit(solution)/shard_map/ppermute | solution.py:408
  882.2 32.5 %collective-permute-done.59.refs_8_ = bf16[1152,768]{1,0:T(8,128)(2,1)S(1)} collective-permute-done((bf16[1152,768]{1,0:T(8,128)(2,1)S(1)}, bf16[1152,768]{1,0:T(8,128)(2,1)S(1)}, u32[]{:S(2)}, u32[]{:S(2)}) %collective-permute-start.59) | collective-permute-done | bytes 1769504 | tf_op jit(solution)/shard_map/ppermute | solution.py:408
  920.6 30.7 %collective-permute-done.18.refs_2_ = bf16[1152,768]{1,0:T(8,128)(2,1)S(1)} collective-permute-done((bf16[1152,768]{1,0:T(8,128)(2,1)S(1)}, bf16[1152,768]{1,0:T(8,128)(2,1)S(1)}, u32[]{:S(2)}, u32[]{:S(2)}) %collective-permute-start.18) | collective-permute-done | bytes 1769504 | tf_op jit(solution)/shard_map/ppermute | solution.py:408
  967.7 24.6 %collective-permute-done.16.refs_2_ = bf16[960,768]{1,0:T(8,128)(2,1)S(1)} collective-permute-done((bf16[960,768]{1,0:T(8,128)(2,1)S(1)}, bf16[960,768]{1,0:T(8,128)(2,1)S(1)}, u32[]{:S(2)}, u32[]{:S(2)}) %collective-permute-start.16) | collective-permute-done | bytes 1474592 | tf_op jit(solution)/shard_map/ppermute | solution.py:408
  993.5 2.5 collective-permute-done.13.refs_0_
  1002.5 27.1 %collective-permute-done.22.refs_2_ = bf16[1152,768]{1,0:T(8,128)(2,1)S(1)} collective-permute-done((bf16[1152,768]{1,0:T(8,128)(2,1)S(1)}, bf16[1152,768]{1,0:T(8,128)(2,1)S(1)}, u32[]{:S(2)}, u32[]{:S(2)}) %collective-permute-start.22) | collective-permute-done | bytes 1769504 | tf_op jit(solution)/shard_map/ppermute | solution.py:408
  1041.6 4.7 shard_map.93
  1057.0 3.7 shard_map.94.refs_12_
  1064.6 10.4 shard_map.95.refs_12_
  1077.5 8.2 shard_map.96.refs_12_
  1086.0 3.5 shard_map.97.refs_12_
  1096.8 3.4 shard_map.100.refs_4_
  1100.8 4.4 shard_map.101.refs_4_
  1105.2 3.0 shard_map.102.refs_2_
  (388 shorter events, 135.5 us)
Async XLA Ops:
  692.8 29.8 %collective-permute-start.27 = (bf16[384,768]{1,0:T(8,128)(2,1)S(1)}, bf16[384,768]{1,0:T(8,128)(2,1)S(1)}, u32[]{:S(2)}, u32[]{:S(2)}) collective-permute-start(bf16[384,768]{1,0:T(8,128)(2,1)S(1)} %copy-done.77), channel_id=1, source_target_pairs={{0,4},{1,5},{2,6},{3,7},{4,0},{5,1},{6,2},{7,3}} | collective-permute-start | bytes 1769480 | tf_op jit(solution)/shard_map/ppermute | solution.py:408
  694.2 28.4 %collective-permute-start.67 = (bf16[384,768]{1,0:T(8,128)(2,1)S(1)}, bf16[384,768]{1,0:T(8,128)(2,1)S(1)}, u32[]{:S(2)}, u32[]{:S(2)}) collective-permute-start(bf16[384,768]{1,0:T(8,128)(2,1)S(1)} %copy-done.77), channel_id=1, source_target_pairs={{0,2},{1,3},{2,0},{3,1},{4,6},{5,7},{6,4},{7,5}} | collective-permute-start | bytes 1769480 | tf_op jit(solution)/shard_map/ppermute | solution.py:408
  781.3 63.5 %collective-permute-start.51 = (bf16[960,768]{1,0:T(8,128)(2,1)S(1)}, bf16[960,768]{1,0:T(8,128)(2,1)S(1)}, u32[]{:S(2)}, u32[]{:S(2)}) collective-permute-start(bf16[960,768]{1,0:T(8,128)(2,1)S(1)} %copy-done.26), channel_id=1, source_target_pairs={{0,2},{1,3},{2,0},{3,1},{4,6},{5,7},{6,4},{7,5}} | collective-permute-start | bytes 4423688 | tf_op jit(solution)/shard_map/ppermute | solution.py:408
  783.6 61.2 %collective-permute-start.15 = (bf16[960,768]{1,0:T(8,128)(2,1)S(1)}, bf16[960,768]{1,0:T(8,128)(2,1)S(1)}, u32[]{:S(2)}, u32[]{:S(2)}) collective-permute-start(bf16[960,768]{1,0:T(8,128)(2,1)S(1)} %copy-done.26), channel_id=1, source_target_pairs={{0,4},{1,5},{2,6},{3,7},{4,0},{5,1},{6,2},{7,3}} | collective-permute-start | bytes 4423688 | tf_op jit(solution)/shard_map/ppermute | solution.py:408
  786.8 42.3 %collective-permute-start.28 = (bf16[384,768]{1,0:T(8,128)(2,1)S(1)}, bf16[384,768]{1,0:T(8,128)(2,1)S(1)}, u32[]{:S(2)}, u32[]{:S(2)}) collective-permute-start(bf16[384,768]{1,0:T(8,128)(2,1)S(1)} %collective-permute-done.27.refs_10_), channel_id=1, source_target_pairs={{0,2},{1,3},{2,0},{3,1},{4,6},{5,7},{6,4},{7,5}} | collective-permute-start | bytes 1769480 | tf_op jit(solution)/shard_map/ppermute | solution.py:408
  789.5 41.6 %collective-permute-start.25 = (bf16[384,768]{1,0:T(8,128)(2,1)S(1)}, bf16[384,768]{1,0:T(8,128)(2,1)S(1)}, u32[]{:S(2)}, u32[]{:S(2)}) collective-permute-start(bf16[384,768]{1,0:T(8,128)(2,1)S(1)} %collective-permute-done.24.refs_2_), channel_id=1, source_target_pairs={{0,4},{1,5},{2,6},{3,7},{4,0},{5,1},{6,2},{7,3}} | collective-permute-start | bytes 1769480 | tf_op jit(solution)/shard_map/ppermute | solution.py:408
  792.1 49.3 %collective-permute-start.10 = (bf16[384,768]{1,0:T(8,128)(2,1)S(1)}, bf16[384,768]{1,0:T(8,128)(2,1)}, u32[]{:S(2)}, u32[]{:S(2)}) collective-permute-start(bf16[384,768]{1,0:T(8,128)(2,1)S(1)} %collective-permute-done.9.refs_10_), channel_id=1, source_target_pairs={{0,2},{1,3},{2,0},{3,1},{4,6},{5,7},{6,4},{7,5}} | collective-permute-start | bytes 1769480 | tf_op jit(solution)/shard_map/ppermute | solution.py:408
  841.4 35.4 %collective-permute-start.12 = (bf16[960,768]{1,0:T(8,128)(2,1)}, bf16[960,768]{1,0:T(8,128)(2,1)S(1)}, u32[]{:S(2)}, u32[]{:S(2)}) collective-permute-start(bf16[960,768]{1,0:T(8,128)(2,1)} %get-tuple-element.82.refs_0_), channel_id=1, source_target_pairs={{0,2},{1,3},{2,0},{3,1},{4,6},{5,7},{6,4},{7,5}} | collective-permute-start | bytes 4423688 | tf_op jit(solution)/shard_map/ppermute | solution.py:408
  843.6 35.4 %collective-permute-start.48 = (bf16[960,768]{1,0:T(8,128)(2,1)}, bf16[960,768]{1,0:T(8,128)(2,1)S(1)}, u32[]{:S(2)}, u32[]{:S(2)}) collective-permute-start(bf16[960,768]{1,0:T(8,128)(2,1)} %get-tuple-element.82.refs_0_), channel_id=1, source_target_pairs={{0,4},{1,5},{2,6},{3,7},{4,0},{5,1},{6,2},{7,3}} | collective-permute-start | bytes 4423688 | tf_op jit(solution)/shard_map/ppermute | solution.py:408
  844.8 35.6 %collective-permute-start.46 = (bf16[960,768]{1,0:T(8,128)(2,1)}, bf16[960,768]{1,0:T(8,128)(2,1)S(1)}, u32[]{:S(2)}, u32[]{:S(2)}) collective-permute-start(bf16[960,768]{1,0:T(8,128)(2,1)} %get-tuple-element.82.refs_0_), channel_id=1, source_target_pairs={{0,1},{1,0},{2,3},{3,2},{4,5},{5,4},{6,7},{7,6}} | collective-permute-start | bytes 4423688 | tf_op jit(solution)/shard_map/ppermute | solution.py:408
  844.8 69.8 %collective-permute-start.59 = (bf16[1152,768]{1,0:T(8,128)(2,1)S(1)}, bf16[1152,768]{1,0:T(8,128)(2,1)S(1)}, u32[]{:S(2)}, u32[]{:S(2)}) collective-permute-start(bf16[1152,768]{1,0:T(8,128)(2,1)S(1)} %copy-done.9), channel_id=1, source_target_pairs={{0,2},{1,3},{2,0},{3,1},{4,6},{5,7},{6,4},{7,5}} | collective-permute-start | bytes 5308424 | tf_op jit(solution)/shard_map/ppermute | solution.py:408
  846.9 70.0 %collective-permute-start.21 = (bf16[1152,768]{1,0:T(8,128)(2,1)S(1)}, bf16[1152,768]{1,0:T(8,128)(2,1)S(1)}, u32[]{:S(2)}, u32[]{:S(2)}) collective-permute-start(bf16[1152,768]{1,0:T(8,128)(2,1)S(1)} %copy-done.9), channel_id=1, source_target_pairs={{0,4},{1,5},{2,6},{3,7},{4,0},{5,1},{6,2},{7,3}} | collective-permute-start | bytes 5308424 | tf_op jit(solution)/shard_map/ppermute | solution.py:408
  876.7 41.3 %collective-permute-start.58 = (bf16[1152,768]{1,0:T(8,128)(2,1)S(1)}, bf16[1152,768]{1,0:T(8,128)(2,1)S(1)}, u32[]{:S(2)}, u32[]{:S(2)}) collective-permute-start(bf16[1152,768]{1,0:T(8,128)(2,1)S(1)} %copy-done.9), channel_id=1, source_target_pairs={{0,1},{1,0},{2,3},{3,2},{4,5},{5,4},{6,7},{7,6}} | collective-permute-start | bytes 5308424 | tf_op jit(solution)/shard_map/ppermute | solution.py:408
  879.0 72.3 %collective-permute-start.18 = (bf16[1152,768]{1,0:T(8,128)(2,1)S(1)}, bf16[1152,768]{1,0:T(8,128)(2,1)S(1)}, u32[]{:S(2)}, u32[]{:S(2)}) collective-permute-start(bf16[1152,768]{1,0:T(8,128)(2,1)S(1)} %copy-done.8), channel_id=1, source_target_pairs={{0,2},{1,3},{2,0},{3,1},{4,6},{5,7},{6,4},{7,5}} | collective-permute-start | bytes 5308424 | tf_op jit(solution)/shard_map/ppermute | solution.py:408
  881.6 70.9 %collective-permute-start.56 = (bf16[1152,768]{1,0:T(8,128)(2,1)S(1)}, bf16[1152,768]{1,0:T(8,128)(2,1)S(1)}, u32[]{:S(2)}, u32[]{:S(2)}) collective-permute-start(bf16[1152,768]{1,0:T(8,128)(2,1)S(1)} %copy-done.8), channel_id=1, source_target_pairs={{0,4},{1,5},{2,6},{3,7},{4,0},{5,1},{6,2},{7,3}} | collective-permute-start | bytes 5308424 | tf_op jit(solution)/shard_map/ppermute | solution.py:408
  914.7 37.9 %collective-permute-start.54 = (bf16[1152,768]{1,0:T(8,128)(2,1)S(1)}, bf16[1152,768]{1,0:T(8,128)(2,1)S(1)}, u32[]{:S(2)}, u32[]{:S(2)}) collective-permute-start(bf16[1152,768]{1,0:T(8,128)(2,1)S(1)} %copy-done.8), channel_id=1, source_target_pairs={{0,1},{1,0},{2,3},{3,2},{4,5},{5,4},{6,7},{7,6}} | collective-permute-start | bytes 5308424 | tf_op jit(solution)/shard_map/ppermute | solution.py:408
  916.9 42.8 %collective-permute-start.52 = (bf16[960,768]{1,0:T(8,128)(2,1)S(1)}, bf16[960,768]{1,0:T(8,128)(2,1)S(1)}, u32[]{:S(2)}, u32[]{:S(2)}) collective-permute-start(bf16[960,768]{1,0:T(8,128)(2,1)S(1)} %collective-permute-done.51.refs_8_), channel_id=1, source_target_pairs={{0,1},{1,0},{2,3},{3,2},{4,5},{5,4},{6,7},{7,6}} | collective-permute-start | bytes 4423688 | tf_op jit(solution)/shard_map/ppermute | solution.py:408
  919.3 34.9 %collective-permute-start.29 = (bf16[384,768]{1,0:T(8,128)(2,1)S(1)}, bf16[384,768]{1,0:T(8,128)(2,1)S(1)}, u32[]{:S(2)}, u32[]{:S(2)}) collective-permute-start(bf16[384,768]{1,0:T(8,128)(2,1)S(1)} %collective-permute-done.28.refs_2_), channel_id=1, source_target_pairs={{0,1},{1,0},{2,3},{3,2},{4,5},{5,4},{6,7},{7,6}} | collective-permute-start | bytes 1769480 | tf_op jit(solution)/shard_map/ppermute | solution.py:408
  957.1 35.2 %collective-permute-start.16 = (bf16[960,768]{1,0:T(8,128)(2,1)S(1)}, bf16[960,768]{1,0:T(8,128)(2,1)S(1)}, u32[]{:S(2)}, u32[]{:S(2)}) collective-permute-start(bf16[960,768]{1,0:T(8,128)(2,1)S(1)} %collective-permute-done.15.refs_10_), channel_id=1, source_target_pairs={{0,2},{1,3},{2,0},{3,1},{4,6},{5,7},{6,4},{7,5}} | collective-permute-start | bytes 4423688 | tf_op jit(solution)/shard_map/ppermute | solution.py:408
  960.8 35.1 %collective-permute-start.13 = (bf16[960,768]{1,0:T(8,128)(2,1)S(1)}, bf16[960,768]{1,0:T(8,128)(2,1)}, u32[]{:S(2)}, u32[]{:S(2)}) collective-permute-start(bf16[960,768]{1,0:T(8,128)(2,1)S(1)} %collective-permute-done.12.refs_2_), channel_id=1, source_target_pairs={{0,4},{1,5},{2,6},{3,7},{4,0},{5,1},{6,2},{7,3}} | collective-permute-start | bytes 4423688 | tf_op jit(solution)/shard_map/ppermute | solution.py:408
  963.8 33.5 %collective-permute-start.60 = (bf16[1152,768]{1,0:T(8,128)(2,1)S(1)}, bf16[1152,768]{1,0:T(8,128)(2,1)S(1)}, u32[]{:S(2)}, u32[]{:S(2)}) collective-permute-start(bf16[1152,768]{1,0:T(8,128)(2,1)S(1)} %collective-permute-done.59.refs_8_), channel_id=1, source_target_pairs={{0,1},{1,0},{2,3},{3,2},{4,5},{5,4},{6,7},{7,6}} | collective-permute-start | bytes 5308424 | tf_op jit(solution)/shard_map/ppermute | solution.py:408
  965.0 35.2 %collective-permute-start.61 = (bf16[1152,768]{1,0:T(8,128)(2,1)S(1)}, bf16[1152,768]{1,0:T(8,128)(2,1)S(1)}, u32[]{:S(2)}, u32[]{:S(2)}) collective-permute-start(bf16[1152,768]{1,0:T(8,128)(2,1)S(1)} %collective-permute-done.21.refs_10_), channel_id=1, source_target_pairs={{0,1},{1,0},{2,3},{3,2},{4,5},{5,4},{6,7},{7,6}} | collective-permute-start | bytes 5308424 | tf_op jit(solution)/shard_map/ppermute | solution.py:408
  966.6 63.0 %collective-permute-start.22 = (bf16[1152,768]{1,0:T(8,128)(2,1)S(1)}, bf16[1152,768]{1,0:T(8,128)(2,1)S(1)}, u32[]{:S(2)}, u32[]{:S(2)}) collective-permute-start(bf16[1152,768]{1,0:T(8,128)(2,1)S(1)} %collective-permute-done.21.refs_10_), channel_id=1, source_target_pairs={{0,2},{1,3},{2,0},{3,1},{4,6},{5,7},{6,4},{7,5}} | collective-permute-start | bytes 5308424 | tf_op jit(solution)/shard_map/ppermute | solution.py:408
  992.3 40.5 %collective-permute-start.19 = (bf16[1152,768]{1,0:T(8,128)(2,1)S(1)}, bf16[1152,768]{1,0:T(8,128)(2,1)S(1)}, u32[]{:S(2)}, u32[]{:S(2)}) collective-permute-start(bf16[1152,768]{1,0:T(8,128)(2,1)S(1)} %collective-permute-done.18.refs_2_), channel_id=1, source_target_pairs={{0,4},{1,5},{2,6},{3,7},{4,0},{5,1},{6,2},{7,3}} | collective-permute-start | bytes 5308424 | tf_op jit(solution)/shard_map/ppermute | solution.py:408
  996.0 38.1 %collective-permute-start.55 = (bf16[1152,768]{1,0:T(8,128)(2,1)S(1)}, bf16[1152,768]{1,0:T(8,128)(2,1)S(1)}, u32[]{:S(2)}, u32[]{:S(2)}) collective-permute-start(bf16[1152,768]{1,0:T(8,128)(2,1)S(1)} %collective-permute-done.18.refs_2_), channel_id=1, source_target_pairs={{0,1},{1,0},{2,3},{3,2},{4,5},{5,4},{6,7},{7,6}} | collective-permute-start | bytes 5308424 | tf_op jit(solution)/shard_map/ppermute | solution.py:408
  998.4 37.3 %collective-permute-start.57 = (bf16[1152,768]{1,0:T(8,128)(2,1)S(1)}, bf16[1152,768]{1,0:T(8,128)(2,1)S(1)}, u32[]{:S(2)}, u32[]{:S(2)}) collective-permute-start(bf16[1152,768]{1,0:T(8,128)(2,1)S(1)} %collective-permute-done.56.refs_4_), channel_id=1, source_target_pairs={{0,1},{1,0},{2,3},{3,2},{4,5},{5,4},{6,7},{7,6}} | collective-permute-start | bytes 5308424 | tf_op jit(solution)/shard_map/ppermute | solution.py:408
  1001.4 35.6 %collective-permute-start.17 = (bf16[960,768]{1,0:T(8,128)(2,1)S(1)}, bf16[960,768]{1,0:T(8,128)(2,1)S(1)}, u32[]{:S(2)}, u32[]{:S(2)}) collective-permute-start(bf16[960,768]{1,0:T(8,128)(2,1)S(1)} %collective-permute-done.16.refs_2_), channel_id=1, source_target_pairs={{0,1},{1,0},{2,3},{3,2},{4,5},{5,4},{6,7},{7,6}} | collective-permute-start | bytes 4423688 | tf_op jit(solution)/shard_map/ppermute | solution.py:408
  1035.2 65.0 %collective-permute-start.14 = (bf16[960,768]{1,0:T(8,128)(2,1)}, bf16[960,768]{1,0:T(8,128)(2,1)}, u32[]{:S(2)}, u32[]{:S(2)}) collective-permute-start(bf16[960,768]{1,0:T(8,128)(2,1)} %collective-permute-done.13.refs_0_), channel_id=1, source_target_pairs={{0,1},{1,0},{2,3},{3,2},{4,5},{5,4},{6,7},{7,6}} | collective-permute-start | bytes 4423688 | tf_op jit(solution)/shard_map/ppermute | solution.py:408
  1037.0 68.2 %collective-permute-start.11 = (bf16[384,768]{1,0:T(8,128)(2,1)}, bf16[384,768]{1,0:T(8,128)(2,1)}, u32[]{:S(2)}, u32[]{:S(2)}) collective-permute-start(bf16[384,768]{1,0:T(8,128)(2,1)} %collective-permute-done.10.refs_2_), channel_id=1, source_target_pairs={{0,1},{1,0},{2,3},{3,2},{4,5},{5,4},{6,7},{7,6}} | collective-permute-start | bytes 1769480 | tf_op jit(solution)/shard_map/ppermute | solution.py:408
  1038.1 67.1 %collective-permute-start.8 = (bf16[384,768]{1,0:T(8,128)(2,1)}, bf16[384,768]{1,0:T(8,128)(2,1)}, u32[]{:S(2)}, u32[]{:S(2)}) collective-permute-start(bf16[384,768]{1,0:T(8,128)(2,1)} %collective-permute-done.7.refs_0_), channel_id=1, source_target_pairs={{0,1},{1,0},{2,3},{3,2},{4,5},{5,4},{6,7},{7,6}} | collective-permute-start | bytes 1769480 | tf_op jit(solution)/shard_map/ppermute | solution.py:408
  1039.9 70.3 %collective-permute-start.5 = (bf16[192,768]{1,0:T(8,128)(2,1)}, bf16[192,768]{1,0:T(8,128)(2,1)}, u32[]{:S(2)}, u32[]{:S(2)}) collective-permute-start(bf16[192,768]{1,0:T(8,128)(2,1)} %collective-permute-done.4.refs_1_), channel_id=1, source_target_pairs={{0,1},{1,0},{2,3},{3,2},{4,5},{5,4},{6,7},{7,6}} | collective-permute-start | bytes 884744 | tf_op jit(solution)/shard_map/ppermute | solution.py:408
  1041.1 69.1 %collective-permute-start.2 = (bf16[192,768]{1,0:T(8,128)(2,1)}, bf16[192,768]{1,0:T(8,128)(2,1)}, u32[]{:S(2)}, u32[]{:S(2)}) collective-permute-start(bf16[192,768]{1,0:T(8,128)(2,1)} %collective-permute-done.1.refs_0_), channel_id=1, source_target_pairs={{0,1},{1,0},{2,3},{3,2},{4,5},{5,4},{6,7},{7,6}} | collective-permute-start | bytes 884744 | tf_op jit(solution)/shard_map/ppermute | solution.py:408
  (167 other events, 1470.6 us)
